TPU v7x, 256 devices: a whole 4x4x8 slice. The times are simulated.
256 devices in a mesh: band: 32 (over z, y_hi, core), chan: 8 (over x, y_lo).
Axes of the slice: x: 4, y: 4 (y_hi: 2, y_lo: 2; y = y_hi * 2 + y_lo), z: 8, core: 2. Of those that a mesh axis runs over, the one named last changes fastest.
Arguments:
- fine_features: bfloat16 [2, 192, 256, 512], P(None, 'chan', 'band'), may hold values from -100 to 100
- coarse_level: bfloat16 [2, 256, 128, 256], P(None, 'chan', 'band'), may hold values from -100 to 100
- lat_weight: bfloat16 [256, 192], P('chan'), may hold values from -0.4375 to 0.4375
- lat_gain: bfloat16 [256], P('chan'), may hold values from 0.099609375 to 1.8984375
- lat_shift: bfloat16 [256], P('chan'), may hold values from -3 to 3
- out_weight: bfloat16 [3, 3, 256, 256], P(None, None, 'chan'), may hold values from -0.125 to 0.125
- out_gain: bfloat16 [256], P('chan'), may hold values from 0.099609375 to 1.8984375
- out_shift: bfloat16 [256], P('chan'), may hold values from -3 to 3
- mask_weight: bfloat16 [256, 256], P('chan'), may hold values from -0.375 to 0.375
- mask_bias: bfloat16 [256], P('chan'), may hold values from -1.796875 to 1.796875
- queries: bfloat16 [200, 256], replicated, may hold values from -128 to 128
Outputs:
- log_probs: float32 [2, 200, 256, 512], P(None, None, ('band', 'chan'))
All inputs are finite; a program needn't handle non-finite values.
Results may differ from a plain program's by a relative error of at most 0.0058.
Values may be sent and summed in bfloat16 or wider, within the bound.
No kernel may reach another device: no remote copies, remote signals or barrier semaphores. Data moves between devices by JAX's collectives and lax.ppermute only.
A program may use at most 64 MiB of HBM per device.

v0:
```python
import jax
import jax.numpy as jnp
from jax import lax
from jax.experimental import pallas as pl
from jax.experimental.pallas import tpu as pltpu
from jax.sharding import Mesh
from jax.sharding import PartitionSpec as P


D = 256
GROUPS = 32
IN_CH = 192
COLS = 512
HALF = 256
QUERIES = 200
BAND = ("band_0", "band_1", "band_2")
CHAN = ("chan_0", "chan_1")
ALL = BAND + CHAN
EPS = 1e-05
F32 = jnp.float32
BF16 = jnp.bfloat16
OWN_ROWS = 96
SIDE_ROWS = 112
MASK_AT = 72
SHARD_ROWS = 80
XORS = (4, 1, 2, 5, 6, 3, 7)


def dot(a, b):
    return lax.dot_general(a, b, (((1,), (0,)), ((), ())), preferred_element_type=F32)


def local_stats(values, lane, offset):
    blocks = values.reshape(GROUPS, D // GROUPS, COLS)
    count = D // GROUPS * COLS
    mean = jnp.sum(jnp.sum(blocks, axis=2, keepdims=True), axis=1, keepdims=True) / count
    dev = blocks - mean
    m2 = jnp.sum(jnp.sum(dev * dev, axis=2, keepdims=True), axis=1, keepdims=True)
    group = lax.broadcasted_iota(jnp.int32, (GROUPS, 1, 128), 0)
    row = jnp.where(lane == group + offset, mean, 0.0)
    row = row + jnp.where(lane == group + (offset + GROUPS), m2, 0.0)
    return jnp.sum(row, axis=0)


def combine(stats):
    devices = stats.shape[0]
    count = D // GROUPS * COLS
    mean = jnp.sum(stats, axis=0, keepdims=True) / devices
    dev = stats - mean
    spread = jnp.sum(dev * dev, axis=0, keepdims=True) * (1.0 / devices)
    return mean, spread, mean * (1.0 / count)


def stat_cols(rows, image):
    mean, spread, inner = rows
    lane = lax.broadcasted_iota(jnp.int32, (D, 128), 1)
    group = lax.broadcasted_iota(jnp.int32, (D, 128), 0) // (D // GROUPS)
    at_mean = lane == group + image * 2 * GROUPS
    at_m2 = lane == group + (image * 2 + 1) * GROUPS
    mean_col = jnp.sum(jnp.where(at_mean, mean, 0.0), axis=1, keepdims=True)
    var_col = jnp.sum(
        jnp.where(at_mean, spread, 0.0) + jnp.where(at_m2, inner, 0.0), axis=1, keepdims=True
    )
    return mean_col, var_col


def combine_kernel(stats_ref, rows_ref):
    mean, spread, inner = combine(stats_ref[...].reshape(stats_ref.shape[0], 128))
    rows_ref[0:1] = mean
    rows_ref[1:2] = spread
    rows_ref[2:3] = inner
    rows_ref[3:8] = jnp.zeros((5, 128), F32)


def vector_col(lat_weight_ref, index):
    return lat_weight_ref[:, 128:256].astype(F32)[:, 64 + index : 65 + index]


def lanes_of(shape):
    return lax.broadcasted_iota(jnp.int32, shape, len(shape) - 1)


def fine_rows(ref, image, low, high):
    return jnp.concatenate(
        [ref[s, 24 * image : 24 * image + 24, low:high] for s in range(8)], axis=0
    )


def pack_own_kernel(
    fine_hbm, coarse_hbm, weight_hbm, *refs
):
    vec_hbm, own_ref, (fine_ref, coarse_ref, weight_ref, vec_ref, rows, coarse, sems) = (
        refs[:5], refs[5], refs[6:]
    )
    pairs = [(fine_hbm, fine_ref), (coarse_hbm, coarse_ref), (weight_hbm, weight_ref)]
    pairs += [(vec, vec_ref.at[i]) for i, vec in enumerate(vec_hbm)]
    copies = [
        pltpu.make_async_copy(source, target, sems.at[i])
        for i, (source, target) in enumerate(pairs)
    ]
    for copy in copies:
        copy.start()
    for copy in copies:
        copy.wait()
    for t in range(4):
        piece = fine_ref[:, :, :, 128 * t : 128 * t + 128].astype(F32)
        rows[t] = piece.reshape(48 * 8, 128)
    for n in range(2):
        for t in range(2):
            piece = coarse_ref[n, :, :, 128 * t : 128 * t + 128].astype(F32)
            coarse[n, t, :, 0:4, :] = piece
    vec_lane = lanes_of((32, 32))
    vec_row = lax.broadcasted_iota(jnp.int32, (32, 32), 0)
    columns = jnp.zeros((32, 256 - IN_CH), F32)
    for i in range(5):
        vec = jnp.where(vec_lane == vec_row, vec_ref[i].astype(F32), 0.0)
        column = jnp.sum(vec, axis=1, keepdims=True)
        columns += jnp.where(lanes_of((32, 256 - IN_CH)) == i, column, 0.0)
    weight = jnp.concatenate([weight_ref[...].astype(F32), columns], axis=1)
    packed = jnp.concatenate([weight[0:16], weight[16:32]], axis=1).astype(BF16)
    fine_lane = lanes_of((24, 128))
    coarse_lane = lanes_of((32, 128))
    for q in range(4):
        for h in range(2):
            d = 2 * q + h
            fine_extra = jnp.zeros((24, 128), F32)
            for r in range(2):
                for t in range(2):
                    row = rows[2 * h + t, pl.ds(2 * q + r, 48, stride=8), :]
                    at = 256 * r + 128 * t
                    own_ref[d, 0:48, at : at + 128] = row.astype(BF16)
                row = rows[2 - h, pl.ds(2 * q + r, 48, stride=8), :]
                edge = row[:, 0:1] if h == 0 else row[:, 127:128]
                for n in range(2):
                    at = 4 * n + 1 + r
                    fine_extra += jnp.where(fine_lane == at, edge[24 * n : 24 * n + 24], 0.0)
            own_ref[d, 48:64, :] = packed
            coarse_extra = jnp.zeros((32, 128), F32)
            for n in range(2):
                row = coarse[n, h, :, q, :].astype(BF16)
                own_ref[d, 64:80, 128 * n : 128 * n + 128] = row[0:16]
                own_ref[d, 64:80, 256 + 128 * n : 384 + 128 * n] = row[16:32]
                row = coarse[n, 1 - h, :, q, :]
                edge = row[:, 0:1] if h == 0 else row[:, 127:128]
                coarse_extra += jnp.where(coarse_lane // 4 == n, edge, 0.0)
            extra = [
                fine_extra[0:16],
                jnp.concatenate([fine_extra[16:24], jnp.zeros((8, 128), F32)], axis=0),
                coarse_extra[0:16],
                coarse_extra[16:32],
            ]
            own_ref[d, 80:96, :] = jnp.concatenate(extra, axis=1).astype(BF16)


def pack_weights_kernel(conv_ref, mask_ref, shard_ref):
    half = pl.multiple_of(16 * lax.axis_index("band_2"), 16)
    for k in range(10):
        if k < 9:
            piece = conv_ref[k // 3, k % 3, pl.ds(half, 16), :].astype(F32)
        else:
            piece = mask_ref[pl.ds(half, 16), :].astype(F32)
        piece = jnp.concatenate([piece[0:8], piece[8:16]], axis=1).astype(BF16)
        shard_ref[8 * k : 8 * k + 8] = piece


def arrange_kernel(*refs):
    chan = lax.axis_index("chan_0") * 2 + lax.axis_index("chan_1")
    all_ref = refs[-1]
    for k, ref in enumerate(refs[:-1]):
        all_ref[chan ^ k] = ref[...]


def lateral_kernel(own_ref, weight_ref, stats_ref, next_ref, prev_ref):
    for s in range(8):
        for half in range(2):
            weight_ref[32 * s + 16 * half : 32 * s + 16 * half + 16, :] = own_ref[
                s, 48:64, 256 * half : 256 * half + 256
            ]
    for ref, at in ((next_ref, 256), (prev_ref, 0)):
        for s in range(8):
            ref[s, 0:48, :] = own_ref[s, 0:48, at : at + 256]
            ref[s, 48:64, :] = own_ref[s, 64:80, 0:256]
            ref[s, 64:80, :] = own_ref[s, 64:80, 256:512]
            ref[s, 80:96, :] = own_ref[s, 80:96, 0:256]
            ref[s, 96:112, :] = own_ref[s, 80:96, 256:512]
    lane = lax.broadcasted_iota(jnp.int32, (GROUPS, 1, 128), 2)
    total = jnp.zeros((1, 128), F32)
    for n in range(2):
        lateral = dot(weight_ref[:, 0:IN_CH], fine_rows(own_ref, n, 0, COLS))
        total = total + local_stats(lateral, lane, 64 * n)
    stats_ref[...] = jnp.broadcast_to(total[None], stats_ref.shape)


def join_kernel(
    own_ref, above_ref, below_ref, lat_weight_ref, lat_stats_ref, joined_ref, beside_ref
):
    core = lax.axis_index("band_2")
    band = (lax.axis_index("band_0") * 2 + lax.axis_index("band_1")) * 2 + core
    side = lax.axis_index("chan_1")
    pair = band * 4 + lax.axis_index("chan_0")
    at_top = pair == 0
    at_bottom = pair == 127
    source = lax.broadcasted_iota(jnp.int32, (128, HALF), 0)
    column = lanes_of((128, HALF))
    inner_edge = jnp.where(side == 0, HALF - 1, 0)
    near = column // 2
    far = jnp.clip(near - 1 + 2 * (column % 2), 0, 127)
    spread = (
        jnp.where(source == near, 0.75, 0.0)
        + jnp.where(jnp.logical_and(source == far, column != inner_edge), 0.25, 0.0)
    ).astype(BF16)
    gain = vector_col(lat_weight_ref, 0)
    shift = vector_col(lat_weight_ref, 1)
    stats = (lat_stats_ref[0:1], lat_stats_ref[1:2], lat_stats_ref[2:3])
    lane_at = lanes_of((D, HALF))
    small = lanes_of((D, 128))
    first_image = small < 4
    time = small % 4
    norm = [stat_cols(stats, n) for n in range(2)]
    norm = [(mean, lax.rsqrt(var + EPS) * gain) for mean, var in norm]
    lat_weight = lat_weight_ref[:, 0:IN_CH]

    def coarse_main(ref, low, high, n):
        at = 128 * n
        if high is None:
            pieces = [ref[s, low : low + 32, at : at + 128] for s in range(8)]
        else:
            pieces = []
            for s in range(8):
                pieces.append(ref[s, low : low + 16, at : at + 128])
                pieces.append(ref[s, low : low + 16, high + at : high + at + 128])
        return jnp.concatenate(pieces, axis=0)

    def extras(ref, low, at):
        fine, coarse = [], []
        for s in range(8):
            fine.append(ref[s, low : low + 16, 0:128])
            fine.append(ref[s, low : low + 8, 128:256])
            if at:
                coarse.append(ref[s, low : low + 16, at : at + 128])
                coarse.append(ref[s, low : low + 16, at + 128 : at + 256])
            else:
                coarse.append(ref[s, low + 16 : low + 32, 0:128])
                coarse.append(ref[s, low + 16 : low + 32, 128:256])
        fine = dot(lat_weight, jnp.concatenate(fine, axis=0))
        return fine, jnp.concatenate(coarse, axis=0).astype(F32)

    fine_above, extra_above = extras(above_ref, 80, 0)
    fine_own, extra_own = extras(own_ref, 80, 256)
    fine_below, extra_below = extras(below_ref, 80, 0)
    extra_above = jnp.where(at_top, extra_own, extra_above)
    extra_below = jnp.where(at_bottom, extra_own, extra_below)
    mains = []
    for n in range(2):
        middle = coarse_main(own_ref, 64, 256, n)
        upper = coarse_main(above_ref, 48, None, n)
        lower = coarse_main(below_ref, 48, None, n)
        upper = jnp.where(at_top, middle, upper)
        lower = jnp.where(at_bottom, middle, lower)
        mains.append((upper, middle, lower))
    edge_at = jnp.where(side == 0, 127, 0)
    ups, columns = [], []
    for k, extra in enumerate((extra_above, extra_own, extra_below)):
        edges = []
        for n in range(2):
            main = mains[n][k]
            edges.append(
                jnp.sum(jnp.where(small == edge_at, main.astype(F32), 0.0), axis=1, keepdims=True)
            )
        columns.append(0.75 * extra + 0.25 * jnp.where(first_image, edges[0], edges[1]))
        ups.append(
            [
                dot(mains[n][k], spread)
                + jnp.where(lane_at == inner_edge, 0.25 * extra[:, 4 * n : 4 * n + 1], 0.0)
                for n in range(2)
            ]
        )

    lateral = jnp.where(
        time == 0,
        pltpu.roll(fine_above, 126, axis=1),
        jnp.where(time == 3, pltpu.roll(fine_below, 2, axis=1), fine_own),
    )
    upsampled = jnp.where(
        time == 0,
        0.75 * columns[0] + 0.25 * columns[1],
        jnp.where(
            time == 1,
            0.25 * columns[0] + 0.75 * columns[1],
            jnp.where(
                time == 2,
                0.75 * columns[1] + 0.25 * columns[2],
                0.25 * columns[1] + 0.75 * columns[2],
            ),
        ),
    )
    mean = jnp.where(first_image, norm[0][0], norm[1][0])
    scale = jnp.where(first_image, norm[0][1], norm[1][1])
    value = (lateral - mean) * scale + shift + upsampled
    outside = jnp.logical_or(
        jnp.logical_and(time == 0, at_top), jnp.logical_and(time == 3, at_bottom)
    )
    value = jnp.where(outside, 0.0, value)
    beside_ref[...] = jnp.concatenate(
        [value, pltpu.roll(value, 127, axis=1), pltpu.roll(value, 126, axis=1)], axis=0
    ).astype(BF16)

    for n in range(2):
        mean, scale = norm[n]
        up = [ups[k][n] for k in range(3)]
        rows = (
            (fine_rows(above_ref, n, 0, HALF), 0.75 * up[0] + 0.25 * up[1]),
            (fine_rows(own_ref, n, 0, HALF), 0.25 * up[0] + 0.75 * up[1]),
            (fine_rows(own_ref, n, HALF, COLS), 0.75 * up[1] + 0.25 * up[2]),
            (fine_rows(below_ref, n, 0, HALF), 0.25 * up[1] + 0.75 * up[2]),
        )
        for t, (fine, upsampled) in enumerate(rows):
            value = ((dot(lat_weight, fine) - mean) * scale + shift + upsampled).astype(BF16)
            if t == 0:
                value = jnp.where(at_top, jnp.zeros_like(value), value)
            if t == 3:
                value = jnp.where(at_bottom, jnp.zeros_like(value), value)
            for r in range(2):
                if 0 <= t - r <= 2:
                    joined_ref[
                        n, 256 * (t - r) : 256 * (t - r) + 256, HALF * r : HALF * r + HALF
                    ] = value


def conv_kernel(
    joined_ref, beside_ref, mine_ref, other_ref, keep_ref, send_ref, stats_ref, weight, taps
):
    core = lax.axis_index("band_2")
    side = lax.axis_index("chan_1")
    for part, ref in ((core, mine_ref), (1 - core, other_ref)):
        for s in range(8):
            at = pl.multiple_of(32 * s + 16 * part, 16)
            for a in range(3):
                for b in range(3):
                    piece = ref[s, (a * 3 + b) * 8 : (a * 3 + b) * 8 + 8, :]
                    both = jnp.concatenate([piece[:, 0:256], piece[:, 256:512]], axis=0)
                    weight[b, pl.ds(at, 16), 256 * a : 256 * a + 256] = both
    inner_edge = jnp.where(side == 0, HALF - 1, 0)
    lane = lax.broadcasted_iota(jnp.int32, (GROUPS, 1, 128), 2)
    lane_at = lanes_of((D, HALF))
    beside = dot(weight[jnp.where(side == 0, 2, 0)], beside_ref[...])
    total = jnp.zeros((1, 128), F32)
    for n in range(2):
        for b in range(3):
            taps[b] = dot(weight[b], joined_ref[n])
        out = []
        for r in range(2):
            at = HALF * r
            left = pltpu.roll(taps[0, :, at : at + HALF], 1, axis=1)
            right = pltpu.roll(taps[2, :, at : at + HALF], HALF - 1, axis=1)
            value = taps[1, :, at : at + HALF] + jnp.where(lane_at == 0, 0.0, left)
            value = value + jnp.where(lane_at == HALF - 1, 0.0, right)
            column = beside[:, 4 * n + r : 4 * n + r + 1]
            out.append(value + jnp.where(lane_at == inner_edge, column, 0.0))
        keep_ref[n] = jnp.where(side == 0, out[0], out[1])
        send_ref[n] = jnp.where(side == 0, out[1], out[0])
        total = total + local_stats(jnp.concatenate(out, axis=1), lane, 64 * n)
    stats_ref[...] = jnp.broadcast_to(total[None], stats_ref.shape)


def query_kernel(
    keep_ref, taken_ref, out_stats_ref, lat_weight_ref, mine_ref, other_ref,
    query_ref, out_ref, weight,
):
    core = lax.axis_index("band_2")
    side = lax.axis_index("chan_1")
    for part, ref in ((core, mine_ref), (1 - core, other_ref)):
        for s in range(8):
            at = pl.multiple_of(32 * s + 16 * part, 16)
            piece = ref[s, MASK_AT : MASK_AT + 8, :]
            both = jnp.concatenate([piece[:, 0:256], piece[:, 256:512]], axis=0)
            weight[pl.ds(at, 16), :] = both
    gain = vector_col(lat_weight_ref, 2)
    shift = vector_col(lat_weight_ref, 3)
    bias = vector_col(lat_weight_ref, 4)
    rows = combine(out_stats_ref[...].reshape(out_stats_ref.shape[0], 128))
    for n in range(2):
        mean, var = stat_cols(rows, n)
        scale = lax.rsqrt(var + EPS) * gain
        for ref, half in ((keep_ref, side), (taken_ref, 1 - side)):
            activated = jnp.maximum((ref[n] - mean) * scale + shift, 0.0).astype(BF16)
            features = (dot(weight[...], activated) + bias).astype(BF16)
            logits = dot(query_ref[...], features)
            shifted = logits - jnp.max(logits, axis=0, keepdims=True)
            result = shifted - jnp.log(jnp.sum(jnp.exp(shifted), axis=0, keepdims=True))
            at = pl.multiple_of(half * HALF, HALF)
            out_ref[n, :, 0, pl.ds(at, HALF)] = result


def call(kernel, out_shape, scratch=(), flops=0, space=pltpu.VMEM, limit=40 << 20):
    vmem = pl.BlockSpec(memory_space=pltpu.VMEM)
    single = not isinstance(out_shape, (tuple, list))
    return lambda *args: pl.pallas_call(
        kernel,
        out_shape=out_shape,
        in_specs=[pl.BlockSpec(memory_space=space)] * len(args),
        out_specs=vmem if single else [vmem] * len(out_shape),
        scratch_shapes=list(scratch),
        cost_estimate=pl.CostEstimate(flops=flops, bytes_accessed=1 << 20, transcendentals=0),
        compiler_params=pltpu.CompilerParams(vmem_limit_bytes=limit),
    )(*args)


def per_device(
    fine_features,
    coarse_level,
    lat_weight,
    lat_gain,
    lat_shift,
    out_weight,
    out_gain,
    out_shift,
    mask_weight,
    mask_bias,
    queries,
):
    everyone = lax.axis_size(ALL)
    stats_shape = jax.ShapeDtypeStruct((everyone, 1, 128), F32)
    shard_shape = jax.ShapeDtypeStruct((SHARD_ROWS, COLS), BF16)
    all_shape = jax.ShapeDtypeStruct((8, SHARD_ROWS, COLS), BF16)
    side_shape = jax.ShapeDtypeStruct((8, SIDE_ROWS, HALF), BF16)
    half_shape = jax.ShapeDtypeStruct((2, D, HALF), F32)
    swap = [(0, 1), (1, 0)]

    vectors = [v.reshape(1, 32) for v in (lat_gain, lat_shift, out_gain, out_shift, mask_bias)]
    own_out = call(
        pack_own_kernel,
        jax.ShapeDtypeStruct((8, OWN_ROWS, COLS), BF16),
        (
            pltpu.VMEM((2, 24, 8, COLS), BF16),
            pltpu.VMEM((2, 32, 4, 256), BF16),
            pltpu.VMEM((32, IN_CH), BF16),
            pltpu.VMEM((5, 1, 32), BF16),
            pltpu.VMEM((4, 48 * 8, 128), F32),
            pltpu.VMEM((2, 2, 32, 8, 128), F32),
            pltpu.SemaphoreType.DMA((8,)),
        ),
        space=pltpu.HBM,
        limit=60 << 20,
    )(fine_features, coarse_level, lat_weight, *vectors)
    own = lax.all_to_all(own_out, CHAN, 0, 0, tiled=True)
    shard = call(pack_weights_kernel, shard_shape)(out_weight, mask_weight)
    moved = [lax.ppermute(shard, CHAN, [(i, i ^ k) for i in range(8)]) for k in XORS]

    full_lat, stats, to_next, to_prev = call(
        lateral_kernel,
        [jax.ShapeDtypeStruct((D, 256), BF16), stats_shape, side_shape, side_shape],
        flops=2 * 2 * 256 * 256 * 512,
    )(own)
    above = lax.ppermute(to_next, ALL, [(i, i + 2) for i in range(everyone - 2)])
    below = lax.ppermute(to_prev, ALL, [(i + 2, i) for i in range(everyone - 2)])
    stats = lax.all_to_all(stats, ALL, 0, 0, tiled=True)
    stats = call(combine_kernel, jax.ShapeDtypeStruct((8, 128), F32), flops=1 << 20)(stats)

    by_xor = dict(zip(XORS, moved))
    mine = call(arrange_kernel, all_shape)(shard, *[by_xor[k] for k in range(1, 8)])
    other = lax.ppermute(mine, "band_2", swap)
    joined, beside = call(
        join_kernel,
        [jax.ShapeDtypeStruct((2, 3 * D, COLS), BF16), jax.ShapeDtypeStruct((3 * D, 128), BF16)],
        flops=2 * 2 * 256 * 256 * 512 * 7,
    )(own, above, below, full_lat, stats)
    keep, send, stats = call(
        conv_kernel,
        [half_shape, half_shape, stats_shape],
        (pltpu.VMEM((3, D, 3 * D), BF16), pltpu.VMEM((3, D, COLS), F32)),
        flops=2 * 2 * 256 * 256 * 512 * 9,
    )(joined, beside, mine, other)
    taken = lax.ppermute(send, "chan_1", swap)
    stats = lax.all_to_all(stats, ALL, 0, 0, tiled=True)
    return call(
        query_kernel,
        jax.ShapeDtypeStruct((2, QUERIES, 1, COLS), F32),
        (pltpu.VMEM((D, D), BF16),),
        flops=2 * 2 * 256 * 256 * 512 * 2,
    )(keep, taken, stats, full_lat, mine, other, queries)


def solution(mesh):
    finer = Mesh(
        mesh.devices.reshape(8, 2, 2, 4, 2), ("band_0", "band_1", "band_2", "chan_0", "chan_1")
    )

    return jax.shard_map(
        per_device,
        mesh=finer,
        in_specs=(
            P(None, CHAN, BAND, None),
            P(None, CHAN, BAND, None),
            P(CHAN, None),
            P(CHAN),
            P(CHAN),
            P(None, None, CHAN, None),
            P(CHAN),
            P(CHAN),
            P(CHAN, None),
            P(CHAN),
            P(),
        ),
        out_specs=P(None, None, BAND + CHAN, None),
        check_vma=False,
    )
```

profile of v0, /device:TPU:1, one launch (start us, length us, event | category | flops | bytes accessed | tf_op | source)
XLA Modules:
  0.0 93.2 jit_solution(15182995345379723609)
XLA Ops:
  0.0 0.0 copy-start
  0.0 0.0 copy-start.2
  0.0 3.0 %shard_map.109 = bf16[8,96,512]{2,1,0:T(8,128)(2,1)} custom-call(bf16[2,24,8,512]{3,2,1,0:T(8,128)(2,1)} %fine_hbm.1, bf16[2,32,4,256]{3,2,1,0:T(4,128)(2,1)} %coarse_hbm.1, bf16[32,192]{1,0:T(8,128)(2,1)} %weight_hbm.1, bf16[1,32]{1,0:T(2,128)(2,1)} %bitcast.5, bf16[1,32]{1,0:T(2,128)(2,1)} %bitcast.6, bf16[1,32]{1,0:T(2,128)(2,1)} %bitcast.7, ...), custom_call_target="tpu_custom_call" | custom-call | bytes 1048576 | tf_op jit(solution)/shard_map/pallas_call | solution.py:398
  3.0 5.9 %all-to-all-start = ((bf16[8,96,512]{2,1,0:T(8,128)(2,1)}), bf16[8,96,512]{2,1,0:T(8,128)(2,1)S(1)}, u32[]{:S(2)}, u32[]{:S(2)}) async-start(bf16[8,96,512]{2,1,0:T(8,128)(2,1)} %shard_map.109), calls=%async_computation | async-start | bytes 1572864 | tf_op jit(solution)/shard_map/all_to_all | solution.py:446
  8.8 0.0 copy-done
  8.8 0.0 copy-done.2
  8.9 1.5 %collective-permute-start.2 = (bf16[80,512]{1,0:T(8,128)(2,1)S(1)}, bf16[80,512]{1,0:T(8,128)(2,1)S(1)}, u32[]{:S(2)}, u32[]{:S(2)}) collective-permute-start(bf16[80,512]{1,0:T(8,128)(2,1)S(1)} %shard_map.113.refs_0_), channel_id=1, source_target_pairs={{0,1},{1,0},{2,3},{3,2},{4,5},{5,4},{6,7},{7,6},{8,9},{9,8},{10,11... | collective-permute-start | bytes 245768 | tf_op jit(solution)/shard_map/ppermute | solution.py:448
  10.4 1.2 %collective-permute-start.3 = (bf16[80,512]{1,0:T(8,128)(2,1)S(1)}, bf16[80,512]{1,0:T(8,128)(2,1)S(1)}, u32[]{:S(2)}, u32[]{:S(2)}) collective-permute-start(bf16[80,512]{1,0:T(8,128)(2,1)S(1)} %shard_map.113.refs_0_), channel_id=1, source_target_pairs={{0,2},{1,3},{2,0},{3,1},{4,6},{5,7},{6,4},{7,5},{8,10},{9,11},{10,... | collective-permute-start | bytes 245768 | tf_op jit(solution)/shard_map/ppermute | solution.py:448
  11.6 0.1 collective-permute-start.4
  11.7 2.9 %collective-permute-start.5 = (bf16[80,512]{1,0:T(8,128)(2,1)S(1)}, bf16[80,512]{1,0:T(8,128)(2,1)S(1)}, u32[]{:S(2)}, u32[]{:S(2)}) collective-permute-start(bf16[80,512]{1,0:T(8,128)(2,1)S(1)} %shard_map.113.refs_0_), channel_id=1, source_target_pairs={{0,4},{1,5},{2,6},{3,7},{4,0},{5,1},{6,2},{7,3},{8,12},{9,13},{10,... | collective-permute-start | bytes 245768 | tf_op jit(solution)/shard_map/ppermute | solution.py:448
  14.6 1.2 %collective-permute-start.6 = (bf16[80,512]{1,0:T(8,128)(2,1)S(1)}, bf16[80,512]{1,0:T(8,128)(2,1)S(1)}, u32[]{:S(2)}, u32[]{:S(2)}) collective-permute-start(bf16[80,512]{1,0:T(8,128)(2,1)S(1)} %shard_map.113.refs_0_), channel_id=1, source_target_pairs={{0,5},{1,4},{2,7},{3,6},{4,1},{5,0},{6,3},{7,2},{8,13},{9,12},{10,... | collective-permute-start | bytes 245768 | tf_op jit(solution)/shard_map/ppermute | solution.py:448
  15.8 2.0 %collective-permute-done.2.refs_1_ = bf16[80,512]{1,0:T(8,128)(2,1)S(1)} collective-permute-done((bf16[80,512]{1,0:T(8,128)(2,1)S(1)}, bf16[80,512]{1,0:T(8,128)(2,1)S(1)}, u32[]{:S(2)}, u32[]{:S(2)}) %collective-permute-start.2) | collective-permute-done | bytes 81952 | tf_op jit(solution)/shard_map/ppermute | solution.py:448
  17.7 5.6 %collective-permute-start.7 = (bf16[80,512]{1,0:T(8,128)(2,1)S(1)}, bf16[80,512]{1,0:T(8,128)(2,1)S(1)}, u32[]{:S(2)}, u32[]{:S(2)}) collective-permute-start(bf16[80,512]{1,0:T(8,128)(2,1)S(1)} %shard_map.113.refs_0_), channel_id=1, source_target_pairs={{0,6},{1,7},{2,4},{3,5},{4,2},{5,3},{6,0},{7,1},{8,14},{9,15},{10,... | collective-permute-start | bytes 245768 | tf_op jit(solution)/shard_map/ppermute | solution.py:448
  23.3 0.0 collective-permute-done.3.refs_2_
  23.4 1.2 %collective-permute-start.8 = (bf16[80,512]{1,0:T(8,128)(2,1)S(1)}, bf16[80,512]{1,0:T(8,128)(2,1)S(1)}, u32[]{:S(2)}, u32[]{:S(2)}) collective-permute-start(bf16[80,512]{1,0:T(8,128)(2,1)S(1)} %shard_map.113.refs_0_), channel_id=1, source_target_pairs={{0,7},{1,6},{2,5},{3,4},{4,3},{5,2},{6,1},{7,0},{8,15},{9,14},{10,... | collective-permute-start | bytes 245768 | tf_op jit(solution)/shard_map/ppermute | solution.py:448
  24.5 0.0 collective-permute-done.4.refs_3_
  24.5 0.9 collective-permute-done.5.refs_4_
  25.4 2.7 %collective-permute-done.6.refs_5_ = bf16[80,512]{1,0:T(8,128)(2,1)S(1)} collective-permute-done((bf16[80,512]{1,0:T(8,128)(2,1)S(1)}, bf16[80,512]{1,0:T(8,128)(2,1)S(1)}, u32[]{:S(2)}, u32[]{:S(2)}) %collective-permute-start.6) | collective-permute-done | bytes 81952 | tf_op jit(solution)/shard_map/ppermute | solution.py:448
  28.1 0.0 collective-permute-done.7.refs_6_
  28.1 3.6 %collective-permute-done.8.refs_7_ = bf16[80,512]{1,0:T(8,128)(2,1)S(1)} collective-permute-done((bf16[80,512]{1,0:T(8,128)(2,1)S(1)}, bf16[80,512]{1,0:T(8,128)(2,1)S(1)}, u32[]{:S(2)}, u32[]{:S(2)}) %collective-permute-start.8) | collective-permute-done | bytes 81952 | tf_op jit(solution)/shard_map/ppermute | solution.py:448
  31.6 0.1 shard_map.114.mine_ref
  31.7 1.1 %collective-permute-start.9 = (bf16[8,80,512]{2,1,0:T(8,128)(2,1)S(1)}, bf16[8,80,512]{2,1,0:T(8,128)(2,1)S(1)}, u32[]{:S(2)}, u32[]{:S(2)}) collective-permute-start(bf16[8,80,512]{2,1,0:T(8,128)(2,1)S(1)} %shard_map.114.mine_ref), channel_id=1, source_target_pairs={{0,8},{8,0},{1,9},{9,1},{2,10},{10,2},{3,11},{11,3},{4,12},{12,4},... | collective-permute-start | bytes 1966088 | tf_op jit(solution)/shard_map/ppermute | solution.py:462
  32.8 0.0 all-to-all-done.own_ref
  32.8 0.6 shard_map.110
  33.5 2.3 %collective-permute-start = (bf16[8,112,256]{2,1,0:T(8,128)(2,1)S(1)}, bf16[8,112,256]{2,1,0:T(8,128)(2,1)S(1)}, u32[]{:S(2)}, u32[]{:S(2)}) collective-permute-start(bf16[8,112,256]{2,1,0:T(8,128)(2,1)S(1)} %get-tuple-element.14), channel_id=1, source_target_pairs={{0,2},{1,3},{2,4},{3,5},{4,6},{5,7},{6,8},{7,9},{8,10},{9,11},{10,... | collective-permute-start | bytes 1376264 | tf_op jit(solution)/shard_map/ppermute | solution.py:455
  35.8 4.4 %collective-permute-start.1 = (bf16[8,112,256]{2,1,0:T(8,128)(2,1)S(1)}, bf16[8,112,256]{2,1,0:T(8,128)(2,1)S(1)}, u32[]{:S(2)}, u32[]{:S(2)}) collective-permute-start(bf16[8,112,256]{2,1,0:T(8,128)(2,1)S(1)} %get-tuple-element.15), channel_id=1, source_target_pairs={{2,0},{3,1},{4,2},{5,3},{6,4},{7,5},{8,6},{9,7},{10,8},{11,9},{12,... | collective-permute-start | bytes 1376264 | tf_op jit(solution)/shard_map/ppermute | solution.py:456
  40.3 26.8 %all_to_all.15.stats_ref = f32[256,1,128]{2,1,0:T(1,128)S(1)} all-to-all(f32[256,1,128]{2,1,0:T(1,128)S(1)} %get-tuple-element.17), channel_id=1, replica_groups=mesh['band_0'=8,'band_1'=2,'band_2'=2,'chan_0'=4,'chan_1'=2] {'band_0','..., dimensions={0} | all-to-all | bytes 262144 | tf_op jit(solution)/shard_map/all_to_all | solution.py:457
  67.1 0.2 shard_map.111.lat_stats_ref
  67.3 0.0 collective-permute-done.above_ref
  67.3 0.0 collective-permute-done.1.below_ref
  67.3 1.7 %shard_map.112 = (bf16[2,768,512]{2,1,0:T(8,128)(2,1)S(1)}, bf16[768,128]{1,0:T(8,128)(2,1)S(1)}) custom-call(bf16[8,96,512]{2,1,0:T(8,128)(2,1)S(1)} %all-to-all-done.own_ref, bf16[8,112,256]{2,1,0:T(8,128)(2,1)S(1)} %collective-permute-done.above_ref, bf16[8,112,256]{2,1,0:T(8,128)(2,1)S(1)} %collective-permute-done.1.below_ref, ...), custom_call_target="tpu_custom_call" | custom-call | flops 939524096 | bytes 1048576 | tf_op jit(solution)/shard_map/pallas_call | solution.py:398
  69.0 0.0 collective-permute-done.9.other_ref
  69.0 0.0 copy-start.1
  69.0 2.1 %shard_map.115 = (f32[2,256,256]{2,1,0:T(8,128)S(1)}, f32[2,256,256]{2,1,0:T(8,128)S(1)}, f32[256,1,128]{2,1,0:T(1,128)S(1)}) custom-call(bf16[2,768,512]{2,1,0:T(8,128)(2,1)S(1)} %get-tuple-element.18.joined_ref, bf16[768,128]{1,0:T(8,128)(2,1)S(1)} %get-tuple-element.19.beside_ref, bf16[8,80,512]{2,1,0:T(8,128)(2,1)S(1)} %shard_map.114.mine_ref, ...), custom_call_target="tpu_custom_call" | custom-call | flops 1207959552 | bytes 1048576 | tf_op jit(solution)/shard_map/pallas_call | solution.py:398
  71.1 0.6 collective-permute-start.10
  71.7 18.9 %all_to_all.16.out_stats_ref = f32[256,1,128]{2,1,0:T(1,128)S(1)} all-to-all(f32[256,1,128]{2,1,0:T(1,128)S(1)} %get-tuple-element.22), channel_id=1, replica_groups=mesh['band_0'=8,'band_1'=2,'band_2'=2,'chan_0'=4,'chan_1'=2] {'band_0','..., dimensions={0} | all-to-all | bytes 262144 | tf_op jit(solution)/shard_map/all_to_all | solution.py:475
  90.6 0.0 collective-permute-done.10.taken_ref
  90.6 0.0 copy-done.1
  90.6 2.6 %shard_map.116 = f32[2,200,1,512]{3,2,1,0:T(1,128)} custom-call(f32[2,256,256]{2,1,0:T(8,128)S(1)} %get-tuple-element.20.keep_ref, f32[2,256,256]{2,1,0:T(8,128)S(1)} %collective-permute-done.10.taken_ref, f32[256,1,128]{2,1,0:T(1,128)S(1)} %all_to_all.16.out_stats_ref, bf16[256,256]{1,0:T(8,128)(2,1)S(1)} %get-tuple-element.16.lat_weight_ref, ...), custom_call_target="tpu_custom_call" | custom-call | flops 268435456 | bytes 1048576 | tf_op jit(solution)/shard_map/pallas_call | solution.py:398
  (1 shorter events, 0.0 us)
Async XLA Ops:
  0.0 8.8 %copy-start = (bf16[3,3,32,256]{3,2,1,0:T(8,128)(2,1)S(1)}, bf16[3,3,32,256]{3,2,1,0:T(8,128)(2,1)}, u32[]{:S(2)}) copy-start(bf16[3,3,32,256]{3,2,1,0:T(8,128)(2,1)} %conv_ref.1) | copy-start | bytes 442372
  0.0 8.8 %copy-start.2 = (bf16[32,256]{1,0:T(8,128)(2,1)S(1)}, bf16[32,256]{1,0:T(8,128)(2,1)}, u32[]{:S(2)}) copy-start(bf16[32,256]{1,0:T(8,128)(2,1)} %mask_ref.1) | copy-start | bytes 49156
  3.0 29.9 %all-to-all-start = ((bf16[8,96,512]{2,1,0:T(8,128)(2,1)}), bf16[8,96,512]{2,1,0:T(8,128)(2,1)S(1)}, u32[]{:S(2)}, u32[]{:S(2)}) async-start(bf16[8,96,512]{2,1,0:T(8,128)(2,1)} %shard_map.109), calls=%async_computation | async-start | bytes 1572864 | tf_op jit(solution)/shard_map/all_to_all | solution.py:446
  8.9 8.8 %collective-permute-start.2 = (bf16[80,512]{1,0:T(8,128)(2,1)S(1)}, bf16[80,512]{1,0:T(8,128)(2,1)S(1)}, u32[]{:S(2)}, u32[]{:S(2)}) collective-permute-start(bf16[80,512]{1,0:T(8,128)(2,1)S(1)} %shard_map.113.refs_0_), channel_id=1, source_target_pairs={{0,1},{1,0},{2,3},{3,2},{4,5},{5,4},{6,7},{7,6},{8,9},{9,8},{10,11... | collective-permute-start | bytes 245768 | tf_op jit(solution)/shard_map/ppermute | solution.py:448
  10.4 12.9 %collective-permute-start.3 = (bf16[80,512]{1,0:T(8,128)(2,1)S(1)}, bf16[80,512]{1,0:T(8,128)(2,1)S(1)}, u32[]{:S(2)}, u32[]{:S(2)}) collective-permute-start(bf16[80,512]{1,0:T(8,128)(2,1)S(1)} %shard_map.113.refs_0_), channel_id=1, source_target_pairs={{0,2},{1,3},{2,0},{3,1},{4,6},{5,7},{6,4},{7,5},{8,10},{9,11},{10,... | collective-permute-start | bytes 245768 | tf_op jit(solution)/shard_map/ppermute | solution.py:448
  11.6 12.9 %collective-permute-start.4 = (bf16[80,512]{1,0:T(8,128)(2,1)S(1)}, bf16[80,512]{1,0:T(8,128)(2,1)S(1)}, u32[]{:S(2)}, u32[]{:S(2)}) collective-permute-start(bf16[80,512]{1,0:T(8,128)(2,1)S(1)} %shard_map.113.refs_0_), channel_id=1, source_target_pairs={{0,3},{1,2},{2,1},{3,0},{4,7},{5,6},{6,5},{7,4},{8,11},{9,10},{10,... | collective-permute-start | bytes 245768 | tf_op jit(solution)/shard_map/ppermute | solution.py:448
  11.7 13.7 %collective-permute-start.5 = (bf16[80,512]{1,0:T(8,128)(2,1)S(1)}, bf16[80,512]{1,0:T(8,128)(2,1)S(1)}, u32[]{:S(2)}, u32[]{:S(2)}) collective-permute-start(bf16[80,512]{1,0:T(8,128)(2,1)S(1)} %shard_map.113.refs_0_), channel_id=1, source_target_pairs={{0,4},{1,5},{2,6},{3,7},{4,0},{5,1},{6,2},{7,3},{8,12},{9,13},{10,... | collective-permute-start | bytes 245768 | tf_op jit(solution)/shard_map/ppermute | solution.py:448
  14.6 13.5 %collective-permute-start.6 = (bf16[80,512]{1,0:T(8,128)(2,1)S(1)}, bf16[80,512]{1,0:T(8,128)(2,1)S(1)}, u32[]{:S(2)}, u32[]{:S(2)}) collective-permute-start(bf16[80,512]{1,0:T(8,128)(2,1)S(1)} %shard_map.113.refs_0_), channel_id=1, source_target_pairs={{0,5},{1,4},{2,7},{3,6},{4,1},{5,0},{6,3},{7,2},{8,13},{9,12},{10,... | collective-permute-start | bytes 245768 | tf_op jit(solution)/shard_map/ppermute | solution.py:448
  17.7 10.4 %collective-permute-start.7 = (bf16[80,512]{1,0:T(8,128)(2,1)S(1)}, bf16[80,512]{1,0:T(8,128)(2,1)S(1)}, u32[]{:S(2)}, u32[]{:S(2)}) collective-permute-start(bf16[80,512]{1,0:T(8,128)(2,1)S(1)} %shard_map.113.refs_0_), channel_id=1, source_target_pairs={{0,6},{1,7},{2,4},{3,5},{4,2},{5,3},{6,0},{7,1},{8,14},{9,15},{10,... | collective-permute-start | bytes 245768 | tf_op jit(solution)/shard_map/ppermute | solution.py:448
  23.4 8.3 %collective-permute-start.8 = (bf16[80,512]{1,0:T(8,128)(2,1)S(1)}, bf16[80,512]{1,0:T(8,128)(2,1)S(1)}, u32[]{:S(2)}, u32[]{:S(2)}) collective-permute-start(bf16[80,512]{1,0:T(8,128)(2,1)S(1)} %shard_map.113.refs_0_), channel_id=1, source_target_pairs={{0,7},{1,6},{2,5},{3,4},{4,3},{5,2},{6,1},{7,0},{8,15},{9,14},{10,... | collective-permute-start | bytes 245768 | tf_op jit(solution)/shard_map/ppermute | solution.py:448
  31.7 37.3 %collective-permute-start.9 = (bf16[8,80,512]{2,1,0:T(8,128)(2,1)S(1)}, bf16[8,80,512]{2,1,0:T(8,128)(2,1)S(1)}, u32[]{:S(2)}, u32[]{:S(2)}) collective-permute-start(bf16[8,80,512]{2,1,0:T(8,128)(2,1)S(1)} %shard_map.114.mine_ref), channel_id=1, source_target_pairs={{0,8},{8,0},{1,9},{9,1},{2,10},{10,2},{3,11},{11,3},{4,12},{12,4},... | collective-permute-start | bytes 1966088 | tf_op jit(solution)/shard_map/ppermute | solution.py:462
  33.5 33.8 %collective-permute-start = (bf16[8,112,256]{2,1,0:T(8,128)(2,1)S(1)}, bf16[8,112,256]{2,1,0:T(8,128)(2,1)S(1)}, u32[]{:S(2)}, u32[]{:S(2)}) collective-permute-start(bf16[8,112,256]{2,1,0:T(8,128)(2,1)S(1)} %get-tuple-element.14), channel_id=1, source_target_pairs={{0,2},{1,3},{2,4},{3,5},{4,6},{5,7},{6,8},{7,9},{8,10},{9,11},{10,... | collective-permute-start | bytes 1376264 | tf_op jit(solution)/shard_map/ppermute | solution.py:455
  35.8 31.5 %collective-permute-start.1 = (bf16[8,112,256]{2,1,0:T(8,128)(2,1)S(1)}, bf16[8,112,256]{2,1,0:T(8,128)(2,1)S(1)}, u32[]{:S(2)}, u32[]{:S(2)}) collective-permute-start(bf16[8,112,256]{2,1,0:T(8,128)(2,1)S(1)} %get-tuple-element.15), channel_id=1, source_target_pairs={{2,0},{3,1},{4,2},{5,3},{6,4},{7,5},{8,6},{9,7},{10,8},{11,9},{12,... | collective-permute-start | bytes 1376264 | tf_op jit(solution)/shard_map/ppermute | solution.py:456
  69.0 21.6 %copy-start.1 = (bf16[200,256]{1,0:T(8,128)(2,1)S(1)}, bf16[200,256]{1,0:T(8,128)(2,1)}, u32[]{:S(2)}) copy-start(bf16[200,256]{1,0:T(8,128)(2,1)} %query_ref.1) | copy-start | bytes 307204
  71.1 19.5 %collective-permute-start.10 = (f32[2,256,256]{2,1,0:T(8,128)S(1)}, f32[2,256,256]{2,1,0:T(8,128)S(1)}, u32[]{:S(2)}, u32[]{:S(2)}) collective-permute-start(f32[2,256,256]{2,1,0:T(8,128)S(1)} %get-tuple-element.21), channel_id=1, source_target_pairs={{0,1},{1,0},{2,3},{3,2},{4,5},{5,4},{6,7},{7,6},{8,9},{9,8},{10,11... | collective-permute-start | bytes 1572872 | tf_op jit(solution)/shard_map/ppermute | solution.py:474
where the time goes:
time: 93.4 us; the launch traced here: 93.2 us
  blocking collectives  45.7 us (49%)
  starting transfers between devices  28 us (30%)
  Pallas kernels  10.2 us (11%)
  waiting for transfers between devices  9.1 us (10%)
    all_to_all x2, blocking collectives, per_device(): stats = lax.all_to_all(stats, ALL, 0, 0, tiled=True)  45.7 us
    ppermute x7, starting transfers between devices, per_device(): lax.ppermute(shard, CHAN, [(i, i ^ k) for i in range(8)])  13.7 us
    pallas_call x8, Pallas kernels, call(): pl.pallas_call(kernel, out_shape=out_shape, in_specs=[pl.BlockSpec(memory...  10.2 us
    ppermute x7, waiting for transfers between devices, per_device(): lax.ppermute(shard, CHAN, [(i, i ^ k) for i in range(8)])  9.09 us
    all_to_all x1, starting transfers between devices, per_device(): own = lax.all_to_all(own_out, CHAN, 0, 0, tiled=True)  5.86 us
    ppermute x1, starting transfers between devices, per_device(): lax.ppermute(to_prev, ALL, [(i + 2, i) for i in range(everyone - 2)])  4.44 us
    ppermute x1, starting transfers between devices, per_device(): lax.ppermute(to_next, ALL, [(i, i + 2) for i in range(everyone - 2)])  2.33 us
  transfers between devices with their start and end apart: 12, of which 4 were waited for; matrix products, arithmetic and copies ran while one was open for 0% of the time, Pallas kernels for 3%

commit v1 on v0

--- a/solution.py
+++ b/solution.py
@@ -23,7 +23,6 @@
 SIDE_ROWS = 112
 MASK_AT = 72
 SHARD_ROWS = 80
-XORS = (4, 1, 2, 5, 6, 3, 7)
 
 
 def dot(a, b):
@@ -65,7 +64,7 @@
 
 
 def combine_kernel(stats_ref, rows_ref):
-    mean, spread, inner = combine(stats_ref[...].reshape(stats_ref.shape[0], 128))
+    mean, spread, inner = combine(stats_ref[...])
     rows_ref[0:1] = mean
     rows_ref[1:2] = spread
     rows_ref[2:3] = inner
@@ -98,13 +97,10 @@
         pltpu.make_async_copy(source, target, sems.at[i])
         for i, (source, target) in enumerate(pairs)
     ]
-    for copy in copies:
+    for copy in copies[1:] + copies[:1]:
         copy.start()
-    for copy in copies:
+    for copy in copies[1:]:
         copy.wait()
-    for t in range(4):
-        piece = fine_ref[:, :, :, 128 * t : 128 * t + 128].astype(F32)
-        rows[t] = piece.reshape(48 * 8, 128)
     for n in range(2):
         for t in range(2):
             piece = coarse_ref[n, :, :, 128 * t : 128 * t + 128].astype(F32)
@@ -123,6 +119,24 @@
     for q in range(4):
         for h in range(2):
             d = 2 * q + h
+            own_ref[d, 48:64, :] = packed
+            coarse_extra = jnp.zeros((32, 128), F32)
+            for n in range(2):
+                row = coarse[n, h, :, q, :].astype(BF16)
+                own_ref[d, 64:80, 128 * n : 128 * n + 128] = row[0:16]
+                own_ref[d, 64:80, 256 + 128 * n : 384 + 128 * n] = row[16:32]
+                row = coarse[n, 1 - h, :, q, :]
+                edge = row[:, 0:1] if h == 0 else row[:, 127:128]
+                coarse_extra += jnp.where(coarse_lane // 4 == n, edge, 0.0)
+            own_ref[d, 80:96, 256:384] = coarse_extra[0:16].astype(BF16)
+            own_ref[d, 80:96, 384:512] = coarse_extra[16:32].astype(BF16)
+    copies[0].wait()
+    for t in range(4):
+        piece = fine_ref[:, :, :, 128 * t : 128 * t + 128].astype(F32)
+        rows[t] = piece.reshape(48 * 8, 128)
+    for q in range(4):
+        for h in range(2):
+            d = 2 * q + h
             fine_extra = jnp.zeros((24, 128), F32)
             for r in range(2):
                 for t in range(2):
@@ -134,22 +148,9 @@
                 for n in range(2):
                     at = 4 * n + 1 + r
                     fine_extra += jnp.where(fine_lane == at, edge[24 * n : 24 * n + 24], 0.0)
-            own_ref[d, 48:64, :] = packed
-            coarse_extra = jnp.zeros((32, 128), F32)
-            for n in range(2):
-                row = coarse[n, h, :, q, :].astype(BF16)
-                own_ref[d, 64:80, 128 * n : 128 * n + 128] = row[0:16]
-                own_ref[d, 64:80, 256 + 128 * n : 384 + 128 * n] = row[16:32]
-                row = coarse[n, 1 - h, :, q, :]
-                edge = row[:, 0:1] if h == 0 else row[:, 127:128]
-                coarse_extra += jnp.where(coarse_lane // 4 == n, edge, 0.0)
-            extra = [
-                fine_extra[0:16],
-                jnp.concatenate([fine_extra[16:24], jnp.zeros((8, 128), F32)], axis=0),
-                coarse_extra[0:16],
-                coarse_extra[16:32],
-            ]
-            own_ref[d, 80:96, :] = jnp.concatenate(extra, axis=1).astype(BF16)
+            tail = jnp.concatenate([fine_extra[16:24], jnp.zeros((8, 128), F32)], axis=0)
+            own_ref[d, 80:96, 0:128] = fine_extra[0:16].astype(BF16)
+            own_ref[d, 80:96, 128:256] = tail.astype(BF16)
 
 
 def pack_weights_kernel(conv_ref, mask_ref, shard_ref):
@@ -163,11 +164,17 @@
         shard_ref[8 * k : 8 * k + 8] = piece
 
 
-def arrange_kernel(*refs):
-    chan = lax.axis_index("chan_0") * 2 + lax.axis_index("chan_1")
-    all_ref = refs[-1]
-    for k, ref in enumerate(refs[:-1]):
-        all_ref[chan ^ k] = ref[...]
+def line_kernel(shard_ref, one_ref, two_ref, three_ref, line_ref):
+    x = lax.axis_index("chan_0")
+    for k, ref in enumerate((shard_ref, one_ref, two_ref, three_ref)):
+        line_ref[(x - k + 4) % 4] = ref[...]
+
+
+def arrange_kernel(line_ref, partner_ref, all_ref):
+    side = lax.axis_index("chan_1")
+    for x in range(4):
+        all_ref[2 * x + side] = line_ref[x]
+        all_ref[2 * x + 1 - side] = partner_ref[x]
 
 
 def lateral_kernel(own_ref, weight_ref, stats_ref, next_ref, prev_ref):
@@ -188,7 +195,7 @@
     for n in range(2):
         lateral = dot(weight_ref[:, 0:IN_CH], fine_rows(own_ref, n, 0, COLS))
         total = total + local_stats(lateral, lane, 64 * n)
-    stats_ref[...] = jnp.broadcast_to(total[None], stats_ref.shape)
+    stats_ref[...] = jnp.broadcast_to(total, stats_ref.shape)
 
 
 def join_kernel(
@@ -360,7 +367,7 @@
         keep_ref[n] = jnp.where(side == 0, out[0], out[1])
         send_ref[n] = jnp.where(side == 0, out[1], out[0])
         total = total + local_stats(jnp.concatenate(out, axis=1), lane, 64 * n)
-    stats_ref[...] = jnp.broadcast_to(total[None], stats_ref.shape)
+    stats_ref[...] = jnp.broadcast_to(total, stats_ref.shape)
 
 
 def query_kernel(
@@ -378,7 +385,7 @@
     gain = vector_col(lat_weight_ref, 2)
     shift = vector_col(lat_weight_ref, 3)
     bias = vector_col(lat_weight_ref, 4)
-    rows = combine(out_stats_ref[...].reshape(out_stats_ref.shape[0], 128))
+    rows = combine(out_stats_ref[...])
     for n in range(2):
         mean, var = stat_cols(rows, n)
         scale = lax.rsqrt(var + EPS) * gain
@@ -388,8 +395,9 @@
             logits = dot(query_ref[...], features)
             shifted = logits - jnp.max(logits, axis=0, keepdims=True)
             result = shifted - jnp.log(jnp.sum(jnp.exp(shifted), axis=0, keepdims=True))
-            at = pl.multiple_of(half * HALF, HALF)
-            out_ref[n, :, 0, pl.ds(at, HALF)] = result
+            for t in range(2):
+                at = 4 * QUERIES * n + 2 * half + t
+                out_ref[pl.ds(at, QUERIES, stride=4), :] = result[:, 128 * t : 128 * t + 128]
 
 
 def call(kernel, out_shape, scratch=(), flops=0, space=pltpu.VMEM, limit=40 << 20):
@@ -420,7 +428,7 @@
     queries,
 ):
     everyone = lax.axis_size(ALL)
-    stats_shape = jax.ShapeDtypeStruct((everyone, 1, 128), F32)
+    stats_shape = jax.ShapeDtypeStruct((everyone, 128), F32)
     shard_shape = jax.ShapeDtypeStruct((SHARD_ROWS, COLS), BF16)
     all_shape = jax.ShapeDtypeStruct((8, SHARD_ROWS, COLS), BF16)
     side_shape = jax.ShapeDtypeStruct((8, SIDE_ROWS, HALF), BF16)
@@ -445,20 +453,21 @@
     )(fine_features, coarse_level, lat_weight, *vectors)
     own = lax.all_to_all(own_out, CHAN, 0, 0, tiled=True)
     shard = call(pack_weights_kernel, shard_shape)(out_weight, mask_weight)
-    moved = [lax.ppermute(shard, CHAN, [(i, i ^ k) for i in range(8)]) for k in XORS]
+    moved = [lax.ppermute(shard, "chan_0", [(i, (i + k) % 4) for i in range(4)]) for k in (1, 2, 3)]
 
     full_lat, stats, to_next, to_prev = call(
         lateral_kernel,
         [jax.ShapeDtypeStruct((D, 256), BF16), stats_shape, side_shape, side_shape],
         flops=2 * 2 * 256 * 256 * 512,
     )(own)
-    above = lax.ppermute(to_next, ALL, [(i, i + 2) for i in range(everyone - 2)])
-    below = lax.ppermute(to_prev, ALL, [(i + 2, i) for i in range(everyone - 2)])
+    above = lax.ppermute(to_next, ALL, [(i, (i + 2) % everyone) for i in range(everyone)])
+    below = lax.ppermute(to_prev, ALL, [((i + 2) % everyone, i) for i in range(everyone)])
+    line = call(line_kernel, jax.ShapeDtypeStruct((4, SHARD_ROWS, COLS), BF16))(shard, *moved)
+    partner = lax.ppermute(line, "chan_1", swap)
     stats = lax.all_to_all(stats, ALL, 0, 0, tiled=True)
     stats = call(combine_kernel, jax.ShapeDtypeStruct((8, 128), F32), flops=1 << 20)(stats)
 
-    by_xor = dict(zip(XORS, moved))
-    mine = call(arrange_kernel, all_shape)(shard, *[by_xor[k] for k in range(1, 8)])
+    mine = call(arrange_kernel, all_shape)(line, partner)
     other = lax.ppermute(mine, "band_2", swap)
     joined, beside = call(
         join_kernel,
@@ -473,12 +482,13 @@
     )(joined, beside, mine, other)
     taken = lax.ppermute(send, "chan_1", swap)
     stats = lax.all_to_all(stats, ALL, 0, 0, tiled=True)
-    return call(
+    log_probs = call(
         query_kernel,
-        jax.ShapeDtypeStruct((2, QUERIES, 1, COLS), F32),
+        jax.ShapeDtypeStruct((2 * QUERIES * 4, 128), F32),
         (pltpu.VMEM((D, D), BF16),),
         flops=2 * 2 * 256 * 256 * 512 * 2,
     )(keep, taken, stats, full_lat, mine, other, queries)
+    return log_probs.reshape(2, QUERIES, 1, COLS)
 
 
 def solution(mesh):

time: 93.4 us -> 91.1 us (0.975)
  starting transfers between devices: 28 us -> 18.8 us
  waiting for transfers between devices: 9.1 us -> 15.9 us
    ppermute x9 -> x6, starting transfers between devices: 20.5 us -> 9.32 us  [the longest x3 5.11 us: per_device(): lax.ppermute(shard, 'chan_0', [(i, (i + k) % 4) for i in range(4)])]
    ppermute x9 -> x6, waiting for transfers between devices: 9.09 us -> 15.9 us  [the longest x3 9.72 us: per_device(): lax.ppermute(shard, 'chan_0', [(i, (i + k) % 4) for i in range(4)])]
    ppermute x1, starting transfers between devices: 1.12 us -> 2.96 us  [per_device(): other = lax.ppermute(mine, 'band_2', swap)]
    pallas_call x8 -> x9, Pallas kernels: 10.2 us -> 9.87 us  [call(): pl.pallas_call(kernel, out_shape=out_shape, in_specs=[pl.BlockSpec(memory...]
  transfers between devices with their start and end apart: 12 -> 9, of which waited for: 4 -> 3; matrix products, arithmetic and copies ran while one was open for 0% -> 0% of each run, Pallas kernels for 3% -> 3%
where the time goes in v1:
time: 91.1 us; the launch traced here: 90.9 us
  blocking collectives  46.3 us (51%)
  starting transfers between devices  18.8 us (21%)
  waiting for transfers between devices  15.9 us (17%)
  Pallas kernels  9.87 us (11%)
    all_to_all x2, blocking collectives, per_device(): stats = lax.all_to_all(stats, ALL, 0, 0, tiled=True)  46.3 us
    pallas_call x9, Pallas kernels, call(): pl.pallas_call(kernel, out_shape=out_shape, in_specs=[pl.BlockSpec(memory...  9.87 us
    ppermute x3, waiting for transfers between devices, per_device(): lax.ppermute(shard, 'chan_0', [(i, (i + k) % 4) for i in range(4)])  9.72 us
    ppermute x1, waiting for transfers between devices, per_device(): partner = lax.ppermute(line, 'chan_1', swap)  6.15 us
    all_to_all x1, starting transfers between devices, per_device(): own = lax.all_to_all(own_out, CHAN, 0, 0, tiled=True)  5.86 us
    ppermute x3, starting transfers between devices, per_device(): lax.ppermute(shard, 'chan_0', [(i, (i + k) % 4) for i in range(4)])  5.11 us
    ppermute x1, starting transfers between devices, per_device(): other = lax.ppermute(mine, 'band_2', swap)  2.96 us
    ppermute x1, starting transfers between devices, per_device(): lax.ppermute(to_prev, ALL, [((i + 2) % everyone, i) for i in range(everyo...  2.94 us
  transfers between devices with their start and end apart: 9, of which 3 were waited for; matrix products, arithmetic and copies ran while one was open for 0% of the time, Pallas kernels for 3%

profile of v1, /device:TPU:1, one launch (start us, length us, event | category | flops | bytes accessed | tf_op | source)
XLA Modules:
  0.0 90.9 jit_solution(3905652584462901029)
XLA Ops:
  0.0 0.0 copy-start
  0.0 0.0 copy-start.2
  0.0 2.9 %shard_map.109 = bf16[8,96,512]{2,1,0:T(8,128)(2,1)} custom-call(bf16[2,24,8,512]{3,2,1,0:T(8,128)(2,1)} %fine_hbm.1, bf16[2,32,4,256]{3,2,1,0:T(4,128)(2,1)} %coarse_hbm.1, bf16[32,192]{1,0:T(8,128)(2,1)} %weight_hbm.1, bf16[1,32]{1,0:T(2,128)(2,1)} %bitcast.18, bf16[1,32]{1,0:T(2,128)(2,1)} %bitcast.19, bf16[1,32]{1,0:T(2,128)(2,1)} %bitcast.20, ...), custom_call_target="tpu_custom_call" | custom-call | bytes 1048576 | tf_op jit(solution)/shard_map/pallas_call | solution.py:406
  2.9 5.9 %all-to-all-start = ((bf16[8,96,512]{2,1,0:T(8,128)(2,1)}), bf16[8,96,512]{2,1,0:T(8,128)(2,1)S(1)}, u32[]{:S(2)}, u32[]{:S(2)}) async-start(bf16[8,96,512]{2,1,0:T(8,128)(2,1)} %shard_map.109), calls=%async_computation | async-start | bytes 1572864 | tf_op jit(solution)/shard_map/all_to_all | solution.py:454
  8.8 0.0 copy-done
  8.8 0.0 copy-done.2
  8.8 1.5 %collective-permute-start.2 = (bf16[80,512]{1,0:T(8,128)(2,1)S(1)}, bf16[80,512]{1,0:T(8,128)(2,1)S(1)}, u32[]{:S(2)}, u32[]{:S(2)}) collective-permute-start(bf16[80,512]{1,0:T(8,128)(2,1)S(1)} %shard_map.113.shard_ref), channel_id=1, source_target_pairs={{0,2},{2,4},{4,6},{6,0},{1,3},{3,5},{5,7},{7,1},{8,10},{10,12},{12... | collective-permute-start | bytes 245768 | tf_op jit(solution)/shard_map/ppermute | solution.py:456
  10.4 2.4 %collective-permute-start.3 = (bf16[80,512]{1,0:T(8,128)(2,1)S(1)}, bf16[80,512]{1,0:T(8,128)(2,1)S(1)}, u32[]{:S(2)}, u32[]{:S(2)}) collective-permute-start(bf16[80,512]{1,0:T(8,128)(2,1)S(1)} %shard_map.113.shard_ref), channel_id=1, source_target_pairs={{0,4},{2,6},{4,0},{6,2},{1,5},{3,7},{5,1},{7,3},{8,12},{10,14},{12... | collective-permute-start | bytes 245768 | tf_op jit(solution)/shard_map/ppermute | solution.py:456
  12.8 1.2 %collective-permute-start.4 = (bf16[80,512]{1,0:T(8,128)(2,1)S(1)}, bf16[80,512]{1,0:T(8,128)(2,1)S(1)}, u32[]{:S(2)}, u32[]{:S(2)}) collective-permute-start(bf16[80,512]{1,0:T(8,128)(2,1)S(1)} %shard_map.113.shard_ref), channel_id=1, source_target_pairs={{0,6},{2,0},{4,2},{6,4},{1,7},{3,1},{5,3},{7,5},{8,14},{10,8},{12,... | collective-permute-start | bytes 245768 | tf_op jit(solution)/shard_map/ppermute | solution.py:456
  14.0 4.8 %collective-permute-done.2.one_ref = bf16[80,512]{1,0:T(8,128)(2,1)S(1)} collective-permute-done((bf16[80,512]{1,0:T(8,128)(2,1)S(1)}, bf16[80,512]{1,0:T(8,128)(2,1)S(1)}, u32[]{:S(2)}, u32[]{:S(2)}) %collective-permute-start.2) | collective-permute-done | bytes 81952 | tf_op jit(solution)/shard_map/ppermute | solution.py:456
  18.8 4.9 %collective-permute-done.3.two_ref = bf16[80,512]{1,0:T(8,128)(2,1)S(1)} collective-permute-done((bf16[80,512]{1,0:T(8,128)(2,1)S(1)}, bf16[80,512]{1,0:T(8,128)(2,1)S(1)}, u32[]{:S(2)}, u32[]{:S(2)}) %collective-permute-start.3) | collective-permute-done | bytes 81952 | tf_op jit(solution)/shard_map/ppermute | solution.py:456
  23.7 0.0 collective-permute-done.4.three_ref
  23.7 1.2 %collective-permute-start.5 = (bf16[4,80,512]{2,1,0:T(8,128)(2,1)S(1)}, bf16[4,80,512]{2,1,0:T(8,128)(2,1)S(1)}, u32[]{:S(2)}, u32[]{:S(2)}) collective-permute-start(bf16[4,80,512]{2,1,0:T(8,128)(2,1)S(1)} %shard_map.114.line_ref), channel_id=1, source_target_pairs={{0,1},{1,0},{2,3},{3,2},{4,5},{5,4},{6,7},{7,6},{8,9},{9,8},{10,11... | collective-permute-start | bytes 983048 | tf_op jit(solution)/shard_map/ppermute | solution.py:466
  24.9 6.2 %collective-permute-done.5.partner_ref = bf16[4,80,512]{2,1,0:T(8,128)(2,1)S(1)} collective-permute-done((bf16[4,80,512]{2,1,0:T(8,128)(2,1)S(1)}, bf16[4,80,512]{2,1,0:T(8,128)(2,1)S(1)}, u32[]{:S(2)}, u32[]{:S(2)}) %collective-permute-start.5) | collective-permute-done | bytes 327712 | tf_op jit(solution)/shard_map/ppermute | solution.py:466
  31.1 0.1 shard_map.115.mine_ref
  31.1 3.0 %collective-permute-start.6 = (bf16[8,80,512]{2,1,0:T(8,128)(2,1)S(1)}, bf16[8,80,512]{2,1,0:T(8,128)(2,1)S(1)}, u32[]{:S(2)}, u32[]{:S(2)}) collective-permute-start(bf16[8,80,512]{2,1,0:T(8,128)(2,1)S(1)} %shard_map.115.mine_ref), channel_id=1, source_target_pairs={{0,8},{8,0},{1,9},{9,1},{2,10},{10,2},{3,11},{11,3},{4,12},{12,4},... | collective-permute-start | bytes 1966088 | tf_op jit(solution)/shard_map/ppermute | solution.py:471
  34.1 0.0 all-to-all-done.own_ref
  34.1 0.6 shard_map.110
  34.7 0.1 collective-permute-start
  34.8 2.9 %collective-permute-start.1 = (bf16[8,112,256]{2,1,0:T(8,128)(2,1)S(1)}, bf16[8,112,256]{2,1,0:T(8,128)(2,1)S(1)}, u32[]{:S(2)}, u32[]{:S(2)}) collective-permute-start(bf16[8,112,256]{2,1,0:T(8,128)(2,1)S(1)} %get-tuple-element.15), channel_id=1, source_target_pairs={{2,0},{3,1},{4,2},{5,3},{6,4},{7,5},{8,6},{9,7},{10,8},{11,9},{12,... | collective-permute-start | bytes 1376264 | tf_op jit(solution)/shard_map/ppermute | solution.py:464
  37.7 27.4 %all_to_all.27 = f32[256,1,128]{2,1,0:T(1,128)S(1)} all-to-all(f32[256,1,128]{2,1,0:T(1,128)S(1)} %bitcast.16), channel_id=1, replica_groups=mesh['band_0'=8,'band_1'=2,'band_2'=2,'chan_0'=4,'chan_1'=2] {'band_0','..., dimensions={0} | all-to-all | bytes 262144 | tf_op jit(solution)/shard_map/all_to_all | solution.py:467
  65.1 0.1 shard_map.111.lat_stats_ref
  65.2 0.0 collective-permute-done.above_ref
  65.2 0.0 collective-permute-done.1.below_ref
  65.2 1.7 %shard_map.112 = (bf16[2,768,512]{2,1,0:T(8,128)(2,1)S(1)}, bf16[768,128]{1,0:T(8,128)(2,1)S(1)}) custom-call(bf16[8,96,512]{2,1,0:T(8,128)(2,1)S(1)} %all-to-all-done.own_ref, bf16[8,112,256]{2,1,0:T(8,128)(2,1)S(1)} %collective-permute-done.above_ref, bf16[8,112,256]{2,1,0:T(8,128)(2,1)S(1)} %collective-permute-done.1.below_ref, ...), custom_call_target="tpu_custom_call" | custom-call | flops 939524096 | bytes 1048576 | tf_op jit(solution)/shard_map/pallas_call | solution.py:406
  66.9 0.0 collective-permute-done.6.other_ref
  66.9 0.0 copy-start.1
  66.9 2.0 %shard_map.116 = (f32[2,256,256]{2,1,0:T(8,128)S(1)}, f32[2,256,256]{2,1,0:T(8,128)S(1)}, f32[256,128]{1,0:T(8,128)S(1)}) custom-call(bf16[2,768,512]{2,1,0:T(8,128)(2,1)S(1)} %get-tuple-element.18.joined_ref, bf16[768,128]{1,0:T(8,128)(2,1)S(1)} %get-tuple-element.19.beside_ref, bf16[8,80,512]{2,1,0:T(8,128)(2,1)S(1)} %shard_map.115.mine_ref, ...), custom_call_target="tpu_custom_call" | custom-call | flops 1207959552 | bytes 1048576 | tf_op jit(solution)/shard_map/pallas_call | solution.py:406
  69.0 0.6 collective-permute-start.7
  69.6 18.9 %all_to_all.28 = f32[256,1,128]{2,1,0:T(1,128)S(1)} all-to-all(f32[256,1,128]{2,1,0:T(1,128)S(1)} %bitcast.17), channel_id=1, replica_groups=mesh['band_0'=8,'band_1'=2,'band_2'=2,'chan_0'=4,'chan_1'=2] {'band_0','..., dimensions={0} | all-to-all | bytes 262144 | tf_op jit(solution)/shard_map/all_to_all | solution.py:484
  88.5 0.0 collective-permute-done.7.taken_ref
  88.5 0.0 copy-done.1
  88.5 2.5 %shard_map.117 = f32[1600,128]{1,0:T(8,128)} custom-call(f32[2,256,256]{2,1,0:T(8,128)S(1)} %get-tuple-element.20.keep_ref, f32[2,256,256]{2,1,0:T(8,128)S(1)} %collective-permute-done.7.taken_ref, f32[256,128]{1,0:T(8,128)S(1)} %bitcast.14, bf16[256,256]{1,0:T(8,128)(2,1)S(1)} %get-tuple-element.16.lat_weight_ref, ...), custom_call_target="tpu_custom_call" | custom-call | flops 268435456 | bytes 1048576 | tf_op jit(solution)/shard_map/pallas_call | solution.py:406
  (2 shorter events, 0.1 us)
Async XLA Ops:
  0.0 8.8 %copy-start = (bf16[3,3,32,256]{3,2,1,0:T(8,128)(2,1)S(1)}, bf16[3,3,32,256]{3,2,1,0:T(8,128)(2,1)}, u32[]{:S(2)}) copy-start(bf16[3,3,32,256]{3,2,1,0:T(8,128)(2,1)} %conv_ref.1) | copy-start | bytes 442372
  0.0 8.8 %copy-start.2 = (bf16[32,256]{1,0:T(8,128)(2,1)S(1)}, bf16[32,256]{1,0:T(8,128)(2,1)}, u32[]{:S(2)}) copy-start(bf16[32,256]{1,0:T(8,128)(2,1)} %mask_ref.1) | copy-start | bytes 49156
  2.9 31.1 %all-to-all-start = ((bf16[8,96,512]{2,1,0:T(8,128)(2,1)}), bf16[8,96,512]{2,1,0:T(8,128)(2,1)S(1)}, u32[]{:S(2)}, u32[]{:S(2)}) async-start(bf16[8,96,512]{2,1,0:T(8,128)(2,1)} %shard_map.109), calls=%async_computation | async-start | bytes 1572864 | tf_op jit(solution)/shard_map/all_to_all | solution.py:454
  8.8 9.9 %collective-permute-start.2 = (bf16[80,512]{1,0:T(8,128)(2,1)S(1)}, bf16[80,512]{1,0:T(8,128)(2,1)S(1)}, u32[]{:S(2)}, u32[]{:S(2)}) collective-permute-start(bf16[80,512]{1,0:T(8,128)(2,1)S(1)} %shard_map.113.shard_ref), channel_id=1, source_target_pairs={{0,2},{2,4},{4,6},{6,0},{1,3},{3,5},{5,7},{7,1},{8,10},{10,12},{12... | collective-permute-start | bytes 245768 | tf_op jit(solution)/shard_map/ppermute | solution.py:456
  10.4 13.3 %collective-permute-start.3 = (bf16[80,512]{1,0:T(8,128)(2,1)S(1)}, bf16[80,512]{1,0:T(8,128)(2,1)S(1)}, u32[]{:S(2)}, u32[]{:S(2)}) collective-permute-start(bf16[80,512]{1,0:T(8,128)(2,1)S(1)} %shard_map.113.shard_ref), channel_id=1, source_target_pairs={{0,4},{2,6},{4,0},{6,2},{1,5},{3,7},{5,1},{7,3},{8,12},{10,14},{12... | collective-permute-start | bytes 245768 | tf_op jit(solution)/shard_map/ppermute | solution.py:456
  12.8 10.9 %collective-permute-start.4 = (bf16[80,512]{1,0:T(8,128)(2,1)S(1)}, bf16[80,512]{1,0:T(8,128)(2,1)S(1)}, u32[]{:S(2)}, u32[]{:S(2)}) collective-permute-start(bf16[80,512]{1,0:T(8,128)(2,1)S(1)} %shard_map.113.shard_ref), channel_id=1, source_target_pairs={{0,6},{2,0},{4,2},{6,4},{1,7},{3,1},{5,3},{7,5},{8,14},{10,8},{12,... | collective-permute-start | bytes 245768 | tf_op jit(solution)/shard_map/ppermute | solution.py:456
  23.7 7.3 %collective-permute-start.5 = (bf16[4,80,512]{2,1,0:T(8,128)(2,1)S(1)}, bf16[4,80,512]{2,1,0:T(8,128)(2,1)S(1)}, u32[]{:S(2)}, u32[]{:S(2)}) collective-permute-start(bf16[4,80,512]{2,1,0:T(8,128)(2,1)S(1)} %shard_map.114.line_ref), channel_id=1, source_target_pairs={{0,1},{1,0},{2,3},{3,2},{4,5},{5,4},{6,7},{7,6},{8,9},{9,8},{10,11... | collective-permute-start | bytes 983048 | tf_op jit(solution)/shard_map/ppermute | solution.py:466
  31.1 35.8 %collective-permute-start.6 = (bf16[8,80,512]{2,1,0:T(8,128)(2,1)S(1)}, bf16[8,80,512]{2,1,0:T(8,128)(2,1)S(1)}, u32[]{:S(2)}, u32[]{:S(2)}) collective-permute-start(bf16[8,80,512]{2,1,0:T(8,128)(2,1)S(1)} %shard_map.115.mine_ref), channel_id=1, source_target_pairs={{0,8},{8,0},{1,9},{9,1},{2,10},{10,2},{3,11},{11,3},{4,12},{12,4},... | collective-permute-start | bytes 1966088 | tf_op jit(solution)/shard_map/ppermute | solution.py:471
  34.7 30.5 %collective-permute-start = (bf16[8,112,256]{2,1,0:T(8,128)(2,1)S(1)}, bf16[8,112,256]{2,1,0:T(8,128)(2,1)S(1)}, u32[]{:S(2)}, u32[]{:S(2)}) collective-permute-start(bf16[8,112,256]{2,1,0:T(8,128)(2,1)S(1)} %get-tuple-element.14), channel_id=1, source_target_pairs={{0,2},{1,3},{2,4},{3,5},{4,6},{5,7},{6,8},{7,9},{8,10},{9,11},{10,... | collective-permute-start | bytes 1376264 | tf_op jit(solution)/shard_map/ppermute | solution.py:463
  34.8 30.4 %collective-permute-start.1 = (bf16[8,112,256]{2,1,0:T(8,128)(2,1)S(1)}, bf16[8,112,256]{2,1,0:T(8,128)(2,1)S(1)}, u32[]{:S(2)}, u32[]{:S(2)}) collective-permute-start(bf16[8,112,256]{2,1,0:T(8,128)(2,1)S(1)} %get-tuple-element.15), channel_id=1, source_target_pairs={{2,0},{3,1},{4,2},{5,3},{6,4},{7,5},{8,6},{9,7},{10,8},{11,9},{12,... | collective-permute-start | bytes 1376264 | tf_op jit(solution)/shard_map/ppermute | solution.py:464
  66.9 21.5 %copy-start.1 = (bf16[200,256]{1,0:T(8,128)(2,1)S(1)}, bf16[200,256]{1,0:T(8,128)(2,1)}, u32[]{:S(2)}) copy-start(bf16[200,256]{1,0:T(8,128)(2,1)} %query_ref.1) | copy-start | bytes 307204
  69.0 19.5 %collective-permute-start.7 = (f32[2,256,256]{2,1,0:T(8,128)S(1)}, f32[2,256,256]{2,1,0:T(8,128)S(1)}, u32[]{:S(2)}, u32[]{:S(2)}) collective-permute-start(f32[2,256,256]{2,1,0:T(8,128)S(1)} %get-tuple-element.21), channel_id=1, source_target_pairs={{0,1},{1,0},{2,3},{3,2},{4,5},{5,4},{6,7},{7,6},{8,9},{9,8},{10,11... | collective-permute-start | bytes 1572872 | tf_op jit(solution)/shard_map/ppermute | solution.py:483

commit v2 on v1

--- a/solution.py
+++ b/solution.py
@@ -19,9 +19,13 @@
 EPS = 1e-05
 F32 = jnp.float32
 BF16 = jnp.bfloat16
-OWN_ROWS = 96
-SIDE_ROWS = 112
+OWN_ROWS = 80
+VECTORS = 64
+FINE_EDGE = 72
+COARSE_EDGE = 80
+SIDE_ROWS = 96
 MASK_AT = 72
+XORS = (4, 1, 2, 5, 6, 3, 7)
 SHARD_ROWS = 80
 
 
@@ -72,7 +76,7 @@
 
 
 def vector_col(lat_weight_ref, index):
-    return lat_weight_ref[:, 128:256].astype(F32)[:, 64 + index : 65 + index]
+    return lat_weight_ref[:, 128:256].astype(F32)[:, VECTORS + index : VECTORS + index + 1]
 
 
 def lanes_of(shape):
@@ -85,59 +89,57 @@
     )
 
 
-def pack_own_kernel(
-    fine_hbm, coarse_hbm, weight_hbm, *refs
-):
-    vec_hbm, own_ref, (fine_ref, coarse_ref, weight_ref, vec_ref, rows, coarse, sems) = (
-        refs[:5], refs[5], refs[6:]
-    )
-    pairs = [(fine_hbm, fine_ref), (coarse_hbm, coarse_ref), (weight_hbm, weight_ref)]
-    pairs += [(vec, vec_ref.at[i]) for i, vec in enumerate(vec_hbm)]
+def pack_own_kernel(fine_hbm, coarse_hbm, weight_hbm, *refs):
+    vec_hbm, own_hbm = refs[:5], refs[5]
+    fine_ref, coarse_ref, weight_ref, vec_ref, own_ref, rows, coarse, sems, out_sems = refs[6:]
+    pairs = [(coarse_hbm, coarse_ref), (weight_hbm, weight_ref)]
+    pairs += [(vec, vec_ref.at[i]) for i, vec in enumerate(vec_hbm)] + [(fine_hbm, fine_ref)]
     copies = [
         pltpu.make_async_copy(source, target, sems.at[i])
         for i, (source, target) in enumerate(pairs)
     ]
-    for copy in copies[1:] + copies[:1]:
+    for copy in copies:
         copy.start()
-    for copy in copies[1:]:
+    for copy in copies[:-1]:
         copy.wait()
     for n in range(2):
         for t in range(2):
             piece = coarse_ref[n, :, :, 128 * t : 128 * t + 128].astype(F32)
-            coarse[n, t, :, 0:4, :] = piece
+            piece = jnp.concatenate([piece, jnp.zeros_like(piece)], axis=1)
+            coarse[n, t] = piece.reshape(256, 128)
+    lane = lanes_of((32, 128))
     vec_lane = lanes_of((32, 32))
     vec_row = lax.broadcasted_iota(jnp.int32, (32, 32), 0)
-    columns = jnp.zeros((32, 256 - IN_CH), F32)
+    weight = weight_ref[...].astype(F32)
+    second = jnp.concatenate([weight[:, 128:IN_CH], jnp.zeros((32, 256 - IN_CH), F32)], axis=1)
     for i in range(5):
         vec = jnp.where(vec_lane == vec_row, vec_ref[i].astype(F32), 0.0)
-        column = jnp.sum(vec, axis=1, keepdims=True)
-        columns += jnp.where(lanes_of((32, 256 - IN_CH)) == i, column, 0.0)
-    weight = jnp.concatenate([weight_ref[...].astype(F32), columns], axis=1)
-    packed = jnp.concatenate([weight[0:16], weight[16:32]], axis=1).astype(BF16)
-    fine_lane = lanes_of((24, 128))
-    coarse_lane = lanes_of((32, 128))
-    for q in range(4):
-        for h in range(2):
+        second += jnp.where(lane == VECTORS + i, jnp.sum(vec, axis=1, keepdims=True), 0.0)
+    first = weight[:, 0:128].astype(BF16)
+    tails = []
+    for h in range(2):
+        for q in range(4):
             d = 2 * q + h
-            own_ref[d, 48:64, :] = packed
-            coarse_extra = jnp.zeros((32, 128), F32)
+            tail = second
+            own_ref[d, 48:64, 0:128] = first[0:16]
+            own_ref[d, 48:64, 256:384] = first[16:32]
             for n in range(2):
-                row = coarse[n, h, :, q, :].astype(BF16)
+                row = coarse[n, h, pl.ds(q, 32, stride=8), :].astype(BF16)
                 own_ref[d, 64:80, 128 * n : 128 * n + 128] = row[0:16]
                 own_ref[d, 64:80, 256 + 128 * n : 384 + 128 * n] = row[16:32]
-                row = coarse[n, 1 - h, :, q, :]
+                row = coarse[n, 1 - h, pl.ds(q, 32, stride=8), :]
                 edge = row[:, 0:1] if h == 0 else row[:, 127:128]
-                coarse_extra += jnp.where(coarse_lane // 4 == n, edge, 0.0)
-            own_ref[d, 80:96, 256:384] = coarse_extra[0:16].astype(BF16)
-            own_ref[d, 80:96, 384:512] = coarse_extra[16:32].astype(BF16)
-    copies[0].wait()
+                tail = jnp.where(lane // 4 == COARSE_EDGE // 4 + n, edge, tail)
+            tails.append(tail)
+    copies[-1].wait()
     for t in range(4):
         piece = fine_ref[:, :, :, 128 * t : 128 * t + 128].astype(F32)
         rows[t] = piece.reshape(48 * 8, 128)
-    for q in range(4):
-        for h in range(2):
+    out = []
+    for h in range(2):
+        for q in range(4):
             d = 2 * q + h
-            fine_extra = jnp.zeros((24, 128), F32)
+            tail = tails[4 * h + q]
             for r in range(2):
                 for t in range(2):
                     row = rows[2 * h + t, pl.ds(2 * q + r, 48, stride=8), :]
@@ -146,11 +148,17 @@
                 row = rows[2 - h, pl.ds(2 * q + r, 48, stride=8), :]
                 edge = row[:, 0:1] if h == 0 else row[:, 127:128]
                 for n in range(2):
-                    at = 4 * n + 1 + r
-                    fine_extra += jnp.where(fine_lane == at, edge[24 * n : 24 * n + 24], 0.0)
-            tail = jnp.concatenate([fine_extra[16:24], jnp.zeros((8, 128), F32)], axis=0)
-            own_ref[d, 80:96, 0:128] = fine_extra[0:16].astype(BF16)
-            own_ref[d, 80:96, 128:256] = tail.astype(BF16)
+                    column = jnp.concatenate(
+                        [edge[24 * n : 24 * n + 24], jnp.zeros((8, 1), F32)], axis=0
+                    )
+                    tail = jnp.where(lane == FINE_EDGE + 4 * n + 1 + r, column, tail)
+            tail = tail.astype(BF16)
+            own_ref[d, 48:64, 128:256] = tail[0:16]
+            own_ref[d, 48:64, 384:512] = tail[16:32]
+            out.append(pltpu.make_async_copy(own_ref.at[d], own_hbm.at[d], out_sems.at[d]))
+            out[-1].start()
+    for copy in out:
+        copy.wait()
 
 
 def pack_weights_kernel(conv_ref, mask_ref, shard_ref):
@@ -164,32 +172,28 @@
         shard_ref[8 * k : 8 * k + 8] = piece
 
 
-def line_kernel(shard_ref, one_ref, two_ref, three_ref, line_ref):
-    x = lax.axis_index("chan_0")
-    for k, ref in enumerate((shard_ref, one_ref, two_ref, three_ref)):
-        line_ref[(x - k + 4) % 4] = ref[...]
-
-
-def arrange_kernel(line_ref, partner_ref, all_ref):
-    side = lax.axis_index("chan_1")
-    for x in range(4):
-        all_ref[2 * x + side] = line_ref[x]
-        all_ref[2 * x + 1 - side] = partner_ref[x]
-
-
-def lateral_kernel(own_ref, weight_ref, stats_ref, next_ref, prev_ref):
+def arrange_kernel(*refs):
+    chan = lax.axis_index("chan_0") * 2 + lax.axis_index("chan_1")
+    all_ref = refs[-1]
+    for k, ref in enumerate(refs[:-1]):
+        all_ref[chan ^ k] = ref[...]
+
+
+def lateral_kernel(own_ref, weight_ref, stats_ref, one_ref, two_ref):
     for s in range(8):
         for half in range(2):
             weight_ref[32 * s + 16 * half : 32 * s + 16 * half + 16, :] = own_ref[
                 s, 48:64, 256 * half : 256 * half + 256
             ]
-    for ref, at in ((next_ref, 256), (prev_ref, 0)):
+    odd = lax.axis_index("chan_0") % 2
+    for ref, row in ((one_ref, 1 - odd), (two_ref, odd)):
+        at = pl.multiple_of(256 * row, 256)
         for s in range(8):
-            ref[s, 0:48, :] = own_ref[s, 0:48, at : at + 256]
+            ref[s, 0:48, :] = own_ref[s, 0:48, pl.ds(at, 256)]
             ref[s, 48:64, :] = own_ref[s, 64:80, 0:256]
             ref[s, 64:80, :] = own_ref[s, 64:80, 256:512]
-            ref[s, 80:96, :] = own_ref[s, 80:96, 0:256]
-            ref[s, 96:112, :] = own_ref[s, 80:96, 256:512]
+            ref[s, 80:96, 0:128] = own_ref[s, 48:64, 128:256]
+            ref[s, 80:96, 128:256] = own_ref[s, 48:64, 384:512]
     lane = lax.broadcasted_iota(jnp.int32, (GROUPS, 1, 128), 2)
     total = jnp.zeros((1, 128), F32)
     for n in range(2):
@@ -199,8 +203,14 @@
 
 
 def join_kernel(
-    own_ref, above_ref, below_ref, lat_weight_ref, lat_stats_ref, joined_ref, beside_ref
+    own_ref, one_ref, two_ref, lat_weight_ref, lat_stats_ref, joined_ref, beside_ref,
+    above_ref, below_ref,
 ):
+    odd = lax.axis_index("chan_0") % 2 == 1
+    for s in range(8):
+        one, two = one_ref[s], two_ref[s]
+        above_ref[s] = jnp.where(odd, one, two)
+        below_ref[s] = jnp.where(odd, two, one)
     core = lax.axis_index("band_2")
     band = (lax.axis_index("band_0") * 2 + lax.axis_index("band_1")) * 2 + core
     side = lax.axis_index("chan_1")
@@ -238,23 +248,21 @@
                 pieces.append(ref[s, low : low + 16, high + at : high + at + 128])
         return jnp.concatenate(pieces, axis=0)
 
-    def extras(ref, low, at):
-        fine, coarse = [], []
+    def extras(tile, move):
+        fine = jnp.concatenate([tile[32 * s : 32 * s + 24] for s in range(8)], axis=0)
+        fine = pltpu.roll(dot(lat_weight, fine), 128 - FINE_EDGE + move, axis=1)
+        return fine, pltpu.roll(tile.astype(F32), 128 - COARSE_EDGE, axis=1)
+
+    def tile_of(ref):
+        pieces = []
         for s in range(8):
-            fine.append(ref[s, low : low + 16, 0:128])
-            fine.append(ref[s, low : low + 8, 128:256])
-            if at:
-                coarse.append(ref[s, low : low + 16, at : at + 128])
-                coarse.append(ref[s, low : low + 16, at + 128 : at + 256])
-            else:
-                coarse.append(ref[s, low + 16 : low + 32, 0:128])
-                coarse.append(ref[s, low + 16 : low + 32, 128:256])
-        fine = dot(lat_weight, jnp.concatenate(fine, axis=0))
-        return fine, jnp.concatenate(coarse, axis=0).astype(F32)
-
-    fine_above, extra_above = extras(above_ref, 80, 0)
-    fine_own, extra_own = extras(own_ref, 80, 256)
-    fine_below, extra_below = extras(below_ref, 80, 0)
+            pieces.append(ref[s, 80:96, 0:128])
+            pieces.append(ref[s, 80:96, 128:256])
+        return jnp.concatenate(pieces, axis=0)
+
+    fine_above, extra_above = extras(tile_of(above_ref), -2)
+    fine_own, extra_own = extras(lat_weight_ref[:, 128:256], 0)
+    fine_below, extra_below = extras(tile_of(below_ref), 2)
     extra_above = jnp.where(at_top, extra_own, extra_above)
     extra_below = jnp.where(at_bottom, extra_own, extra_below)
     mains = []
@@ -284,9 +292,7 @@
         )
 
     lateral = jnp.where(
-        time == 0,
-        pltpu.roll(fine_above, 126, axis=1),
-        jnp.where(time == 3, pltpu.roll(fine_below, 2, axis=1), fine_own),
+        time == 0, fine_above, jnp.where(time == 3, fine_below, fine_own)
     )
     upsampled = jnp.where(
         time == 0,
@@ -400,14 +406,14 @@
                 out_ref[pl.ds(at, QUERIES, stride=4), :] = result[:, 128 * t : 128 * t + 128]
 
 
-def call(kernel, out_shape, scratch=(), flops=0, space=pltpu.VMEM, limit=40 << 20):
-    vmem = pl.BlockSpec(memory_space=pltpu.VMEM)
+def call(kernel, out_shape, scratch=(), flops=0, space=pltpu.VMEM, out_space=pltpu.VMEM, limit=40 << 20):
+    out = pl.BlockSpec(memory_space=out_space)
     single = not isinstance(out_shape, (tuple, list))
     return lambda *args: pl.pallas_call(
         kernel,
         out_shape=out_shape,
         in_specs=[pl.BlockSpec(memory_space=space)] * len(args),
-        out_specs=vmem if single else [vmem] * len(out_shape),
+        out_specs=out if single else [out] * len(out_shape),
         scratch_shapes=list(scratch),
         cost_estimate=pl.CostEstimate(flops=flops, bytes_accessed=1 << 20, transcendentals=0),
         compiler_params=pltpu.CompilerParams(vmem_limit_bytes=limit),
@@ -444,36 +450,48 @@
             pltpu.VMEM((2, 32, 4, 256), BF16),
             pltpu.VMEM((32, IN_CH), BF16),
             pltpu.VMEM((5, 1, 32), BF16),
+            pltpu.VMEM((8, OWN_ROWS, COLS), BF16),
             pltpu.VMEM((4, 48 * 8, 128), F32),
-            pltpu.VMEM((2, 2, 32, 8, 128), F32),
+            pltpu.VMEM((2, 2, 256, 128), F32),
+            pltpu.SemaphoreType.DMA((8,)),
             pltpu.SemaphoreType.DMA((8,)),
         ),
         space=pltpu.HBM,
+        out_space=pltpu.HBM,
         limit=60 << 20,
     )(fine_features, coarse_level, lat_weight, *vectors)
     own = lax.all_to_all(own_out, CHAN, 0, 0, tiled=True)
     shard = call(pack_weights_kernel, shard_shape)(out_weight, mask_weight)
-    moved = [lax.ppermute(shard, "chan_0", [(i, (i + k) % 4) for i in range(4)]) for k in (1, 2, 3)]
-
-    full_lat, stats, to_next, to_prev = call(
+    moved = [lax.ppermute(shard, CHAN, [(i, i ^ k) for i in range(8)]) for k in XORS]
+
+    full_lat, stats, first, second = call(
         lateral_kernel,
         [jax.ShapeDtypeStruct((D, 256), BF16), stats_shape, side_shape, side_shape],
         flops=2 * 2 * 256 * 256 * 512,
     )(own)
-    above = lax.ppermute(to_next, ALL, [(i, (i + 2) % everyone) for i in range(everyone)])
-    below = lax.ppermute(to_prev, ALL, [((i + 2) % everyone, i) for i in range(everyone)])
-    line = call(line_kernel, jax.ShapeDtypeStruct((4, SHARD_ROWS, COLS), BF16))(shard, *moved)
-    partner = lax.ppermute(line, "chan_1", swap)
+    pairs = everyone // 2
+    swap_at = lambda shift: [
+        (2 * p + yl, 2 * ((((p + shift) % pairs ^ 1) - shift) % pairs) + yl)
+        for p in range(pairs)
+        for yl in range(2)
+    ]
+    first = lax.ppermute(first, ALL, swap_at(0))
+    second = lax.ppermute(second, ALL, swap_at(1))
     stats = lax.all_to_all(stats, ALL, 0, 0, tiled=True)
     stats = call(combine_kernel, jax.ShapeDtypeStruct((8, 128), F32), flops=1 << 20)(stats)
 
-    mine = call(arrange_kernel, all_shape)(line, partner)
+    by_xor = dict(zip(XORS, moved))
+    mine = call(arrange_kernel, all_shape)(shard, *[by_xor[k] for k in range(1, 8)])
     other = lax.ppermute(mine, "band_2", swap)
     joined, beside = call(
         join_kernel,
         [jax.ShapeDtypeStruct((2, 3 * D, COLS), BF16), jax.ShapeDtypeStruct((3 * D, 128), BF16)],
+        (
+            pltpu.VMEM((8, SIDE_ROWS, HALF), BF16),
+            pltpu.VMEM((8, SIDE_ROWS, HALF), BF16),
+        ),
         flops=2 * 2 * 256 * 256 * 512 * 7,
-    )(own, above, below, full_lat, stats)
+    )(own, first, second, full_lat, stats)
     keep, send, stats = call(
         conv_kernel,
         [half_shape, half_shape, stats_shape],

time: 91.1 us -> 85.5 us (0.939)
  waiting for transfers between devices: 15.9 us -> 8.27 us
  starting transfers between devices: 18.8 us -> 22.5 us
  blocking collectives: 46.3 us -> 45.1 us
    ppermute x6 -> x9, waiting for transfers between devices: 15.9 us -> 8.26 us  [the longest x7 8.25 us: per_device(): lax.ppermute(shard, CHAN, [(i, i ^ k) for i in range(8)])]
    ppermute x6 -> x9, starting transfers between devices: 9.32 us -> 15 us  [the longest x7 13.2 us: per_device(): lax.ppermute(shard, CHAN, [(i, i ^ k) for i in range(8)])]
    ppermute x1, starting transfers between devices: 2.96 us -> 1.08 us  [per_device(): other = lax.ppermute(mine, 'band_2', swap)]
    all_to_all x2, blocking collectives: 46.3 us -> 45.1 us  [per_device(): stats = lax.all_to_all(stats, ALL, 0, 0, tiled=True)]
    pallas_call x9 -> x8, Pallas kernels: 9.87 us -> 9.26 us  [call(): pl.pallas_call(kernel, out_shape=out_shape, in_specs=[pl.BlockSpec(memory...]
  transfers between devices with their start and end apart: 9 -> 12, of which waited for: 3 -> 4; matrix products, arithmetic and copies ran while one was open for 0% -> 0% of each run, Pallas kernels for 3% -> 3%
where the time goes in v2:
time: 85.5 us; the launch traced here: 85.3 us
  blocking collectives  45.1 us (53%)
  starting transfers between devices  22.5 us (26%)
  Pallas kernels  9.26 us (11%)
  waiting for transfers between devices  8.27 us (10%)
    all_to_all x2, blocking collectives, per_device(): stats = lax.all_to_all(stats, ALL, 0, 0, tiled=True)  45.1 us
    ppermute x7, starting transfers between devices, per_device(): lax.ppermute(shard, CHAN, [(i, i ^ k) for i in range(8)])  13.2 us
    pallas_call x8, Pallas kernels, call(): pl.pallas_call(kernel, out_shape=out_shape, in_specs=[pl.BlockSpec(memory...  9.26 us
    ppermute x7, waiting for transfers between devices, per_device(): lax.ppermute(shard, CHAN, [(i, i ^ k) for i in range(8)])  8.25 us
    all_to_all x1, starting transfers between devices, per_device(): own = lax.all_to_all(own_out, CHAN, 0, 0, tiled=True)  5.86 us
  transfers between devices with their start and end apart: 12, of which 4 were waited for; matrix products, arithmetic and copies ran while one was open for 0% of the time, Pallas kernels for 3%

profile of v2, /device:TPU:1, one launch (start us, length us, event | category | flops | bytes accessed | tf_op | source)
XLA Modules:
  0.0 85.3 jit_solution(11935215615234415641)
XLA Ops:
  0.0 0.0 copy-start
  0.0 0.0 copy-start.2
  0.0 2.3 %shard_map.109 = bf16[8,80,512]{2,1,0:T(8,128)(2,1)} custom-call(bf16[2,24,8,512]{3,2,1,0:T(8,128)(2,1)} %fine_hbm.1, bf16[2,32,4,256]{3,2,1,0:T(4,128)(2,1)} %coarse_hbm.1, bf16[32,192]{1,0:T(8,128)(2,1)} %weight_hbm.1, bf16[1,32]{1,0:T(2,128)(2,1)} %bitcast.18, bf16[1,32]{1,0:T(2,128)(2,1)} %bitcast.19, bf16[1,32]{1,0:T(2,128)(2,1)} %bitcast.20, ...), custom_call_target="tpu_custom_call" | custom-call | bytes 1048576 | tf_op jit(solution)/shard_map/pallas_call | solution.py:412
  2.3 5.9 %all-to-all-start = ((bf16[8,80,512]{2,1,0:T(8,128)(2,1)}), bf16[8,80,512]{2,1,0:T(8,128)(2,1)S(1)}, u32[]{:S(2)}, u32[]{:S(2)}) async-start(bf16[8,80,512]{2,1,0:T(8,128)(2,1)} %shard_map.109), calls=%async_computation | async-start | bytes 1310720 | tf_op jit(solution)/shard_map/all_to_all | solution.py:463
  8.2 0.0 copy-done
  8.2 0.0 copy-done.2
  8.2 1.5 %collective-permute-start.2 = (bf16[80,512]{1,0:T(8,128)(2,1)S(1)}, bf16[80,512]{1,0:T(8,128)(2,1)S(1)}, u32[]{:S(2)}, u32[]{:S(2)}) collective-permute-start(bf16[80,512]{1,0:T(8,128)(2,1)S(1)} %shard_map.113.refs_0_), channel_id=1, source_target_pairs={{0,1},{1,0},{2,3},{3,2},{4,5},{5,4},{6,7},{7,6},{8,9},{9,8},{10,11... | collective-permute-start | bytes 245768 | tf_op jit(solution)/shard_map/ppermute | solution.py:465
  9.7 1.2 %collective-permute-start.3 = (bf16[80,512]{1,0:T(8,128)(2,1)S(1)}, bf16[80,512]{1,0:T(8,128)(2,1)S(1)}, u32[]{:S(2)}, u32[]{:S(2)}) collective-permute-start(bf16[80,512]{1,0:T(8,128)(2,1)S(1)} %shard_map.113.refs_0_), channel_id=1, source_target_pairs={{0,2},{1,3},{2,0},{3,1},{4,6},{5,7},{6,4},{7,5},{8,10},{9,11},{10,... | collective-permute-start | bytes 245768 | tf_op jit(solution)/shard_map/ppermute | solution.py:465
  10.9 0.1 collective-permute-start.4
  11.0 2.9 %collective-permute-start.5 = (bf16[80,512]{1,0:T(8,128)(2,1)S(1)}, bf16[80,512]{1,0:T(8,128)(2,1)S(1)}, u32[]{:S(2)}, u32[]{:S(2)}) collective-permute-start(bf16[80,512]{1,0:T(8,128)(2,1)S(1)} %shard_map.113.refs_0_), channel_id=1, source_target_pairs={{0,4},{1,5},{2,6},{3,7},{4,0},{5,1},{6,2},{7,3},{8,12},{9,13},{10,... | collective-permute-start | bytes 245768 | tf_op jit(solution)/shard_map/ppermute | solution.py:465
  13.9 1.2 %collective-permute-start.6 = (bf16[80,512]{1,0:T(8,128)(2,1)S(1)}, bf16[80,512]{1,0:T(8,128)(2,1)S(1)}, u32[]{:S(2)}, u32[]{:S(2)}) collective-permute-start(bf16[80,512]{1,0:T(8,128)(2,1)S(1)} %shard_map.113.refs_0_), channel_id=1, source_target_pairs={{0,5},{1,4},{2,7},{3,6},{4,1},{5,0},{6,3},{7,2},{8,13},{9,12},{10,... | collective-permute-start | bytes 245768 | tf_op jit(solution)/shard_map/ppermute | solution.py:465
  15.1 1.2 %collective-permute-done.2.refs_1_ = bf16[80,512]{1,0:T(8,128)(2,1)S(1)} collective-permute-done((bf16[80,512]{1,0:T(8,128)(2,1)S(1)}, bf16[80,512]{1,0:T(8,128)(2,1)S(1)}, u32[]{:S(2)}, u32[]{:S(2)}) %collective-permute-start.2) | collective-permute-done | bytes 81952 | tf_op jit(solution)/shard_map/ppermute | solution.py:465
  16.3 5.1 %collective-permute-start.7 = (bf16[80,512]{1,0:T(8,128)(2,1)S(1)}, bf16[80,512]{1,0:T(8,128)(2,1)S(1)}, u32[]{:S(2)}, u32[]{:S(2)}) collective-permute-start(bf16[80,512]{1,0:T(8,128)(2,1)S(1)} %shard_map.113.refs_0_), channel_id=1, source_target_pairs={{0,6},{1,7},{2,4},{3,5},{4,2},{5,3},{6,0},{7,1},{8,14},{9,15},{10,... | collective-permute-start | bytes 245768 | tf_op jit(solution)/shard_map/ppermute | solution.py:465
  21.4 0.0 collective-permute-done.3.refs_2_
  21.4 1.2 %collective-permute-start.8 = (bf16[80,512]{1,0:T(8,128)(2,1)S(1)}, bf16[80,512]{1,0:T(8,128)(2,1)S(1)}, u32[]{:S(2)}, u32[]{:S(2)}) collective-permute-start(bf16[80,512]{1,0:T(8,128)(2,1)S(1)} %shard_map.113.refs_0_), channel_id=1, source_target_pairs={{0,7},{1,6},{2,5},{3,4},{4,3},{5,2},{6,1},{7,0},{8,15},{9,14},{10,... | collective-permute-start | bytes 245768 | tf_op jit(solution)/shard_map/ppermute | solution.py:465
  22.6 0.0 collective-permute-done.4.refs_3_
  22.6 0.5 collective-permute-done.5.refs_4_
  23.2 2.8 %collective-permute-done.6.refs_5_ = bf16[80,512]{1,0:T(8,128)(2,1)S(1)} collective-permute-done((bf16[80,512]{1,0:T(8,128)(2,1)S(1)}, bf16[80,512]{1,0:T(8,128)(2,1)S(1)}, u32[]{:S(2)}, u32[]{:S(2)}) %collective-permute-start.6) | collective-permute-done | bytes 81952 | tf_op jit(solution)/shard_map/ppermute | solution.py:465
  25.9 0.0 collective-permute-done.7.refs_6_
  25.9 3.7 %collective-permute-done.8.refs_7_ = bf16[80,512]{1,0:T(8,128)(2,1)S(1)} collective-permute-done((bf16[80,512]{1,0:T(8,128)(2,1)S(1)}, bf16[80,512]{1,0:T(8,128)(2,1)S(1)}, u32[]{:S(2)}, u32[]{:S(2)}) %collective-permute-start.8) | collective-permute-done | bytes 81952 | tf_op jit(solution)/shard_map/ppermute | solution.py:465
  29.6 0.1 shard_map.114.mine_ref
  29.7 1.1 %collective-permute-start.9 = (bf16[8,80,512]{2,1,0:T(8,128)(2,1)S(1)}, bf16[8,80,512]{2,1,0:T(8,128)(2,1)S(1)}, u32[]{:S(2)}, u32[]{:S(2)}) collective-permute-start(bf16[8,80,512]{2,1,0:T(8,128)(2,1)S(1)} %shard_map.114.mine_ref), channel_id=1, source_target_pairs={{0,8},{8,0},{1,9},{9,1},{2,10},{10,2},{3,11},{11,3},{4,12},{12,4},... | collective-permute-start | bytes 1966088 | tf_op jit(solution)/shard_map/ppermute | solution.py:485
  30.8 0.0 all-to-all-done.own_ref
  30.8 0.6 shard_map.110
  31.4 0.3 collective-permute-start
  31.7 1.4 %collective-permute-start.1 = (bf16[8,96,256]{2,1,0:T(8,128)(2,1)S(1)}, bf16[8,96,256]{2,1,0:T(8,128)(2,1)S(1)}, u32[]{:S(2)}, u32[]{:S(2)}) collective-permute-start(bf16[8,96,256]{2,1,0:T(8,128)(2,1)S(1)} %get-tuple-element.15), channel_id=1, source_target_pairs={{0,254},{1,255},{2,4},{3,5},{4,2},{5,3},{6,8},{7,9},{8,6},{9,7},{1... | collective-permute-start | bytes 1179656 | tf_op jit(solution)/shard_map/ppermute | solution.py:479
  33.2 26.3 %all_to_all.27 = f32[256,1,128]{2,1,0:T(1,128)S(1)} all-to-all(f32[256,1,128]{2,1,0:T(1,128)S(1)} %bitcast.16), channel_id=1, replica_groups=mesh['band_0'=8,'band_1'=2,'band_2'=2,'chan_0'=4,'chan_1'=2] {'band_0','..., dimensions={0} | all-to-all | bytes 262144 | tf_op jit(solution)/shard_map/all_to_all | solution.py:480
  59.4 0.1 shard_map.111.lat_stats_ref
  59.5 0.0 collective-permute-done.one_ref
  59.5 0.0 collective-permute-done.1.two_ref
  59.5 1.8 %shard_map.112 = (bf16[2,768,512]{2,1,0:T(8,128)(2,1)S(1)}, bf16[768,128]{1,0:T(8,128)(2,1)S(1)}) custom-call(bf16[8,80,512]{2,1,0:T(8,128)(2,1)S(1)} %all-to-all-done.own_ref, bf16[8,96,256]{2,1,0:T(8,128)(2,1)S(1)} %collective-permute-done.one_ref, bf16[8,96,256]{2,1,0:T(8,128)(2,1)S(1)} %collective-permute-done.1.two_ref, ...), custom_call_target="tpu_custom_call" | custom-call | flops 939524096 | bytes 1048576 | tf_op jit(solution)/shard_map/pallas_call | solution.py:412
  61.3 0.0 collective-permute-done.9.other_ref
  61.3 0.0 copy-start.1
  61.3 2.0 %shard_map.115 = (f32[2,256,256]{2,1,0:T(8,128)S(1)}, f32[2,256,256]{2,1,0:T(8,128)S(1)}, f32[256,128]{1,0:T(8,128)S(1)}) custom-call(bf16[2,768,512]{2,1,0:T(8,128)(2,1)S(1)} %get-tuple-element.18.joined_ref, bf16[768,128]{1,0:T(8,128)(2,1)S(1)} %get-tuple-element.19.beside_ref, bf16[8,80,512]{2,1,0:T(8,128)(2,1)S(1)} %shard_map.114.mine_ref, ...), custom_call_target="tpu_custom_call" | custom-call | flops 1207959552 | bytes 1048576 | tf_op jit(solution)/shard_map/pallas_call | solution.py:412
  63.3 0.6 collective-permute-start.10
  63.9 18.9 %all_to_all.28 = f32[256,1,128]{2,1,0:T(1,128)S(1)} all-to-all(f32[256,1,128]{2,1,0:T(1,128)S(1)} %bitcast.17), channel_id=1, replica_groups=mesh['band_0'=8,'band_1'=2,'band_2'=2,'chan_0'=4,'chan_1'=2] {'band_0','..., dimensions={0} | all-to-all | bytes 262144 | tf_op jit(solution)/shard_map/all_to_all | solution.py:502
  82.8 0.0 collective-permute-done.10.taken_ref
  82.8 0.0 copy-done.1
  82.8 2.4 %shard_map.116 = f32[1600,128]{1,0:T(8,128)} custom-call(f32[2,256,256]{2,1,0:T(8,128)S(1)} %get-tuple-element.20.keep_ref, f32[2,256,256]{2,1,0:T(8,128)S(1)} %collective-permute-done.10.taken_ref, f32[256,128]{1,0:T(8,128)S(1)} %bitcast.14, bf16[256,256]{1,0:T(8,128)(2,1)S(1)} %get-tuple-element.16.lat_weight_ref, ...), custom_call_target="tpu_custom_call" | custom-call | flops 268435456 | bytes 1048576 | tf_op jit(solution)/shard_map/pallas_call | solution.py:412
  (1 shorter events, 0.0 us)
Async XLA Ops:
  0.0 8.2 %copy-start = (bf16[3,3,32,256]{3,2,1,0:T(8,128)(2,1)S(1)}, bf16[3,3,32,256]{3,2,1,0:T(8,128)(2,1)}, u32[]{:S(2)}) copy-start(bf16[3,3,32,256]{3,2,1,0:T(8,128)(2,1)} %conv_ref.1) | copy-start | bytes 442372
  0.0 8.2 %copy-start.2 = (bf16[32,256]{1,0:T(8,128)(2,1)S(1)}, bf16[32,256]{1,0:T(8,128)(2,1)}, u32[]{:S(2)}) copy-start(bf16[32,256]{1,0:T(8,128)(2,1)} %mask_ref.1) | copy-start | bytes 49156
  2.3 28.5 %all-to-all-start = ((bf16[8,80,512]{2,1,0:T(8,128)(2,1)}), bf16[8,80,512]{2,1,0:T(8,128)(2,1)S(1)}, u32[]{:S(2)}, u32[]{:S(2)}) async-start(bf16[8,80,512]{2,1,0:T(8,128)(2,1)} %shard_map.109), calls=%async_computation | async-start | bytes 1310720 | tf_op jit(solution)/shard_map/all_to_all | solution.py:463
  8.2 8.1 %collective-permute-start.2 = (bf16[80,512]{1,0:T(8,128)(2,1)S(1)}, bf16[80,512]{1,0:T(8,128)(2,1)S(1)}, u32[]{:S(2)}, u32[]{:S(2)}) collective-permute-start(bf16[80,512]{1,0:T(8,128)(2,1)S(1)} %shard_map.113.refs_0_), channel_id=1, source_target_pairs={{0,1},{1,0},{2,3},{3,2},{4,5},{5,4},{6,7},{7,6},{8,9},{9,8},{10,11... | collective-permute-start | bytes 245768 | tf_op jit(solution)/shard_map/ppermute | solution.py:465
  9.7 11.7 %collective-permute-start.3 = (bf16[80,512]{1,0:T(8,128)(2,1)S(1)}, bf16[80,512]{1,0:T(8,128)(2,1)S(1)}, u32[]{:S(2)}, u32[]{:S(2)}) collective-permute-start(bf16[80,512]{1,0:T(8,128)(2,1)S(1)} %shard_map.113.refs_0_), channel_id=1, source_target_pairs={{0,2},{1,3},{2,0},{3,1},{4,6},{5,7},{6,4},{7,5},{8,10},{9,11},{10,... | collective-permute-start | bytes 245768 | tf_op jit(solution)/shard_map/ppermute | solution.py:465
  10.9 11.7 %collective-permute-start.4 = (bf16[80,512]{1,0:T(8,128)(2,1)S(1)}, bf16[80,512]{1,0:T(8,128)(2,1)S(1)}, u32[]{:S(2)}, u32[]{:S(2)}) collective-permute-start(bf16[80,512]{1,0:T(8,128)(2,1)S(1)} %shard_map.113.refs_0_), channel_id=1, source_target_pairs={{0,3},{1,2},{2,1},{3,0},{4,7},{5,6},{6,5},{7,4},{8,11},{9,10},{10,... | collective-permute-start | bytes 245768 | tf_op jit(solution)/shard_map/ppermute | solution.py:465
  11.0 12.1 %collective-permute-start.5 = (bf16[80,512]{1,0:T(8,128)(2,1)S(1)}, bf16[80,512]{1,0:T(8,128)(2,1)S(1)}, u32[]{:S(2)}, u32[]{:S(2)}) collective-permute-start(bf16[80,512]{1,0:T(8,128)(2,1)S(1)} %shard_map.113.refs_0_), channel_id=1, source_target_pairs={{0,4},{1,5},{2,6},{3,7},{4,0},{5,1},{6,2},{7,3},{8,12},{9,13},{10,... | collective-permute-start | bytes 245768 | tf_op jit(solution)/shard_map/ppermute | solution.py:465
  13.9 12.0 %collective-permute-start.6 = (bf16[80,512]{1,0:T(8,128)(2,1)S(1)}, bf16[80,512]{1,0:T(8,128)(2,1)S(1)}, u32[]{:S(2)}, u32[]{:S(2)}) collective-permute-start(bf16[80,512]{1,0:T(8,128)(2,1)S(1)} %shard_map.113.refs_0_), channel_id=1, source_target_pairs={{0,5},{1,4},{2,7},{3,6},{4,1},{5,0},{6,3},{7,2},{8,13},{9,12},{10,... | collective-permute-start | bytes 245768 | tf_op jit(solution)/shard_map/ppermute | solution.py:465
  16.3 9.6 %collective-permute-start.7 = (bf16[80,512]{1,0:T(8,128)(2,1)S(1)}, bf16[80,512]{1,0:T(8,128)(2,1)S(1)}, u32[]{:S(2)}, u32[]{:S(2)}) collective-permute-start(bf16[80,512]{1,0:T(8,128)(2,1)S(1)} %shard_map.113.refs_0_), channel_id=1, source_target_pairs={{0,6},{1,7},{2,4},{3,5},{4,2},{5,3},{6,0},{7,1},{8,14},{9,15},{10,... | collective-permute-start | bytes 245768 | tf_op jit(solution)/shard_map/ppermute | solution.py:465
  21.4 8.2 %collective-permute-start.8 = (bf16[80,512]{1,0:T(8,128)(2,1)S(1)}, bf16[80,512]{1,0:T(8,128)(2,1)S(1)}, u32[]{:S(2)}, u32[]{:S(2)}) collective-permute-start(bf16[80,512]{1,0:T(8,128)(2,1)S(1)} %shard_map.113.refs_0_), channel_id=1, source_target_pairs={{0,7},{1,6},{2,5},{3,4},{4,3},{5,2},{6,1},{7,0},{8,15},{9,14},{10,... | collective-permute-start | bytes 245768 | tf_op jit(solution)/shard_map/ppermute | solution.py:465
  29.7 31.6 %collective-permute-start.9 = (bf16[8,80,512]{2,1,0:T(8,128)(2,1)S(1)}, bf16[8,80,512]{2,1,0:T(8,128)(2,1)S(1)}, u32[]{:S(2)}, u32[]{:S(2)}) collective-permute-start(bf16[8,80,512]{2,1,0:T(8,128)(2,1)S(1)} %shard_map.114.mine_ref), channel_id=1, source_target_pairs={{0,8},{8,0},{1,9},{9,1},{2,10},{10,2},{3,11},{11,3},{4,12},{12,4},... | collective-permute-start | bytes 1966088 | tf_op jit(solution)/shard_map/ppermute | solution.py:485
  31.4 28.1 %collective-permute-start = (bf16[8,96,256]{2,1,0:T(8,128)(2,1)S(1)}, bf16[8,96,256]{2,1,0:T(8,128)(2,1)S(1)}, u32[]{:S(2)}, u32[]{:S(2)}) collective-permute-start(bf16[8,96,256]{2,1,0:T(8,128)(2,1)S(1)} %get-tuple-element.14), channel_id=1, source_target_pairs={{0,2},{1,3},{2,0},{3,1},{4,6},{5,7},{6,4},{7,5},{8,10},{9,11},{10,... | collective-permute-start | bytes 1179656 | tf_op jit(solution)/shard_map/ppermute | solution.py:478
  31.7 27.8 %collective-permute-start.1 = (bf16[8,96,256]{2,1,0:T(8,128)(2,1)S(1)}, bf16[8,96,256]{2,1,0:T(8,128)(2,1)S(1)}, u32[]{:S(2)}, u32[]{:S(2)}) collective-permute-start(bf16[8,96,256]{2,1,0:T(8,128)(2,1)S(1)} %get-tuple-element.15), channel_id=1, source_target_pairs={{0,254},{1,255},{2,4},{3,5},{4,2},{5,3},{6,8},{7,9},{8,6},{9,7},{1... | collective-permute-start | bytes 1179656 | tf_op jit(solution)/shard_map/ppermute | solution.py:479
  61.3 21.5 %copy-start.1 = (bf16[200,256]{1,0:T(8,128)(2,1)S(1)}, bf16[200,256]{1,0:T(8,128)(2,1)}, u32[]{:S(2)}) copy-start(bf16[200,256]{1,0:T(8,128)(2,1)} %query_ref.1) | copy-start | bytes 307204
  63.3 19.5 %collective-permute-start.10 = (f32[2,256,256]{2,1,0:T(8,128)S(1)}, f32[2,256,256]{2,1,0:T(8,128)S(1)}, u32[]{:S(2)}, u32[]{:S(2)}) collective-permute-start(f32[2,256,256]{2,1,0:T(8,128)S(1)} %get-tuple-element.21), channel_id=1, source_target_pairs={{0,1},{1,0},{2,3},{3,2},{4,5},{5,4},{6,7},{7,6},{8,9},{9,8},{10,11... | collective-permute-start | bytes 1572872 | tf_op jit(solution)/shard_map/ppermute | solution.py:501

commit v3 on v2

--- a/solution.py
+++ b/solution.py
@@ -24,9 +24,9 @@
 FINE_EDGE = 72
 COARSE_EDGE = 80
 SIDE_ROWS = 96
-MASK_AT = 72
+MASK_AT = 144
+SHARD_ROWS = 176
 XORS = (4, 1, 2, 5, 6, 3, 7)
-SHARD_ROWS = 80
 
 
 def dot(a, b):
@@ -92,21 +92,25 @@
 def pack_own_kernel(fine_hbm, coarse_hbm, weight_hbm, *refs):
     vec_hbm, own_hbm = refs[:5], refs[5]
     fine_ref, coarse_ref, weight_ref, vec_ref, own_ref, rows, coarse, sems, out_sems = refs[6:]
-    pairs = [(coarse_hbm, coarse_ref), (weight_hbm, weight_ref)]
-    pairs += [(vec, vec_ref.at[i]) for i, vec in enumerate(vec_hbm)] + [(fine_hbm, fine_ref)]
+    pairs = [(coarse_hbm.at[n], coarse_ref.at[n]) for n in range(2)] + [(weight_hbm, weight_ref)]
+    pairs += [(vec, vec_ref.at[i]) for i, vec in enumerate(vec_hbm)]
+    for n in range(2):
+        for j in range(3):
+            at = (n, pl.ds(8 * j, 8))
+            pairs.append((fine_hbm.at[at], fine_ref.at[at]))
     copies = [
         pltpu.make_async_copy(source, target, sems.at[i])
         for i, (source, target) in enumerate(pairs)
     ]
     for copy in copies:
         copy.start()
-    for copy in copies[:-1]:
+    for copy in copies[:-6]:
         copy.wait()
     for n in range(2):
         for t in range(2):
             piece = coarse_ref[n, :, :, 128 * t : 128 * t + 128].astype(F32)
             piece = jnp.concatenate([piece, jnp.zeros_like(piece)], axis=1)
-            coarse[n, t] = piece.reshape(256, 128)
+            coarse[n, t, 0:256] = piece.reshape(256, 128)
     lane = lanes_of((32, 128))
     vec_lane = lanes_of((32, 32))
     vec_row = lax.broadcasted_iota(jnp.int32, (32, 32), 0)
@@ -131,10 +135,11 @@
                 edge = row[:, 0:1] if h == 0 else row[:, 127:128]
                 tail = jnp.where(lane // 4 == COARSE_EDGE // 4 + n, edge, tail)
             tails.append(tail)
-    copies[-1].wait()
+    for copy in copies[-6:]:
+        copy.wait()
     for t in range(4):
         piece = fine_ref[:, :, :, 128 * t : 128 * t + 128].astype(F32)
-        rows[t] = piece.reshape(48 * 8, 128)
+        rows[t, 0:384] = piece.reshape(48 * 8, 128)
     out = []
     for h in range(2):
         for q in range(4):
@@ -163,20 +168,22 @@
 
 def pack_weights_kernel(conv_ref, mask_ref, shard_ref):
     half = pl.multiple_of(16 * lax.axis_index("band_2"), 16)
-    for k in range(10):
-        if k < 9:
-            piece = conv_ref[k // 3, k % 3, pl.ds(half, 16), :].astype(F32)
-        else:
-            piece = mask_ref[pl.ds(half, 16), :].astype(F32)
-        piece = jnp.concatenate([piece[0:8], piece[8:16]], axis=1).astype(BF16)
-        shard_ref[8 * k : 8 * k + 8] = piece
+    for k in range(9):
+        shard_ref[16 * k : 16 * k + 16] = conv_ref[k // 3, k % 3, pl.ds(half, 16), :]
+    shard_ref[MASK_AT : MASK_AT + 32] = mask_ref[...]
 
 
 def arrange_kernel(*refs):
     chan = lax.axis_index("chan_0") * 2 + lax.axis_index("chan_1")
-    all_ref = refs[-1]
-    for k, ref in enumerate(refs[:-1]):
-        all_ref[chan ^ k] = ref[...]
+    half_ref, mask_ref = refs[-2:]
+    for k, ref in enumerate(refs[:-2]):
+        s = chan ^ k
+        for a in range(3):
+            for b in range(3):
+                at = pl.multiple_of(128 * b + 16 * s, 16)
+                piece = ref[16 * (3 * a + b) : 16 * (3 * a + b) + 16]
+                half_ref[pl.ds(at, 16), 256 * a : 256 * a + 256] = piece
+        mask_ref[pl.ds(pl.multiple_of(32 * s, 32), 32)] = ref[MASK_AT : MASK_AT + 32]
 
 
 def lateral_kernel(own_ref, weight_ref, stats_ref, one_ref, two_ref):
@@ -341,26 +348,29 @@
 
 
 def conv_kernel(
-    joined_ref, beside_ref, mine_ref, other_ref, keep_ref, send_ref, stats_ref, weight, taps
+    joined_ref, beside_ref, mine_ref, other_ref, keep_ref, send_ref, stats_ref, taps, beside
 ):
     core = lax.axis_index("band_2")
     side = lax.axis_index("chan_1")
-    for part, ref in ((core, mine_ref), (1 - core, other_ref)):
+    halves = ((core, mine_ref), (1 - core, other_ref))
+    edge_tap = pl.multiple_of(jnp.where(side == 0, 256, 0), 128)
+    for part, ref in halves:
+        value = dot(ref[pl.ds(edge_tap, 128)], beside_ref[...])
         for s in range(8):
             at = pl.multiple_of(32 * s + 16 * part, 16)
-            for a in range(3):
-                for b in range(3):
-                    piece = ref[s, (a * 3 + b) * 8 : (a * 3 + b) * 8 + 8, :]
-                    both = jnp.concatenate([piece[:, 0:256], piece[:, 256:512]], axis=0)
-                    weight[b, pl.ds(at, 16), 256 * a : 256 * a + 256] = both
+            beside[pl.ds(at, 16)] = value[16 * s : 16 * s + 16]
     inner_edge = jnp.where(side == 0, HALF - 1, 0)
     lane = lax.broadcasted_iota(jnp.int32, (GROUPS, 1, 128), 2)
     lane_at = lanes_of((D, HALF))
-    beside = dot(weight[jnp.where(side == 0, 2, 0)], beside_ref[...])
     total = jnp.zeros((1, 128), F32)
     for n in range(2):
-        for b in range(3):
-            taps[b] = dot(weight[b], joined_ref[n])
+        for part, ref in halves:
+            value = dot(ref[...], joined_ref[n])
+            for b in range(3):
+                for s in range(8):
+                    at = pl.multiple_of(32 * s + 16 * part, 16)
+                    row = 128 * b + 16 * s
+                    taps[b, pl.ds(at, 16), :] = value[row : row + 16]
         out = []
         for r in range(2):
             at = HALF * r
@@ -377,33 +387,34 @@
 
 
 def query_kernel(
-    keep_ref, taken_ref, out_stats_ref, lat_weight_ref, mine_ref, other_ref,
-    query_ref, out_ref, weight,
+    keep_ref, taken_ref, out_stats_ref, lat_weight_ref, mask_ref, query_ref, out_hbm, out_ref, sems
 ):
-    core = lax.axis_index("band_2")
     side = lax.axis_index("chan_1")
-    for part, ref in ((core, mine_ref), (1 - core, other_ref)):
-        for s in range(8):
-            at = pl.multiple_of(32 * s + 16 * part, 16)
-            piece = ref[s, MASK_AT : MASK_AT + 8, :]
-            both = jnp.concatenate([piece[:, 0:256], piece[:, 256:512]], axis=0)
-            weight[pl.ds(at, 16), :] = both
     gain = vector_col(lat_weight_ref, 2)
     shift = vector_col(lat_weight_ref, 3)
     bias = vector_col(lat_weight_ref, 4)
     rows = combine(out_stats_ref[...])
+    copies = []
     for n in range(2):
         mean, var = stat_cols(rows, n)
         scale = lax.rsqrt(var + EPS) * gain
         for ref, half in ((keep_ref, side), (taken_ref, 1 - side)):
             activated = jnp.maximum((ref[n] - mean) * scale + shift, 0.0).astype(BF16)
-            features = (dot(weight[...], activated) + bias).astype(BF16)
+            features = (dot(mask_ref[...], activated) + bias).astype(BF16)
             logits = dot(query_ref[...], features)
             shifted = logits - jnp.max(logits, axis=0, keepdims=True)
             result = shifted - jnp.log(jnp.sum(jnp.exp(shifted), axis=0, keepdims=True))
             for t in range(2):
                 at = 4 * QUERIES * n + 2 * half + t
                 out_ref[pl.ds(at, QUERIES, stride=4), :] = result[:, 128 * t : 128 * t + 128]
+        for i in range(4):
+            piece = pl.ds(QUERIES * (4 * n + i), QUERIES)
+            copies.append(
+                pltpu.make_async_copy(out_ref.at[piece], out_hbm.at[piece], sems.at[4 * n + i])
+            )
+            copies[-1].start()
+    for copy in copies:
+        copy.wait()
 
 
 def call(kernel, out_shape, scratch=(), flops=0, space=pltpu.VMEM, out_space=pltpu.VMEM, limit=40 << 20):
@@ -435,8 +446,11 @@
 ):
     everyone = lax.axis_size(ALL)
     stats_shape = jax.ShapeDtypeStruct((everyone, 128), F32)
-    shard_shape = jax.ShapeDtypeStruct((SHARD_ROWS, COLS), BF16)
-    all_shape = jax.ShapeDtypeStruct((8, SHARD_ROWS, COLS), BF16)
+    shard_shape = jax.ShapeDtypeStruct((SHARD_ROWS, D), BF16)
+    weight_shapes = [
+        jax.ShapeDtypeStruct((3 * D // 2, 3 * D), BF16),
+        jax.ShapeDtypeStruct((D, D), BF16),
+    ]
     side_shape = jax.ShapeDtypeStruct((8, SIDE_ROWS, HALF), BF16)
     half_shape = jax.ShapeDtypeStruct((2, D, HALF), F32)
     swap = [(0, 1), (1, 0)]
@@ -451,9 +465,9 @@
             pltpu.VMEM((32, IN_CH), BF16),
             pltpu.VMEM((5, 1, 32), BF16),
             pltpu.VMEM((8, OWN_ROWS, COLS), BF16),
-            pltpu.VMEM((4, 48 * 8, 128), F32),
-            pltpu.VMEM((2, 2, 256, 128), F32),
-            pltpu.SemaphoreType.DMA((8,)),
+            pltpu.VMEM((4, 48 * 8 + 8, 128), F32),
+            pltpu.VMEM((2, 2, 256 + 8, 128), F32),
+            pltpu.SemaphoreType.DMA((14,)),
             pltpu.SemaphoreType.DMA((8,)),
         ),
         space=pltpu.HBM,
@@ -481,7 +495,9 @@
     stats = call(combine_kernel, jax.ShapeDtypeStruct((8, 128), F32), flops=1 << 20)(stats)
 
     by_xor = dict(zip(XORS, moved))
-    mine = call(arrange_kernel, all_shape)(shard, *[by_xor[k] for k in range(1, 8)])
+    mine, mask = call(arrange_kernel, weight_shapes)(
+        shard, *[by_xor[k] for k in range(1, 8)]
+    )
     other = lax.ppermute(mine, "band_2", swap)
     joined, beside = call(
         join_kernel,
@@ -495,7 +511,7 @@
     keep, send, stats = call(
         conv_kernel,
         [half_shape, half_shape, stats_shape],
-        (pltpu.VMEM((3, D, 3 * D), BF16), pltpu.VMEM((3, D, COLS), F32)),
+        (pltpu.VMEM((3, D, COLS), F32), pltpu.VMEM((D, 128), F32)),
         flops=2 * 2 * 256 * 256 * 512 * 9,
     )(joined, beside, mine, other)
     taken = lax.ppermute(send, "chan_1", swap)
@@ -503,9 +519,13 @@
     log_probs = call(
         query_kernel,
         jax.ShapeDtypeStruct((2 * QUERIES * 4, 128), F32),
-        (pltpu.VMEM((D, D), BF16),),
+        (
+            pltpu.VMEM((2 * QUERIES * 4 + 8, 128), F32),
+            pltpu.SemaphoreType.DMA((8,)),
+        ),
         flops=2 * 2 * 256 * 256 * 512 * 2,
-    )(keep, taken, stats, full_lat, mine, other, queries)
+        out_space=pltpu.HBM,
+    )(keep, taken, stats, full_lat, mask, queries)
     return log_probs.reshape(2, QUERIES, 1, COLS)
 
 

time: 85.5 us -> 86.8 us (1.015)
  waiting for transfers between devices: 8.27 us -> 9.21 us
    ppermute x7, waiting for transfers between devices: 8.25 us -> 9.19 us  [per_device(): lax.ppermute(shard, CHAN, [(i, i ^ k) for i in range(8)])]
where the time goes in v3:
time: 86.8 us; the launch traced here: 86.5 us
  blocking collectives  45.1 us (52%)
  starting transfers between devices  22.6 us (26%)
  Pallas kernels  9.39 us (11%)
  waiting for transfers between devices  9.21 us (11%)
    all_to_all x2, blocking collectives, per_device(): stats = lax.all_to_all(stats, ALL, 0, 0, tiled=True)  45.1 us
    ppermute x7, starting transfers between devices, per_device(): lax.ppermute(shard, CHAN, [(i, i ^ k) for i in range(8)])  13.2 us
    pallas_call x8, Pallas kernels, call(): pl.pallas_call(kernel, out_shape=out_shape, in_specs=[pl.BlockSpec(memory...  9.39 us
    ppermute x7, waiting for transfers between devices, per_device(): lax.ppermute(shard, CHAN, [(i, i ^ k) for i in range(8)])  9.19 us
    all_to_all x1, starting transfers between devices, per_device(): own = lax.all_to_all(own_out, CHAN, 0, 0, tiled=True)  5.86 us
  transfers between devices with their start and end apart: 12, of which 4 were waited for; matrix products, arithmetic and copies ran while one was open for 0% of the time, Pallas kernels for 3%

profile of v3, /device:TPU:1, one launch (start us, length us, event | category | flops | bytes accessed | tf_op | source)
XLA Modules:
  0.0 86.5 jit_solution(927743364874433278)
XLA Ops:
  0.0 0.0 copy-start
  0.0 0.0 copy-start.2
  0.0 2.3 %shard_map.109 = bf16[8,80,512]{2,1,0:T(8,128)(2,1)} custom-call(bf16[2,24,8,512]{3,2,1,0:T(8,128)(2,1)} %fine_hbm.1, bf16[2,32,4,256]{3,2,1,0:T(4,128)(2,1)} %coarse_hbm.1, bf16[32,192]{1,0:T(8,128)(2,1)} %weight_hbm.1, bf16[1,32]{1,0:T(2,128)(2,1)} %bitcast.18, bf16[1,32]{1,0:T(2,128)(2,1)} %bitcast.19, bf16[1,32]{1,0:T(2,128)(2,1)} %bitcast.20, ...), custom_call_target="tpu_custom_call" | custom-call | bytes 1048576 | tf_op jit(solution)/shard_map/pallas_call | solution.py:423
  2.3 5.9 %all-to-all-start = ((bf16[8,80,512]{2,1,0:T(8,128)(2,1)}), bf16[8,80,512]{2,1,0:T(8,128)(2,1)S(1)}, u32[]{:S(2)}, u32[]{:S(2)}) async-start(bf16[8,80,512]{2,1,0:T(8,128)(2,1)} %shard_map.109), calls=%async_computation | async-start | bytes 1310720 | tf_op jit(solution)/shard_map/all_to_all | solution.py:477
  8.2 0.0 copy-done
  8.2 0.0 copy-done.2
  8.2 1.5 %collective-permute-start.2 = (bf16[176,256]{1,0:T(8,128)(2,1)S(1)}, bf16[176,256]{1,0:T(8,128)(2,1)S(1)}, u32[]{:S(2)}, u32[]{:S(2)}) collective-permute-start(bf16[176,256]{1,0:T(8,128)(2,1)S(1)} %shard_map.113.refs_0_), channel_id=1, source_target_pairs={{0,1},{1,0},{2,3},{3,2},{4,5},{5,4},{6,7},{7,6},{8,9},{9,8},{10,11... | collective-permute-start | bytes 270344 | tf_op jit(solution)/shard_map/ppermute | solution.py:479
  9.8 1.2 %collective-permute-start.3 = (bf16[176,256]{1,0:T(8,128)(2,1)S(1)}, bf16[176,256]{1,0:T(8,128)(2,1)S(1)}, u32[]{:S(2)}, u32[]{:S(2)}) collective-permute-start(bf16[176,256]{1,0:T(8,128)(2,1)S(1)} %shard_map.113.refs_0_), channel_id=1, source_target_pairs={{0,2},{1,3},{2,0},{3,1},{4,6},{5,7},{6,4},{7,5},{8,10},{9,11},{10,... | collective-permute-start | bytes 270344 | tf_op jit(solution)/shard_map/ppermute | solution.py:479
  11.0 0.1 collective-permute-start.4
  11.1 2.9 %collective-permute-start.5 = (bf16[176,256]{1,0:T(8,128)(2,1)S(1)}, bf16[176,256]{1,0:T(8,128)(2,1)S(1)}, u32[]{:S(2)}, u32[]{:S(2)}) collective-permute-start(bf16[176,256]{1,0:T(8,128)(2,1)S(1)} %shard_map.113.refs_0_), channel_id=1, source_target_pairs={{0,4},{1,5},{2,6},{3,7},{4,0},{5,1},{6,2},{7,3},{8,12},{9,13},{10,... | collective-permute-start | bytes 270344 | tf_op jit(solution)/shard_map/ppermute | solution.py:479
  13.9 1.2 %collective-permute-start.6 = (bf16[176,256]{1,0:T(8,128)(2,1)S(1)}, bf16[176,256]{1,0:T(8,128)(2,1)S(1)}, u32[]{:S(2)}, u32[]{:S(2)}) collective-permute-start(bf16[176,256]{1,0:T(8,128)(2,1)S(1)} %shard_map.113.refs_0_), channel_id=1, source_target_pairs={{0,5},{1,4},{2,7},{3,6},{4,1},{5,0},{6,3},{7,2},{8,13},{9,12},{10,... | collective-permute-start | bytes 270344 | tf_op jit(solution)/shard_map/ppermute | solution.py:479
  15.1 1.4 %collective-permute-done.2.refs_1_ = bf16[176,256]{1,0:T(8,128)(2,1)S(1)} collective-permute-done((bf16[176,256]{1,0:T(8,128)(2,1)S(1)}, bf16[176,256]{1,0:T(8,128)(2,1)S(1)}, u32[]{:S(2)}, u32[]{:S(2)}) %collective-permute-start.2) | collective-permute-done | bytes 90144 | tf_op jit(solution)/shard_map/ppermute | solution.py:479
  16.5 5.1 %collective-permute-start.7 = (bf16[176,256]{1,0:T(8,128)(2,1)S(1)}, bf16[176,256]{1,0:T(8,128)(2,1)S(1)}, u32[]{:S(2)}, u32[]{:S(2)}) collective-permute-start(bf16[176,256]{1,0:T(8,128)(2,1)S(1)} %shard_map.113.refs_0_), channel_id=1, source_target_pairs={{0,6},{1,7},{2,4},{3,5},{4,2},{5,3},{6,0},{7,1},{8,14},{9,15},{10,... | collective-permute-start | bytes 270344 | tf_op jit(solution)/shard_map/ppermute | solution.py:479
  21.6 0.0 collective-permute-done.3.refs_2_
  21.6 1.2 %collective-permute-start.8 = (bf16[176,256]{1,0:T(8,128)(2,1)S(1)}, bf16[176,256]{1,0:T(8,128)(2,1)S(1)}, u32[]{:S(2)}, u32[]{:S(2)}) collective-permute-start(bf16[176,256]{1,0:T(8,128)(2,1)S(1)} %shard_map.113.refs_0_), channel_id=1, source_target_pairs={{0,7},{1,6},{2,5},{3,4},{4,3},{5,2},{6,1},{7,0},{8,15},{9,14},{10,... | collective-permute-start | bytes 270344 | tf_op jit(solution)/shard_map/ppermute | solution.py:479
  22.8 0.0 collective-permute-done.4.refs_3_
  22.8 0.9 %collective-permute-done.5.refs_4_ = bf16[176,256]{1,0:T(8,128)(2,1)S(1)} collective-permute-done((bf16[176,256]{1,0:T(8,128)(2,1)S(1)}, bf16[176,256]{1,0:T(8,128)(2,1)S(1)}, u32[]{:S(2)}, u32[]{:S(2)}) %collective-permute-start.5) | collective-permute-done | bytes 90144 | tf_op jit(solution)/shard_map/ppermute | solution.py:479
  23.7 2.9 %collective-permute-done.6.refs_5_ = bf16[176,256]{1,0:T(8,128)(2,1)S(1)} collective-permute-done((bf16[176,256]{1,0:T(8,128)(2,1)S(1)}, bf16[176,256]{1,0:T(8,128)(2,1)S(1)}, u32[]{:S(2)}, u32[]{:S(2)}) %collective-permute-start.6) | collective-permute-done | bytes 90144 | tf_op jit(solution)/shard_map/ppermute | solution.py:479
  26.6 0.0 collective-permute-done.7.refs_6_
  26.6 4.0 %collective-permute-done.8.refs_7_ = bf16[176,256]{1,0:T(8,128)(2,1)S(1)} collective-permute-done((bf16[176,256]{1,0:T(8,128)(2,1)S(1)}, bf16[176,256]{1,0:T(8,128)(2,1)S(1)}, u32[]{:S(2)}, u32[]{:S(2)}) %collective-permute-start.8) | collective-permute-done | bytes 90144 | tf_op jit(solution)/shard_map/ppermute | solution.py:479
  30.6 0.1 shard_map.114
  30.7 1.1 %collective-permute-start.9 = (bf16[384,768]{1,0:T(8,128)(2,1)S(1)}, bf16[384,768]{1,0:T(8,128)(2,1)S(1)}, u32[]{:S(2)}, u32[]{:S(2)}) collective-permute-start(bf16[384,768]{1,0:T(8,128)(2,1)S(1)} %get-tuple-element.22.mine_ref), channel_id=1, source_target_pairs={{0,8},{8,0},{1,9},{9,1},{2,10},{10,2},{3,11},{11,3},{4,12},{12,4},... | collective-permute-start | bytes 1769480 | tf_op jit(solution)/shard_map/ppermute | solution.py:501
  31.8 0.0 all-to-all-done.own_ref
  31.8 0.6 shard_map.110
  32.4 0.3 collective-permute-start
  32.7 1.5 %collective-permute-start.1 = (bf16[8,96,256]{2,1,0:T(8,128)(2,1)S(1)}, bf16[8,96,256]{2,1,0:T(8,128)(2,1)S(1)}, u32[]{:S(2)}, u32[]{:S(2)}) collective-permute-start(bf16[8,96,256]{2,1,0:T(8,128)(2,1)S(1)} %get-tuple-element.17), channel_id=1, source_target_pairs={{0,254},{1,255},{2,4},{3,5},{4,2},{5,3},{6,8},{7,9},{8,6},{9,7},{1... | collective-permute-start | bytes 1179656 | tf_op jit(solution)/shard_map/ppermute | solution.py:493
  34.2 26.2 %all_to_all.27 = f32[256,1,128]{2,1,0:T(1,128)S(1)} all-to-all(f32[256,1,128]{2,1,0:T(1,128)S(1)} %bitcast.16), channel_id=1, replica_groups=mesh['band_0'=8,'band_1'=2,'band_2'=2,'chan_0'=4,'chan_1'=2] {'band_0','..., dimensions={0} | all-to-all | bytes 262144 | tf_op jit(solution)/shard_map/all_to_all | solution.py:494
  60.4 0.1 shard_map.111.lat_stats_ref
  60.5 0.0 collective-permute-done.one_ref
  60.5 0.0 collective-permute-done.1.two_ref
  60.5 1.8 %shard_map.112 = (bf16[2,768,512]{2,1,0:T(8,128)(2,1)S(1)}, bf16[768,128]{1,0:T(8,128)(2,1)S(1)}) custom-call(bf16[8,80,512]{2,1,0:T(8,128)(2,1)S(1)} %all-to-all-done.own_ref, bf16[8,96,256]{2,1,0:T(8,128)(2,1)S(1)} %collective-permute-done.one_ref, bf16[8,96,256]{2,1,0:T(8,128)(2,1)S(1)} %collective-permute-done.1.two_ref, ...), custom_call_target="tpu_custom_call" | custom-call | flops 939524096 | bytes 1048576 | tf_op jit(solution)/shard_map/pallas_call | solution.py:423
  62.3 0.0 collective-permute-done.9.other_ref
  62.3 0.0 copy-start.1
  62.3 2.2 %shard_map.115 = (f32[2,256,256]{2,1,0:T(8,128)S(1)}, f32[2,256,256]{2,1,0:T(8,128)S(1)}, f32[256,128]{1,0:T(8,128)S(1)}) custom-call(bf16[2,768,512]{2,1,0:T(8,128)(2,1)S(1)} %get-tuple-element.20.joined_ref, bf16[768,128]{1,0:T(8,128)(2,1)S(1)} %get-tuple-element.21.beside_ref, bf16[384,768]{1,0:T(8,128)(2,1)S(1)} %get-tuple-element.22.mine_ref, ...), custom_call_target="tpu_custom_call" | custom-call | flops 1207959552 | bytes 1048576 | tf_op jit(solution)/shard_map/pallas_call | solution.py:423
  64.5 0.6 collective-permute-start.10
  65.1 18.9 %all_to_all.28 = f32[256,1,128]{2,1,0:T(1,128)S(1)} all-to-all(f32[256,1,128]{2,1,0:T(1,128)S(1)} %bitcast.17), channel_id=1, replica_groups=mesh['band_0'=8,'band_1'=2,'band_2'=2,'chan_0'=4,'chan_1'=2] {'band_0','..., dimensions={0} | all-to-all | bytes 262144 | tf_op jit(solution)/shard_map/all_to_all | solution.py:518
  84.0 0.0 collective-permute-done.10.taken_ref
  84.0 0.0 copy-done.1
  84.0 2.4 %shard_map.116 = f32[1600,128]{1,0:T(8,128)} custom-call(f32[2,256,256]{2,1,0:T(8,128)S(1)} %get-tuple-element.23.keep_ref, f32[2,256,256]{2,1,0:T(8,128)S(1)} %collective-permute-done.10.taken_ref, f32[256,128]{1,0:T(8,128)S(1)} %bitcast.14, bf16[256,256]{1,0:T(8,128)(2,1)S(1)} %get-tuple-element.18.lat_weight_ref, ...), custom_call_target="tpu_custom_call" | custom-call | flops 268435456 | bytes 1048576 | tf_op jit(solution)/shard_map/pallas_call | solution.py:423
  (1 shorter events, 0.0 us)
Async XLA Ops:
  0.0 8.2 %copy-start = (bf16[3,3,32,256]{3,2,1,0:T(8,128)(2,1)S(1)}, bf16[3,3,32,256]{3,2,1,0:T(8,128)(2,1)}, u32[]{:S(2)}) copy-start(bf16[3,3,32,256]{3,2,1,0:T(8,128)(2,1)} %conv_ref.1) | copy-start | bytes 442372
  0.0 8.2 %copy-start.2 = (bf16[32,256]{1,0:T(8,128)(2,1)S(1)}, bf16[32,256]{1,0:T(8,128)(2,1)}, u32[]{:S(2)}) copy-start(bf16[32,256]{1,0:T(8,128)(2,1)} %mask_ref.1) | copy-start | bytes 49156
  2.3 29.5 %all-to-all-start = ((bf16[8,80,512]{2,1,0:T(8,128)(2,1)}), bf16[8,80,512]{2,1,0:T(8,128)(2,1)S(1)}, u32[]{:S(2)}, u32[]{:S(2)}) async-start(bf16[8,80,512]{2,1,0:T(8,128)(2,1)} %shard_map.109), calls=%async_computation | async-start | bytes 1310720 | tf_op jit(solution)/shard_map/all_to_all | solution.py:477
  8.2 8.3 %collective-permute-start.2 = (bf16[176,256]{1,0:T(8,128)(2,1)S(1)}, bf16[176,256]{1,0:T(8,128)(2,1)S(1)}, u32[]{:S(2)}, u32[]{:S(2)}) collective-permute-start(bf16[176,256]{1,0:T(8,128)(2,1)S(1)} %shard_map.113.refs_0_), channel_id=1, source_target_pairs={{0,1},{1,0},{2,3},{3,2},{4,5},{5,4},{6,7},{7,6},{8,9},{9,8},{10,11... | collective-permute-start | bytes 270344 | tf_op jit(solution)/shard_map/ppermute | solution.py:479
  9.8 11.8 %collective-permute-start.3 = (bf16[176,256]{1,0:T(8,128)(2,1)S(1)}, bf16[176,256]{1,0:T(8,128)(2,1)S(1)}, u32[]{:S(2)}, u32[]{:S(2)}) collective-permute-start(bf16[176,256]{1,0:T(8,128)(2,1)S(1)} %shard_map.113.refs_0_), channel_id=1, source_target_pairs={{0,2},{1,3},{2,0},{3,1},{4,6},{5,7},{6,4},{7,5},{8,10},{9,11},{10,... | collective-permute-start | bytes 270344 | tf_op jit(solution)/shard_map/ppermute | solution.py:479
  11.0 11.9 %collective-permute-start.4 = (bf16[176,256]{1,0:T(8,128)(2,1)S(1)}, bf16[176,256]{1,0:T(8,128)(2,1)S(1)}, u32[]{:S(2)}, u32[]{:S(2)}) collective-permute-start(bf16[176,256]{1,0:T(8,128)(2,1)S(1)} %shard_map.113.refs_0_), channel_id=1, source_target_pairs={{0,3},{1,2},{2,1},{3,0},{4,7},{5,6},{6,5},{7,4},{8,11},{9,10},{10,... | collective-permute-start | bytes 270344 | tf_op jit(solution)/shard_map/ppermute | solution.py:479
  11.1 12.7 %collective-permute-start.5 = (bf16[176,256]{1,0:T(8,128)(2,1)S(1)}, bf16[176,256]{1,0:T(8,128)(2,1)S(1)}, u32[]{:S(2)}, u32[]{:S(2)}) collective-permute-start(bf16[176,256]{1,0:T(8,128)(2,1)S(1)} %shard_map.113.refs_0_), channel_id=1, source_target_pairs={{0,4},{1,5},{2,6},{3,7},{4,0},{5,1},{6,2},{7,3},{8,12},{9,13},{10,... | collective-permute-start | bytes 270344 | tf_op jit(solution)/shard_map/ppermute | solution.py:479
  13.9 12.7 %collective-permute-start.6 = (bf16[176,256]{1,0:T(8,128)(2,1)S(1)}, bf16[176,256]{1,0:T(8,128)(2,1)S(1)}, u32[]{:S(2)}, u32[]{:S(2)}) collective-permute-start(bf16[176,256]{1,0:T(8,128)(2,1)S(1)} %shard_map.113.refs_0_), channel_id=1, source_target_pairs={{0,5},{1,4},{2,7},{3,6},{4,1},{5,0},{6,3},{7,2},{8,13},{9,12},{10,... | collective-permute-start | bytes 270344 | tf_op jit(solution)/shard_map/ppermute | solution.py:479
  16.5 10.1 %collective-permute-start.7 = (bf16[176,256]{1,0:T(8,128)(2,1)S(1)}, bf16[176,256]{1,0:T(8,128)(2,1)S(1)}, u32[]{:S(2)}, u32[]{:S(2)}) collective-permute-start(bf16[176,256]{1,0:T(8,128)(2,1)S(1)} %shard_map.113.refs_0_), channel_id=1, source_target_pairs={{0,6},{1,7},{2,4},{3,5},{4,2},{5,3},{6,0},{7,1},{8,14},{9,15},{10,... | collective-permute-start | bytes 270344 | tf_op jit(solution)/shard_map/ppermute | solution.py:479
  21.6 9.0 %collective-permute-start.8 = (bf16[176,256]{1,0:T(8,128)(2,1)S(1)}, bf16[176,256]{1,0:T(8,128)(2,1)S(1)}, u32[]{:S(2)}, u32[]{:S(2)}) collective-permute-start(bf16[176,256]{1,0:T(8,128)(2,1)S(1)} %shard_map.113.refs_0_), channel_id=1, source_target_pairs={{0,7},{1,6},{2,5},{3,4},{4,3},{5,2},{6,1},{7,0},{8,15},{9,14},{10,... | collective-permute-start | bytes 270344 | tf_op jit(solution)/shard_map/ppermute | solution.py:479
  30.7 31.6 %collective-permute-start.9 = (bf16[384,768]{1,0:T(8,128)(2,1)S(1)}, bf16[384,768]{1,0:T(8,128)(2,1)S(1)}, u32[]{:S(2)}, u32[]{:S(2)}) collective-permute-start(bf16[384,768]{1,0:T(8,128)(2,1)S(1)} %get-tuple-element.22.mine_ref), channel_id=1, source_target_pairs={{0,8},{8,0},{1,9},{9,1},{2,10},{10,2},{3,11},{11,3},{4,12},{12,4},... | collective-permute-start | bytes 1769480 | tf_op jit(solution)/shard_map/ppermute | solution.py:501
  32.4 28.1 %collective-permute-start = (bf16[8,96,256]{2,1,0:T(8,128)(2,1)S(1)}, bf16[8,96,256]{2,1,0:T(8,128)(2,1)S(1)}, u32[]{:S(2)}, u32[]{:S(2)}) collective-permute-start(bf16[8,96,256]{2,1,0:T(8,128)(2,1)S(1)} %get-tuple-element.16), channel_id=1, source_target_pairs={{0,2},{1,3},{2,0},{3,1},{4,6},{5,7},{6,4},{7,5},{8,10},{9,11},{10,... | collective-permute-start | bytes 1179656 | tf_op jit(solution)/shard_map/ppermute | solution.py:492
  32.7 27.8 %collective-permute-start.1 = (bf16[8,96,256]{2,1,0:T(8,128)(2,1)S(1)}, bf16[8,96,256]{2,1,0:T(8,128)(2,1)S(1)}, u32[]{:S(2)}, u32[]{:S(2)}) collective-permute-start(bf16[8,96,256]{2,1,0:T(8,128)(2,1)S(1)} %get-tuple-element.17), channel_id=1, source_target_pairs={{0,254},{1,255},{2,4},{3,5},{4,2},{5,3},{6,8},{7,9},{8,6},{9,7},{1... | collective-permute-start | bytes 1179656 | tf_op jit(solution)/shard_map/ppermute | solution.py:493
  62.3 21.7 %copy-start.1 = (bf16[200,256]{1,0:T(8,128)(2,1)S(1)}, bf16[200,256]{1,0:T(8,128)(2,1)}, u32[]{:S(2)}) copy-start(bf16[200,256]{1,0:T(8,128)(2,1)} %query_ref.1) | copy-start | bytes 307204
  64.5 19.5 %collective-permute-start.10 = (f32[2,256,256]{2,1,0:T(8,128)S(1)}, f32[2,256,256]{2,1,0:T(8,128)S(1)}, u32[]{:S(2)}, u32[]{:S(2)}) collective-permute-start(f32[2,256,256]{2,1,0:T(8,128)S(1)} %get-tuple-element.24), channel_id=1, source_target_pairs={{0,1},{1,0},{2,3},{3,2},{4,5},{5,4},{6,7},{7,6},{8,9},{9,8},{10,11... | collective-permute-start | bytes 1572872 | tf_op jit(solution)/shard_map/ppermute | solution.py:517

commit v4 on v2

--- a/solution.py
+++ b/solution.py
@@ -19,14 +19,13 @@
 EPS = 1e-05
 F32 = jnp.float32
 BF16 = jnp.bfloat16
-OWN_ROWS = 80
+OWN_ROWS = 120
 VECTORS = 64
 FINE_EDGE = 72
 COARSE_EDGE = 80
 SIDE_ROWS = 96
-MASK_AT = 72
-XORS = (4, 1, 2, 5, 6, 3, 7)
-SHARD_ROWS = 80
+BLOCKS = 5
+MASK_AT = 144
 
 
 def dot(a, b):
@@ -89,11 +88,12 @@
     )
 
 
-def pack_own_kernel(fine_hbm, coarse_hbm, weight_hbm, *refs):
-    vec_hbm, own_hbm = refs[:5], refs[5]
-    fine_ref, coarse_ref, weight_ref, vec_ref, own_ref, rows, coarse, sems, out_sems = refs[6:]
+def pack_own_kernel(fine_hbm, coarse_hbm, weight_hbm, conv_hbm, mask_hbm, *refs):
+    vec_hbm, own_ref = refs[:5], refs[5]
+    fine_ref, coarse_ref, weight_ref, conv_ref, vec_ref, rows, coarse, sems = refs[6:]
     pairs = [(coarse_hbm, coarse_ref), (weight_hbm, weight_ref)]
-    pairs += [(vec, vec_ref.at[i]) for i, vec in enumerate(vec_hbm)] + [(fine_hbm, fine_ref)]
+    pairs += [(vec, vec_ref.at[i]) for i, vec in enumerate(vec_hbm)]
+    pairs += [(conv_hbm, conv_ref.at[pl.ds(0, 9)]), (mask_hbm, conv_ref.at[9]), (fine_hbm, fine_ref)]
     copies = [
         pltpu.make_async_copy(source, target, sems.at[i])
         for i, (source, target) in enumerate(pairs)
@@ -106,7 +106,7 @@
         for t in range(2):
             piece = coarse_ref[n, :, :, 128 * t : 128 * t + 128].astype(F32)
             piece = jnp.concatenate([piece, jnp.zeros_like(piece)], axis=1)
-            coarse[n, t] = piece.reshape(256, 128)
+            coarse[n, t, 0:256] = piece.reshape(256, 128)
     lane = lanes_of((32, 128))
     vec_lane = lanes_of((32, 32))
     vec_row = lax.broadcasted_iota(jnp.int32, (32, 32), 0)
@@ -116,6 +116,11 @@
         vec = jnp.where(vec_lane == vec_row, vec_ref[i].astype(F32), 0.0)
         second += jnp.where(lane == VECTORS + i, jnp.sum(vec, axis=1, keepdims=True), 0.0)
     first = weight[:, 0:128].astype(BF16)
+    half = pl.multiple_of(16 * lax.axis_index("band_2"), 16)
+    block = BLOCKS * (lax.axis_index("band_0") % 2)
+    blocks = [conv_ref[block + i, pl.ds(half, 16), :] for i in range(BLOCKS)]
+    last = blocks[4].astype(F32)
+    last = jnp.concatenate([last[0:8], last[8:16]], axis=1).astype(BF16)
     tails = []
     for h in range(2):
         for q in range(4):
@@ -123,6 +128,10 @@
             tail = second
             own_ref[d, 48:64, 0:128] = first[0:16]
             own_ref[d, 48:64, 256:384] = first[16:32]
+            for i in range(4):
+                at = 80 + 16 * (i // 2)
+                own_ref[d, at : at + 16, 256 * (i % 2) : 256 * (i % 2) + 256] = blocks[i]
+            own_ref[d, 112:120, :] = last
             for n in range(2):
                 row = coarse[n, h, pl.ds(q, 32, stride=8), :].astype(BF16)
                 own_ref[d, 64:80, 128 * n : 128 * n + 128] = row[0:16]
@@ -134,8 +143,7 @@
     copies[-1].wait()
     for t in range(4):
         piece = fine_ref[:, :, :, 128 * t : 128 * t + 128].astype(F32)
-        rows[t] = piece.reshape(48 * 8, 128)
-    out = []
+        rows[t, 0:384] = piece.reshape(48 * 8, 128)
     for h in range(2):
         for q in range(4):
             d = 2 * q + h
@@ -155,36 +163,29 @@
             tail = tail.astype(BF16)
             own_ref[d, 48:64, 128:256] = tail[0:16]
             own_ref[d, 48:64, 384:512] = tail[16:32]
-            out.append(pltpu.make_async_copy(own_ref.at[d], own_hbm.at[d], out_sems.at[d]))
-            out[-1].start()
-    for copy in out:
-        copy.wait()
-
-
-def pack_weights_kernel(conv_ref, mask_ref, shard_ref):
-    half = pl.multiple_of(16 * lax.axis_index("band_2"), 16)
-    for k in range(10):
-        if k < 9:
-            piece = conv_ref[k // 3, k % 3, pl.ds(half, 16), :].astype(F32)
-        else:
-            piece = mask_ref[pl.ds(half, 16), :].astype(F32)
-        piece = jnp.concatenate([piece[0:8], piece[8:16]], axis=1).astype(BF16)
-        shard_ref[8 * k : 8 * k + 8] = piece
-
-
-def arrange_kernel(*refs):
-    chan = lax.axis_index("chan_0") * 2 + lax.axis_index("chan_1")
-    all_ref = refs[-1]
-    for k, ref in enumerate(refs[:-1]):
-        all_ref[chan ^ k] = ref[...]
-
-
-def lateral_kernel(own_ref, weight_ref, stats_ref, one_ref, two_ref):
+
+
+def arrange_kernel(quarter_ref, other_ref, all_ref):
+    parity = lax.axis_index("band_0") % 2
+    rows = 16 * BLOCKS
+    all_ref[:, pl.ds(pl.multiple_of(rows * parity, 16), rows), :] = quarter_ref[...]
+    all_ref[:, pl.ds(pl.multiple_of(rows - rows * parity, 16), rows), :] = other_ref[...]
+
+
+def lateral_kernel(own_ref, weight_ref, stats_ref, one_ref, two_ref, quarter_ref):
     for s in range(8):
         for half in range(2):
             weight_ref[32 * s + 16 * half : 32 * s + 16 * half + 16, :] = own_ref[
                 s, 48:64, 256 * half : 256 * half + 256
             ]
+    for s in range(8):
+        for i in range(4):
+            at = 80 + 16 * (i // 2)
+            quarter_ref[s, 16 * i : 16 * i + 16] = own_ref[
+                s, at : at + 16, 256 * (i % 2) : 256 * (i % 2) + 256
+            ]
+        last = own_ref[s, 112:120, :]
+        quarter_ref[s, 64:80] = jnp.concatenate([last[:, 0:256], last[:, 256:512]], axis=0)
     odd = lax.axis_index("chan_0") % 2
     for ref, row in ((one_ref, 1 - odd), (two_ref, odd)):
         at = pl.multiple_of(256 * row, 256)
@@ -350,9 +351,8 @@
             at = pl.multiple_of(32 * s + 16 * part, 16)
             for a in range(3):
                 for b in range(3):
-                    piece = ref[s, (a * 3 + b) * 8 : (a * 3 + b) * 8 + 8, :]
-                    both = jnp.concatenate([piece[:, 0:256], piece[:, 256:512]], axis=0)
-                    weight[b, pl.ds(at, 16), 256 * a : 256 * a + 256] = both
+                    block = ref[s, 16 * (3 * a + b) : 16 * (3 * a + b) + 16, :]
+                    weight[b, pl.ds(at, 16), 256 * a : 256 * a + 256] = block
     inner_edge = jnp.where(side == 0, HALF - 1, 0)
     lane = lax.broadcasted_iota(jnp.int32, (GROUPS, 1, 128), 2)
     lane_at = lanes_of((D, HALF))
@@ -385,9 +385,7 @@
     for part, ref in ((core, mine_ref), (1 - core, other_ref)):
         for s in range(8):
             at = pl.multiple_of(32 * s + 16 * part, 16)
-            piece = ref[s, MASK_AT : MASK_AT + 8, :]
-            both = jnp.concatenate([piece[:, 0:256], piece[:, 256:512]], axis=0)
-            weight[pl.ds(at, 16), :] = both
+            weight[pl.ds(at, 16), :] = ref[s, MASK_AT : MASK_AT + 16, :]
     gain = vector_col(lat_weight_ref, 2)
     shift = vector_col(lat_weight_ref, 3)
     bias = vector_col(lat_weight_ref, 4)
@@ -435,8 +433,8 @@
 ):
     everyone = lax.axis_size(ALL)
     stats_shape = jax.ShapeDtypeStruct((everyone, 128), F32)
-    shard_shape = jax.ShapeDtypeStruct((SHARD_ROWS, COLS), BF16)
-    all_shape = jax.ShapeDtypeStruct((8, SHARD_ROWS, COLS), BF16)
+    quarter_shape = jax.ShapeDtypeStruct((8, 16 * BLOCKS, D), BF16)
+    all_shape = jax.ShapeDtypeStruct((8, 32 * BLOCKS, D), BF16)
     side_shape = jax.ShapeDtypeStruct((8, SIDE_ROWS, HALF), BF16)
     half_shape = jax.ShapeDtypeStruct((2, D, HALF), F32)
     swap = [(0, 1), (1, 0)]
@@ -444,29 +442,24 @@
     vectors = [v.reshape(1, 32) for v in (lat_gain, lat_shift, out_gain, out_shift, mask_bias)]
     own_out = call(
         pack_own_kernel,
-        jax.ShapeDtypeStruct((8, OWN_ROWS, COLS), BF16),
+        pltpu.VMEM((8, OWN_ROWS, COLS), BF16),
         (
             pltpu.VMEM((2, 24, 8, COLS), BF16),
             pltpu.VMEM((2, 32, 4, 256), BF16),
             pltpu.VMEM((32, IN_CH), BF16),
+            pltpu.VMEM((10, 32, D), BF16),
             pltpu.VMEM((5, 1, 32), BF16),
-            pltpu.VMEM((8, OWN_ROWS, COLS), BF16),
-            pltpu.VMEM((4, 48 * 8, 128), F32),
-            pltpu.VMEM((2, 2, 256, 128), F32),
-            pltpu.SemaphoreType.DMA((8,)),
-            pltpu.SemaphoreType.DMA((8,)),
+            pltpu.VMEM((4, 48 * 8 + 8, 128), F32),
+            pltpu.VMEM((2, 2, 256 + 8, 128), F32),
+            pltpu.SemaphoreType.DMA((10,)),
         ),
         space=pltpu.HBM,
-        out_space=pltpu.HBM,
         limit=60 << 20,
-    )(fine_features, coarse_level, lat_weight, *vectors)
+    )(fine_features, coarse_level, lat_weight, out_weight.reshape(9, 32, D), mask_weight, *vectors)
     own = lax.all_to_all(own_out, CHAN, 0, 0, tiled=True)
-    shard = call(pack_weights_kernel, shard_shape)(out_weight, mask_weight)
-    moved = [lax.ppermute(shard, CHAN, [(i, i ^ k) for i in range(8)]) for k in XORS]
-
-    full_lat, stats, first, second = call(
+    full_lat, stats, first, second, quarter = call(
         lateral_kernel,
-        [jax.ShapeDtypeStruct((D, 256), BF16), stats_shape, side_shape, side_shape],
+        [jax.ShapeDtypeStruct((D, 256), BF16), stats_shape, side_shape, side_shape, quarter_shape],
         flops=2 * 2 * 256 * 256 * 512,
     )(own)
     pairs = everyone // 2
@@ -477,11 +470,12 @@
     ]
     first = lax.ppermute(first, ALL, swap_at(0))
     second = lax.ppermute(second, ALL, swap_at(1))
+    depth = lax.axis_size("band_0")
+    other_quarter = lax.ppermute(quarter, "band_0", [(i, i ^ 1) for i in range(depth)])
     stats = lax.all_to_all(stats, ALL, 0, 0, tiled=True)
     stats = call(combine_kernel, jax.ShapeDtypeStruct((8, 128), F32), flops=1 << 20)(stats)
 
-    by_xor = dict(zip(XORS, moved))
-    mine = call(arrange_kernel, all_shape)(shard, *[by_xor[k] for k in range(1, 8)])
+    mine = call(arrange_kernel, all_shape)(quarter, other_quarter)
     other = lax.ppermute(mine, "band_2", swap)
     joined, beside = call(
         join_kernel,

time: 85.5 us -> 86.5 us (1.012)
  blocking collectives: 45.1 us -> 64.7 us
  starting transfers between devices: 22.5 us -> 6.82 us
  waiting for transfers between devices: 8.27 us -> 5.93 us
    all_to_all x0 -> x1, blocking collectives: none -> 19.3 us  [per_device(): own = lax.all_to_all(own_out, CHAN, 0, 0, tiled=True)]
    ppermute x7 -> x1, starting transfers between devices: 13.2 us -> 1.73 us  [per_device(): lax.ppermute(quarter, 'band_0', [(i, i ^ 1) for i in range(depth)])]
    all_to_all x1 -> x0, starting transfers between devices: 5.86 us -> none  [per_device(): own = lax.all_to_all(own_out, CHAN, 0, 0, tiled=True)]
    ppermute x7 -> x1, waiting for transfers between devices: 8.25 us -> 5.92 us  [per_device(): lax.ppermute(quarter, 'band_0', [(i, i ^ 1) for i in range(depth)])]
    ppermute x1, starting transfers between devices: 1.08 us -> 2.83 us  [per_device(): other = lax.ppermute(mine, 'band_2', swap)]
    pallas_call x8 -> x7, Pallas kernels: 9.26 us -> 8.74 us  [call(): pl.pallas_call(kernel, out_shape=out_shape, in_specs=[pl.BlockSpec(memory...]
  transfers between devices with their start and end apart: 12 -> 5, of which waited for: 4 -> 1; matrix products, arithmetic and copies ran while one was open for 0% -> 0% of each run, Pallas kernels for 3% -> 2%
where the time goes in v4:
time: 86.5 us; the launch traced here: 86.3 us
  blocking collectives  64.7 us (75%)
  Pallas kernels  8.74 us (10%)
  starting transfers between devices  6.82 us (8%)
  waiting for transfers between devices  5.93 us (7%)
    all_to_all x2, blocking collectives, per_device(): stats = lax.all_to_all(stats, ALL, 0, 0, tiled=True)  45.4 us
    all_to_all x1, blocking collectives, per_device(): own = lax.all_to_all(own_out, CHAN, 0, 0, tiled=True)  19.3 us
    pallas_call x7, Pallas kernels, call(): pl.pallas_call(kernel, out_shape=out_shape, in_specs=[pl.BlockSpec(memory...  8.74 us
    ppermute x1, waiting for transfers between devices, per_device(): lax.ppermute(quarter, 'band_0', [(i, i ^ 1) for i in range(depth)])  5.92 us
    ppermute x1, starting transfers between devices, per_device(): other = lax.ppermute(mine, 'band_2', swap)  2.83 us
  transfers between devices with their start and end apart: 5, of which 1 were waited for; matrix products, arithmetic and copies ran while one was open for 0% of the time, Pallas kernels for 2%

profile of v4, /device:TPU:1, one launch (start us, length us, event | category | flops | bytes accessed | tf_op | source)
XLA Modules:
  0.0 86.3 jit_solution(8584943402080226554)
XLA Ops:
  0.0 1.7 %shard_map.109 = bf16[8,120,512]{2,1,0:T(8,128)(2,1)S(1)} custom-call(bf16[2,24,8,512]{3,2,1,0:T(8,128)(2,1)} %fine_hbm.1, bf16[2,32,4,256]{3,2,1,0:T(4,128)(2,1)} %coarse_hbm.1, bf16[32,192]{1,0:T(8,128)(2,1)} %weight_hbm.1, bf16[9,32,256]{2,1,0:T(8,128)(2,1)} %bitcast.19, bf16[32,256]{1,0:T(8,128)(2,1)} %mask_hbm.1, bf16[1,32]{1,0:T(2,128)(2,1)} %bitcast.20, ...), custom_call_target="tpu_custom_call" | custom-call | bytes 1048576 | tf_op jit(solution)/shard_map/pallas_call | solution.py:410
  1.7 19.3 %all_to_all.27.own_ref = bf16[8,120,512]{2,1,0:T(8,128)(2,1)S(1)} all-to-all(bf16[8,120,512]{2,1,0:T(8,128)(2,1)S(1)} %shard_map.109), channel_id=1, replica_groups=mesh['band_0'=8,'band_1'=2,'band_2'=2,'chan_0'=4,'chan_1'=2] {'chan_0','..., dimensions={0} | all-to-all | bytes 1966080 | tf_op jit(solution)/shard_map/all_to_all | solution.py:459
  21.0 0.6 shard_map.110
  21.6 1.7 %collective-permute-start.2 = (bf16[8,80,256]{2,1,0:T(8,128)(2,1)S(1)}, bf16[8,80,256]{2,1,0:T(8,128)(2,1)S(1)}, u32[]{:S(2)}, u32[]{:S(2)}) collective-permute-start(bf16[8,80,256]{2,1,0:T(8,128)(2,1)S(1)} %get-tuple-element.21.quarter_ref), channel_id=1, source_target_pairs={{0,32},{32,0},{64,96},{96,64},{128,160},{160,128},{192,224},{224,1... | collective-permute-start | bytes 983048 | tf_op jit(solution)/shard_map/ppermute | solution.py:474
  23.3 5.9 %collective-permute-done.2.other_ref = bf16[8,80,256]{2,1,0:T(8,128)(2,1)S(1)} collective-permute-done((bf16[8,80,256]{2,1,0:T(8,128)(2,1)S(1)}, bf16[8,80,256]{2,1,0:T(8,128)(2,1)S(1)}, u32[]{:S(2)}, u32[]{:S(2)}) %collective-permute-start.2) | collective-permute-done | bytes 327712 | tf_op jit(solution)/shard_map/ppermute | solution.py:474
  29.2 0.1 shard_map.113.mine_ref
  29.3 2.8 %collective-permute-start.3 = (bf16[8,160,256]{2,1,0:T(8,128)(2,1)S(1)}, bf16[8,160,256]{2,1,0:T(8,128)(2,1)S(1)}, u32[]{:S(2)}, u32[]{:S(2)}) collective-permute-start(bf16[8,160,256]{2,1,0:T(8,128)(2,1)S(1)} %shard_map.113.mine_ref), channel_id=1, source_target_pairs={{0,8},{8,0},{1,9},{9,1},{2,10},{10,2},{3,11},{11,3},{4,12},{12,4},... | collective-permute-start | bytes 1966088 | tf_op jit(solution)/shard_map/ppermute | solution.py:479
  32.1 0.2 collective-permute-start
  32.4 1.6 %collective-permute-start.1 = (bf16[8,96,256]{2,1,0:T(8,128)(2,1)S(1)}, bf16[8,96,256]{2,1,0:T(8,128)(2,1)S(1)}, u32[]{:S(2)}, u32[]{:S(2)}) collective-permute-start(bf16[8,96,256]{2,1,0:T(8,128)(2,1)S(1)} %get-tuple-element.16), channel_id=1, source_target_pairs={{0,254},{1,255},{2,4},{3,5},{4,2},{5,3},{6,8},{7,9},{8,6},{9,7},{1... | collective-permute-start | bytes 1179656 | tf_op jit(solution)/shard_map/ppermute | solution.py:472
  34.0 26.6 %all_to_all.28 = f32[256,1,128]{2,1,0:T(1,128)S(1)} all-to-all(f32[256,1,128]{2,1,0:T(1,128)S(1)} %bitcast.17), channel_id=1, replica_groups=mesh['band_0'=8,'band_1'=2,'band_2'=2,'chan_0'=4,'chan_1'=2] {'band_0','..., dimensions={0} | all-to-all | bytes 262144 | tf_op jit(solution)/shard_map/all_to_all | solution.py:475
  60.5 0.1 shard_map.111.lat_stats_ref
  60.6 0.0 collective-permute-done.one_ref
  60.6 0.0 collective-permute-done.1.two_ref
  60.6 1.8 %shard_map.112 = (bf16[2,768,512]{2,1,0:T(8,128)(2,1)S(1)}, bf16[768,128]{1,0:T(8,128)(2,1)S(1)}) custom-call(bf16[8,120,512]{2,1,0:T(8,128)(2,1)S(1)} %all_to_all.27.own_ref, bf16[8,96,256]{2,1,0:T(8,128)(2,1)S(1)} %collective-permute-done.one_ref, bf16[8,96,256]{2,1,0:T(8,128)(2,1)S(1)} %collective-permute-done.1.two_ref, ...), custom_call_target="tpu_custom_call" | custom-call | flops 939524096 | bytes 1048576 | tf_op jit(solution)/shard_map/pallas_call | solution.py:410
  62.5 0.0 collective-permute-done.3.other_ref
  62.5 0.0 copy-start
  62.5 2.0 %shard_map.114 = (f32[2,256,256]{2,1,0:T(8,128)S(1)}, f32[2,256,256]{2,1,0:T(8,128)S(1)}, f32[256,128]{1,0:T(8,128)S(1)}) custom-call(bf16[2,768,512]{2,1,0:T(8,128)(2,1)S(1)} %get-tuple-element.19.joined_ref, bf16[768,128]{1,0:T(8,128)(2,1)S(1)} %get-tuple-element.20.beside_ref, bf16[8,160,256]{2,1,0:T(8,128)(2,1)S(1)} %shard_map.113.mine_ref, ...), custom_call_target="tpu_custom_call" | custom-call | flops 1207959552 | bytes 1048576 | tf_op jit(solution)/shard_map/pallas_call | solution.py:410
  64.5 0.4 collective-permute-start.4
  64.9 18.9 %all_to_all.29 = f32[256,1,128]{2,1,0:T(1,128)S(1)} all-to-all(f32[256,1,128]{2,1,0:T(1,128)S(1)} %bitcast.18), channel_id=1, replica_groups=mesh['band_0'=8,'band_1'=2,'band_2'=2,'chan_0'=4,'chan_1'=2] {'band_0','..., dimensions={0} | all-to-all | bytes 262144 | tf_op jit(solution)/shard_map/all_to_all | solution.py:496
  83.8 0.0 collective-permute-done.4.taken_ref
  83.8 0.0 copy-done
  83.8 2.5 %shard_map.115 = f32[1600,128]{1,0:T(8,128)} custom-call(f32[2,256,256]{2,1,0:T(8,128)S(1)} %get-tuple-element.22.keep_ref, f32[2,256,256]{2,1,0:T(8,128)S(1)} %collective-permute-done.4.taken_ref, f32[256,128]{1,0:T(8,128)S(1)} %bitcast.15, bf16[256,256]{1,0:T(8,128)(2,1)S(1)} %get-tuple-element.17.lat_weight_ref, ...), custom_call_target="tpu_custom_call" | custom-call | flops 268435456 | bytes 1048576 | tf_op jit(solution)/shard_map/pallas_call | solution.py:410
Async XLA Ops:
  21.6 7.7 %collective-permute-start.2 = (bf16[8,80,256]{2,1,0:T(8,128)(2,1)S(1)}, bf16[8,80,256]{2,1,0:T(8,128)(2,1)S(1)}, u32[]{:S(2)}, u32[]{:S(2)}) collective-permute-start(bf16[8,80,256]{2,1,0:T(8,128)(2,1)S(1)} %get-tuple-element.21.quarter_ref), channel_id=1, source_target_pairs={{0,32},{32,0},{64,96},{96,64},{128,160},{160,128},{192,224},{224,1... | collective-permute-start | bytes 983048 | tf_op jit(solution)/shard_map/ppermute | solution.py:474
  29.3 33.2 %collective-permute-start.3 = (bf16[8,160,256]{2,1,0:T(8,128)(2,1)S(1)}, bf16[8,160,256]{2,1,0:T(8,128)(2,1)S(1)}, u32[]{:S(2)}, u32[]{:S(2)}) collective-permute-start(bf16[8,160,256]{2,1,0:T(8,128)(2,1)S(1)} %shard_map.113.mine_ref), channel_id=1, source_target_pairs={{0,8},{8,0},{1,9},{9,1},{2,10},{10,2},{3,11},{11,3},{4,12},{12,4},... | collective-permute-start | bytes 1966088 | tf_op jit(solution)/shard_map/ppermute | solution.py:479
  32.1 28.5 %collective-permute-start = (bf16[8,96,256]{2,1,0:T(8,128)(2,1)S(1)}, bf16[8,96,256]{2,1,0:T(8,128)(2,1)S(1)}, u32[]{:S(2)}, u32[]{:S(2)}) collective-permute-start(bf16[8,96,256]{2,1,0:T(8,128)(2,1)S(1)} %get-tuple-element.15), channel_id=1, source_target_pairs={{0,2},{1,3},{2,0},{3,1},{4,6},{5,7},{6,4},{7,5},{8,10},{9,11},{10,... | collective-permute-start | bytes 1179656 | tf_op jit(solution)/shard_map/ppermute | solution.py:471
  32.4 28.3 %collective-permute-start.1 = (bf16[8,96,256]{2,1,0:T(8,128)(2,1)S(1)}, bf16[8,96,256]{2,1,0:T(8,128)(2,1)S(1)}, u32[]{:S(2)}, u32[]{:S(2)}) collective-permute-start(bf16[8,96,256]{2,1,0:T(8,128)(2,1)S(1)} %get-tuple-element.16), channel_id=1, source_target_pairs={{0,254},{1,255},{2,4},{3,5},{4,2},{5,3},{6,8},{7,9},{8,6},{9,7},{1... | collective-permute-start | bytes 1179656 | tf_op jit(solution)/shard_map/ppermute | solution.py:472
  62.5 21.3 %copy-start = (bf16[200,256]{1,0:T(8,128)(2,1)S(1)}, bf16[200,256]{1,0:T(8,128)(2,1)}, u32[]{:S(2)}) copy-start(bf16[200,256]{1,0:T(8,128)(2,1)} %query_ref.1) | copy-start | bytes 307204
  64.5 19.3 %collective-permute-start.4 = (f32[2,256,256]{2,1,0:T(8,128)S(1)}, f32[2,256,256]{2,1,0:T(8,128)S(1)}, u32[]{:S(2)}, u32[]{:S(2)}) collective-permute-start(f32[2,256,256]{2,1,0:T(8,128)S(1)} %get-tuple-element.23), channel_id=1, source_target_pairs={{0,1},{1,0},{2,3},{3,2},{4,5},{5,4},{6,7},{7,6},{8,9},{9,8},{10,11... | collective-permute-start | bytes 1572872 | tf_op jit(solution)/shard_map/ppermute | solution.py:495

commit v5 on v2

--- a/solution.py
+++ b/solution.py
@@ -25,7 +25,6 @@
 COARSE_EDGE = 80
 SIDE_ROWS = 96
 MASK_AT = 72
-XORS = (4, 1, 2, 5, 6, 3, 7)
 SHARD_ROWS = 80
 
 
@@ -90,8 +89,9 @@
 
 
 def pack_own_kernel(fine_hbm, coarse_hbm, weight_hbm, *refs):
-    vec_hbm, own_hbm = refs[:5], refs[5]
-    fine_ref, coarse_ref, weight_ref, vec_ref, own_ref, rows, coarse, sems, out_sems = refs[6:]
+    vec_hbm, own_refs = refs[:5], refs[5:13]
+    fine_ref, coarse_ref, weight_ref, vec_ref, rows, coarse, sems = refs[13:]
+    chan = lax.axis_index("chan_0") * 2 + lax.axis_index("chan_1")
     pairs = [(coarse_hbm, coarse_ref), (weight_hbm, weight_ref)]
     pairs += [(vec, vec_ref.at[i]) for i, vec in enumerate(vec_hbm)] + [(fine_hbm, fine_ref)]
     copies = [
@@ -106,7 +106,7 @@
         for t in range(2):
             piece = coarse_ref[n, :, :, 128 * t : 128 * t + 128].astype(F32)
             piece = jnp.concatenate([piece, jnp.zeros_like(piece)], axis=1)
-            coarse[n, t] = piece.reshape(256, 128)
+            coarse[n, t, 0:256] = piece.reshape(256, 128)
     lane = lanes_of((32, 128))
     vec_lane = lanes_of((32, 32))
     vec_row = lax.broadcasted_iota(jnp.int32, (32, 32), 0)
@@ -117,48 +117,43 @@
         second += jnp.where(lane == VECTORS + i, jnp.sum(vec, axis=1, keepdims=True), 0.0)
     first = weight[:, 0:128].astype(BF16)
     tails = []
-    for h in range(2):
-        for q in range(4):
-            d = 2 * q + h
-            tail = second
-            own_ref[d, 48:64, 0:128] = first[0:16]
-            own_ref[d, 48:64, 256:384] = first[16:32]
-            for n in range(2):
-                row = coarse[n, h, pl.ds(q, 32, stride=8), :].astype(BF16)
-                own_ref[d, 64:80, 128 * n : 128 * n + 128] = row[0:16]
-                own_ref[d, 64:80, 256 + 128 * n : 384 + 128 * n] = row[16:32]
-                row = coarse[n, 1 - h, pl.ds(q, 32, stride=8), :]
-                edge = row[:, 0:1] if h == 0 else row[:, 127:128]
-                tail = jnp.where(lane // 4 == COARSE_EDGE // 4 + n, edge, tail)
-            tails.append(tail)
+    for k in range(8):
+        own_ref = own_refs[k]
+        q, h = (chan ^ k) // 2, (chan ^ k) % 2
+        tail = second
+        own_ref[48:64, 0:128] = first[0:16]
+        own_ref[48:64, 256:384] = first[16:32]
+        for n in range(2):
+            row = coarse[n, h, pl.ds(q, 32, stride=8), :].astype(BF16)
+            own_ref[64:80, 128 * n : 128 * n + 128] = row[0:16]
+            own_ref[64:80, 256 + 128 * n : 384 + 128 * n] = row[16:32]
+            row = coarse[n, 1 - h, pl.ds(q, 32, stride=8), :]
+            edge = jnp.where(h == 0, row[:, 0:1], row[:, 127:128])
+            tail = jnp.where(lane // 4 == COARSE_EDGE // 4 + n, edge, tail)
+        tails.append(tail)
     copies[-1].wait()
     for t in range(4):
         piece = fine_ref[:, :, :, 128 * t : 128 * t + 128].astype(F32)
-        rows[t] = piece.reshape(48 * 8, 128)
-    out = []
-    for h in range(2):
-        for q in range(4):
-            d = 2 * q + h
-            tail = tails[4 * h + q]
-            for r in range(2):
-                for t in range(2):
-                    row = rows[2 * h + t, pl.ds(2 * q + r, 48, stride=8), :]
-                    at = 256 * r + 128 * t
-                    own_ref[d, 0:48, at : at + 128] = row.astype(BF16)
-                row = rows[2 - h, pl.ds(2 * q + r, 48, stride=8), :]
-                edge = row[:, 0:1] if h == 0 else row[:, 127:128]
-                for n in range(2):
-                    column = jnp.concatenate(
-                        [edge[24 * n : 24 * n + 24], jnp.zeros((8, 1), F32)], axis=0
-                    )
-                    tail = jnp.where(lane == FINE_EDGE + 4 * n + 1 + r, column, tail)
-            tail = tail.astype(BF16)
-            own_ref[d, 48:64, 128:256] = tail[0:16]
-            own_ref[d, 48:64, 384:512] = tail[16:32]
-            out.append(pltpu.make_async_copy(own_ref.at[d], own_hbm.at[d], out_sems.at[d]))
-            out[-1].start()
-    for copy in out:
-        copy.wait()
+        rows[t, 0:384] = piece.reshape(48 * 8, 128)
+    for k in range(8):
+        own_ref = own_refs[k]
+        q, h = (chan ^ k) // 2, (chan ^ k) % 2
+        tail = tails[k]
+        for r in range(2):
+            for t in range(2):
+                row = rows[2 * h + t, pl.ds(2 * q + r, 48, stride=8), :]
+                at = 256 * r + 128 * t
+                own_ref[0:48, at : at + 128] = row.astype(BF16)
+            row = rows[2 - h, pl.ds(2 * q + r, 48, stride=8), :]
+            edge = jnp.where(h == 0, row[:, 0:1], row[:, 127:128])
+            for n in range(2):
+                column = jnp.concatenate(
+                    [edge[24 * n : 24 * n + 24], jnp.zeros((8, 1), F32)], axis=0
+                )
+                tail = jnp.where(lane == FINE_EDGE + 4 * n + 1 + r, column, tail)
+        tail = tail.astype(BF16)
+        own_ref[48:64, 128:256] = tail[0:16]
+        own_ref[48:64, 384:512] = tail[16:32]
 
 
 def pack_weights_kernel(conv_ref, mask_ref, shard_ref):
@@ -172,14 +167,24 @@
         shard_ref[8 * k : 8 * k + 8] = piece
 
 
-def arrange_kernel(*refs):
+def line_kernel(shard_ref, one_ref, two_ref, three_ref, line_ref):
+    x = lax.axis_index("chan_0")
+    for k, ref in enumerate((shard_ref, one_ref, two_ref, three_ref)):
+        line_ref[x ^ k] = ref[...]
+
+
+def arrange_kernel(line_ref, partner_ref, all_ref):
+    side = lax.axis_index("chan_1")
+    for x in range(4):
+        all_ref[2 * x + side] = line_ref[x]
+        all_ref[2 * x + 1 - side] = partner_ref[x]
+
+
+def lateral_kernel(*refs):
+    own_ref, weight_ref, stats_ref, one_ref, two_ref = refs[8:]
     chan = lax.axis_index("chan_0") * 2 + lax.axis_index("chan_1")
-    all_ref = refs[-1]
-    for k, ref in enumerate(refs[:-1]):
-        all_ref[chan ^ k] = ref[...]
-
-
-def lateral_kernel(own_ref, weight_ref, stats_ref, one_ref, two_ref):
+    for k in range(8):
+        own_ref[chan ^ k] = refs[k][...]
     for s in range(8):
         for half in range(2):
             weight_ref[32 * s + 16 * half : 32 * s + 16 * half + 16, :] = own_ref[
@@ -439,36 +444,38 @@
     all_shape = jax.ShapeDtypeStruct((8, SHARD_ROWS, COLS), BF16)
     side_shape = jax.ShapeDtypeStruct((8, SIDE_ROWS, HALF), BF16)
     half_shape = jax.ShapeDtypeStruct((2, D, HALF), F32)
+    own_shape = jax.ShapeDtypeStruct((8, OWN_ROWS, COLS), BF16)
     swap = [(0, 1), (1, 0)]
 
     vectors = [v.reshape(1, 32) for v in (lat_gain, lat_shift, out_gain, out_shift, mask_bias)]
-    own_out = call(
+    blocks = call(
         pack_own_kernel,
-        jax.ShapeDtypeStruct((8, OWN_ROWS, COLS), BF16),
+        [pltpu.VMEM((OWN_ROWS, COLS), BF16)] * 8,
         (
             pltpu.VMEM((2, 24, 8, COLS), BF16),
             pltpu.VMEM((2, 32, 4, 256), BF16),
             pltpu.VMEM((32, IN_CH), BF16),
             pltpu.VMEM((5, 1, 32), BF16),
-            pltpu.VMEM((8, OWN_ROWS, COLS), BF16),
-            pltpu.VMEM((4, 48 * 8, 128), F32),
-            pltpu.VMEM((2, 2, 256, 128), F32),
-            pltpu.SemaphoreType.DMA((8,)),
+            pltpu.VMEM((4, 48 * 8 + 8, 128), F32),
+            pltpu.VMEM((2, 2, 256 + 8, 128), F32),
             pltpu.SemaphoreType.DMA((8,)),
         ),
         space=pltpu.HBM,
-        out_space=pltpu.HBM,
         limit=60 << 20,
     )(fine_features, coarse_level, lat_weight, *vectors)
-    own = lax.all_to_all(own_out, CHAN, 0, 0, tiled=True)
+    taken_in = [blocks[0]] + [
+        lax.ppermute(blocks[k], CHAN, [(i, i ^ k) for i in range(8)]) for k in range(1, 8)
+    ]
     shard = call(pack_weights_kernel, shard_shape)(out_weight, mask_weight)
-    moved = [lax.ppermute(shard, CHAN, [(i, i ^ k) for i in range(8)]) for k in XORS]
-
-    full_lat, stats, first, second = call(
+    moved = [
+        lax.ppermute(shard, "chan_0", [(i, i ^ k) for i in range(4)]) for k in (1, 2, 3)
+    ]
+
+    own, full_lat, stats, first, second = call(
         lateral_kernel,
-        [jax.ShapeDtypeStruct((D, 256), BF16), stats_shape, side_shape, side_shape],
+        [own_shape, jax.ShapeDtypeStruct((D, 256), BF16), stats_shape, side_shape, side_shape],
         flops=2 * 2 * 256 * 256 * 512,
-    )(own)
+    )(*taken_in)
     pairs = everyone // 2
     swap_at = lambda shift: [
         (2 * p + yl, 2 * ((((p + shift) % pairs ^ 1) - shift) % pairs) + yl)
@@ -477,11 +484,12 @@
     ]
     first = lax.ppermute(first, ALL, swap_at(0))
     second = lax.ppermute(second, ALL, swap_at(1))
+    line = call(line_kernel, jax.ShapeDtypeStruct((4, SHARD_ROWS, COLS), BF16))(shard, *moved)
+    partner = lax.ppermute(line, "chan_1", swap)
     stats = lax.all_to_all(stats, ALL, 0, 0, tiled=True)
     stats = call(combine_kernel, jax.ShapeDtypeStruct((8, 128), F32), flops=1 << 20)(stats)
 
-    by_xor = dict(zip(XORS, moved))
-    mine = call(arrange_kernel, all_shape)(shard, *[by_xor[k] for k in range(1, 8)])
+    mine = call(arrange_kernel, all_shape)(line, partner)
     other = lax.ppermute(mine, "band_2", swap)
     joined, beside = call(
         join_kernel,

time: 85.5 us -> 91.5 us (1.070)
  waiting for transfers between devices: 8.27 us -> 13.2 us
  local copies, waits for them, and re-layouts: 0.01 us -> 1.63 us
  starting transfers between devices: 22.5 us -> 21.2 us
    all_to_all x1 -> x0, starting transfers between devices: 5.86 us -> none  [per_device(): own = lax.all_to_all(own_out, CHAN, 0, 0, tiled=True)]
    ppermute x7 -> x11, waiting for transfers between devices: 8.25 us -> 13.2 us  [the longest x3 5.15 us: per_device(): lax.ppermute(shard, 'chan_0', [(i, i ^ k) for i in range(4)])]
    ppermute x1, starting transfers between devices: 1.08 us -> 3.63 us  [per_device(): other = lax.ppermute(mine, 'band_2', swap)]
    unnamed x6, local copies, waits for them, and re-layouts: 0.01 us -> 1.63 us
    ppermute x1, starting transfers between devices: 0.34 us -> 1.78 us  [per_device(): first = lax.ppermute(first, ALL, swap_at(0))]
    ppermute x7 -> x11, starting transfers between devices: 13.2 us -> 13.9 us  [the longest x7 9.36 us: per_device(): lax.ppermute(blocks[k], CHAN, [(i, i ^ k) for i in range(8)])]
    pallas_call x8 -> x9, Pallas kernels: 9.26 us -> 9.3 us  [call(): pl.pallas_call(kernel, out_shape=out_shape, in_specs=[pl.BlockSpec(memory...]
  transfers between devices with their start and end apart: 12 -> 15, of which waited for: 4 -> 6; matrix products, arithmetic and copies ran while one was open for 0% -> 0% of each run, Pallas kernels for 3% -> 5%
where the time goes in v5:
time: 91.5 us; the launch traced here: 91.2 us
  blocking collectives  45.8 us (50%)
  starting transfers between devices  21.2 us (23%)
  waiting for transfers between devices  13.2 us (14%)
  Pallas kernels  9.3 us (10%)
  local copies, waits for them, and re-layouts  1.63 us (2%)
    all_to_all x2, blocking collectives, per_device(): stats = lax.all_to_all(stats, ALL, 0, 0, tiled=True)  45.8 us
    ppermute x7, starting transfers between devices, per_device(): lax.ppermute(blocks[k], CHAN, [(i, i ^ k) for i in range(8)])  9.36 us
    pallas_call x9, Pallas kernels, call(): pl.pallas_call(kernel, out_shape=out_shape, in_specs=[pl.BlockSpec(memory...  9.3 us
    ppermute x3, waiting for transfers between devices, per_device(): lax.ppermute(shard, 'chan_0', [(i, i ^ k) for i in range(4)])  5.15 us
    ppermute x3, starting transfers between devices, per_device(): lax.ppermute(shard, 'chan_0', [(i, i ^ k) for i in range(4)])  4.42 us
    ppermute x1, waiting for transfers between devices, per_device(): partner = lax.ppermute(line, 'chan_1', swap)  4.22 us
    ppermute x7, waiting for transfers between devices, per_device(): lax.ppermute(blocks[k], CHAN, [(i, i ^ k) for i in range(8)])  3.83 us
    ppermute x1, starting transfers between devices, per_device(): other = lax.ppermute(mine, 'band_2', swap)  3.63 us
  transfers between devices with their start and end apart: 15, of which 6 were waited for; matrix products, arithmetic and copies ran while one was open for 0% of the time, Pallas kernels for 5%

profile of v5, /device:TPU:1, one launch (start us, length us, event | category | flops | bytes accessed | tf_op | source)
XLA Modules:
  0.0 91.2 jit_solution(2290077573693405409)
XLA Ops:
  0.0 0.0 copy-start
  0.0 0.9 copy-done
  0.9 0.0 copy-start.2
  0.9 0.7 copy-done.2
  1.6 3.6 %collective-permute-start.10 = (bf16[80,512]{1,0:T(8,128)(2,1)S(1)}, bf16[80,512]{1,0:T(8,128)(2,1)S(1)}, u32[]{:S(2)}, u32[]{:S(2)}) collective-permute-start(bf16[80,512]{1,0:T(8,128)(2,1)S(1)} %shard_map.113.shard_ref), channel_id=1, source_target_pairs={{0,4},{2,6},{4,0},{6,2},{1,5},{3,7},{5,1},{7,3},{8,12},{10,14},{12... | collective-permute-start | bytes 245768 | tf_op jit(solution)/shard_map/ppermute | solution.py:471
  5.2 0.9 collective-permute-start.11
  6.1 0.0 collective-permute-start.9
  6.1 1.0 %collective-permute-done.10.two_ref = bf16[80,512]{1,0:T(8,128)(2,1)S(1)} collective-permute-done((bf16[80,512]{1,0:T(8,128)(2,1)S(1)}, bf16[80,512]{1,0:T(8,128)(2,1)S(1)}, u32[]{:S(2)}, u32[]{:S(2)}) %collective-permute-start.10) | collective-permute-done | bytes 81952 | tf_op jit(solution)/shard_map/ppermute | solution.py:471
  7.0 4.2 %collective-permute-done.11.three_ref = bf16[80,512]{1,0:T(8,128)(2,1)S(1)} collective-permute-done((bf16[80,512]{1,0:T(8,128)(2,1)S(1)}, bf16[80,512]{1,0:T(8,128)(2,1)S(1)}, u32[]{:S(2)}, u32[]{:S(2)}) %collective-permute-start.11) | collective-permute-done | bytes 81952 | tf_op jit(solution)/shard_map/ppermute | solution.py:471
  11.2 0.0 collective-permute-done.9.one_ref
  11.3 0.1 collective-permute-start.12
  11.4 2.2 %shard_map.109 = (bf16[80,512]{1,0:T(8,128)(2,1)S(1)}, bf16[80,512]{1,0:T(8,128)(2,1)S(1)}, bf16[80,512]{1,0:T(8,128)(2,1)S(1)}, bf16[80,512]{1,0:T(8,128)(2,1)S...) custom-call(bf16[2,24,8,512]{3,2,1,0:T(8,128)(2,1)} %fine_hbm.1, ...), custom_call_target="tpu_custom_call" | custom-call | bytes 1048576 | tf_op jit(solution)/shard_map/pallas_call | solution.py:417
  13.5 1.5 %collective-permute-start = (bf16[80,512]{1,0:T(8,128)(2,1)S(1)}, bf16[80,512]{1,0:T(8,128)(2,1)S(1)}, u32[]{:S(2)}, u32[]{:S(2)}) collective-permute-start(bf16[80,512]{1,0:T(8,128)(2,1)S(1)} %get-tuple-element.24), channel_id=1, source_target_pairs={{0,1},{1,0},{2,3},{3,2},{4,5},{5,4},{6,7},{7,6},{8,9},{9,8},{10,11... | collective-permute-start | bytes 245768 | tf_op jit(solution)/shard_map/ppermute | solution.py:467
  15.1 0.0 collective-permute-start.1
  15.1 1.3 %collective-permute-start.2 = (bf16[80,512]{1,0:T(8,128)(2,1)S(1)}, bf16[80,512]{1,0:T(8,128)(2,1)S(1)}, u32[]{:S(2)}, u32[]{:S(2)}) collective-permute-start(bf16[80,512]{1,0:T(8,128)(2,1)S(1)} %get-tuple-element.26), channel_id=1, source_target_pairs={{0,3},{1,2},{2,1},{3,0},{4,7},{5,6},{6,5},{7,4},{8,11},{9,10},{10,... | collective-permute-start | bytes 245768 | tf_op jit(solution)/shard_map/ppermute | solution.py:467
  16.3 4.2 %collective-permute-done.12.partner_ref = bf16[4,80,512]{2,1,0:T(8,128)(2,1)S(1)} collective-permute-done((bf16[4,80,512]{2,1,0:T(8,128)(2,1)S(1)}, bf16[4,80,512]{2,1,0:T(8,128)(2,1)S(1)}, u32[]{:S(2)}, u32[]{:S(2)}) %collective-permute-start.12) | collective-permute-done | bytes 327712 | tf_op jit(solution)/shard_map/ppermute | solution.py:488
  20.6 0.1 shard_map.115.mine_ref
  20.6 3.6 %collective-permute-start.13 = (bf16[8,80,512]{2,1,0:T(8,128)(2,1)S(1)}, bf16[8,80,512]{2,1,0:T(8,128)(2,1)S(1)}, u32[]{:S(2)}, u32[]{:S(2)}) collective-permute-start(bf16[8,80,512]{2,1,0:T(8,128)(2,1)S(1)} %shard_map.115.mine_ref), channel_id=1, source_target_pairs={{0,8},{8,0},{1,9},{9,1},{2,10},{10,2},{3,11},{11,3},{4,12},{12,4},... | collective-permute-start | bytes 1966088 | tf_op jit(solution)/shard_map/ppermute | solution.py:493
  24.2 0.0 collective-permute-start.3
  24.2 0.0 collective-permute-done.refs_1_
  24.3 2.7 %collective-permute-start.4 = (bf16[80,512]{1,0:T(8,128)(2,1)S(1)}, bf16[80,512]{1,0:T(8,128)(2,1)S(1)}, u32[]{:S(2)}, u32[]{:S(2)}) collective-permute-start(bf16[80,512]{1,0:T(8,128)(2,1)S(1)} %get-tuple-element.28), channel_id=1, source_target_pairs={{0,5},{1,4},{2,7},{3,6},{4,1},{5,0},{6,3},{7,2},{8,13},{9,12},{10,... | collective-permute-start | bytes 245768 | tf_op jit(solution)/shard_map/ppermute | solution.py:467
  26.9 0.0 collective-permute-done.1.refs_2_
  26.9 2.2 %collective-permute-start.5 = (bf16[80,512]{1,0:T(8,128)(2,1)S(1)}, bf16[80,512]{1,0:T(8,128)(2,1)S(1)}, u32[]{:S(2)}, u32[]{:S(2)}) collective-permute-start(bf16[80,512]{1,0:T(8,128)(2,1)S(1)} %get-tuple-element.29), channel_id=1, source_target_pairs={{0,6},{1,7},{2,4},{3,5},{4,2},{5,3},{6,0},{7,1},{8,14},{9,15},{10,... | collective-permute-start | bytes 245768 | tf_op jit(solution)/shard_map/ppermute | solution.py:467
  29.2 0.0 collective-permute-done.2.refs_3_
  29.2 1.6 %collective-permute-start.6 = (bf16[80,512]{1,0:T(8,128)(2,1)S(1)}, bf16[80,512]{1,0:T(8,128)(2,1)S(1)}, u32[]{:S(2)}, u32[]{:S(2)}) collective-permute-start(bf16[80,512]{1,0:T(8,128)(2,1)S(1)} %get-tuple-element.30), channel_id=1, source_target_pairs={{0,7},{1,6},{2,5},{3,4},{4,3},{5,2},{6,1},{7,0},{8,15},{9,14},{10,... | collective-permute-start | bytes 245768 | tf_op jit(solution)/shard_map/ppermute | solution.py:467
  30.8 0.0 collective-permute-done.3.refs_4_
  30.8 0.3 collective-permute-done.4.refs_5_
  31.1 2.6 %collective-permute-done.5.refs_6_ = bf16[80,512]{1,0:T(8,128)(2,1)S(1)} collective-permute-done((bf16[80,512]{1,0:T(8,128)(2,1)S(1)}, bf16[80,512]{1,0:T(8,128)(2,1)S(1)}, u32[]{:S(2)}, u32[]{:S(2)}) %collective-permute-start.5) | collective-permute-done | bytes 81952 | tf_op jit(solution)/shard_map/ppermute | solution.py:467
  33.6 1.0 %collective-permute-done.6.refs_7_ = bf16[80,512]{1,0:T(8,128)(2,1)S(1)} collective-permute-done((bf16[80,512]{1,0:T(8,128)(2,1)S(1)}, bf16[80,512]{1,0:T(8,128)(2,1)S(1)}, u32[]{:S(2)}, u32[]{:S(2)}) %collective-permute-start.6) | collective-permute-done | bytes 81952 | tf_op jit(solution)/shard_map/ppermute | solution.py:467
  34.6 0.6 shard_map.110
  35.3 1.8 %collective-permute-start.7 = (bf16[8,96,256]{2,1,0:T(8,128)(2,1)S(1)}, bf16[8,96,256]{2,1,0:T(8,128)(2,1)S(1)}, u32[]{:S(2)}, u32[]{:S(2)}) collective-permute-start(bf16[8,96,256]{2,1,0:T(8,128)(2,1)S(1)} %get-tuple-element.32), channel_id=1, source_target_pairs={{0,2},{1,3},{2,0},{3,1},{4,6},{5,7},{6,4},{7,5},{8,10},{9,11},{10,... | collective-permute-start | bytes 1179656 | tf_op jit(solution)/shard_map/ppermute | solution.py:485
  37.0 1.5 %collective-permute-start.8 = (bf16[8,96,256]{2,1,0:T(8,128)(2,1)S(1)}, bf16[8,96,256]{2,1,0:T(8,128)(2,1)S(1)}, u32[]{:S(2)}, u32[]{:S(2)}) collective-permute-start(bf16[8,96,256]{2,1,0:T(8,128)(2,1)S(1)} %get-tuple-element.33), channel_id=1, source_target_pairs={{0,254},{1,255},{2,4},{3,5},{4,2},{5,3},{6,8},{7,9},{8,6},{9,7},{1... | collective-permute-start | bytes 1179656 | tf_op jit(solution)/shard_map/ppermute | solution.py:486
  38.6 26.9 %all_to_all.22 = f32[256,1,128]{2,1,0:T(1,128)S(1)} all-to-all(f32[256,1,128]{2,1,0:T(1,128)S(1)} %bitcast.16), channel_id=1, replica_groups=mesh['band_0'=8,'band_1'=2,'band_2'=2,'chan_0'=4,'chan_1'=2] {'band_0','..., dimensions={0} | all-to-all | bytes 262144 | tf_op jit(solution)/shard_map/all_to_all | solution.py:489
  65.5 0.1 shard_map.111.lat_stats_ref
  65.5 0.0 collective-permute-done.7.one_ref
  65.6 0.0 collective-permute-done.8.two_ref
  65.6 1.8 %shard_map.112 = (bf16[2,768,512]{2,1,0:T(8,128)(2,1)S(1)}, bf16[768,128]{1,0:T(8,128)(2,1)S(1)}) custom-call(bf16[8,80,512]{2,1,0:T(8,128)(2,1)S(1)} %get-tuple-element.31.own_ref, bf16[8,96,256]{2,1,0:T(8,128)(2,1)S(1)} %collective-permute-done.7.one_ref, bf16[8,96,256]{2,1,0:T(8,128)(2,1)S(1)} %collective-permute-done.8.two_ref, ...), custom_call_target="tpu_custom_call" | custom-call | flops 939524096 | bytes 1048576 | tf_op jit(solution)/shard_map/pallas_call | solution.py:417
  67.4 0.0 collective-permute-done.13.other_ref
  67.4 0.0 copy-start.1
  67.4 2.0 %shard_map.116 = (f32[2,256,256]{2,1,0:T(8,128)S(1)}, f32[2,256,256]{2,1,0:T(8,128)S(1)}, f32[256,128]{1,0:T(8,128)S(1)}) custom-call(bf16[2,768,512]{2,1,0:T(8,128)(2,1)S(1)} %get-tuple-element.36.joined_ref, bf16[768,128]{1,0:T(8,128)(2,1)S(1)} %get-tuple-element.37.beside_ref, bf16[8,80,512]{2,1,0:T(8,128)(2,1)S(1)} %shard_map.115.mine_ref, ...), custom_call_target="tpu_custom_call" | custom-call | flops 1207959552 | bytes 1048576 | tf_op jit(solution)/shard_map/pallas_call | solution.py:417
  69.5 0.4 collective-permute-start.14
  69.9 18.9 %all_to_all.23 = f32[256,1,128]{2,1,0:T(1,128)S(1)} all-to-all(f32[256,1,128]{2,1,0:T(1,128)S(1)} %bitcast.17), channel_id=1, replica_groups=mesh['band_0'=8,'band_1'=2,'band_2'=2,'chan_0'=4,'chan_1'=2] {'band_0','..., dimensions={0} | all-to-all | bytes 262144 | tf_op jit(solution)/shard_map/all_to_all | solution.py:510
  88.8 0.0 collective-permute-done.14.taken_ref
  88.8 0.0 copy-done.1
  88.8 2.5 %shard_map.117 = f32[1600,128]{1,0:T(8,128)} custom-call(f32[2,256,256]{2,1,0:T(8,128)S(1)} %get-tuple-element.38.keep_ref, f32[2,256,256]{2,1,0:T(8,128)S(1)} %collective-permute-done.14.taken_ref, f32[256,128]{1,0:T(8,128)S(1)} %bitcast.14, bf16[256,256]{1,0:T(8,128)(2,1)S(1)} %get-tuple-element.34.lat_weight_ref, ...), custom_call_target="tpu_custom_call" | custom-call | flops 268435456 | bytes 1048576 | tf_op jit(solution)/shard_map/pallas_call | solution.py:417
  (2 shorter events, 0.0 us)
Async XLA Ops:
  0.0 0.9 copy-start
  0.9 0.7 copy-start.2
  1.6 5.4 %collective-permute-start.10 = (bf16[80,512]{1,0:T(8,128)(2,1)S(1)}, bf16[80,512]{1,0:T(8,128)(2,1)S(1)}, u32[]{:S(2)}, u32[]{:S(2)}) collective-permute-start(bf16[80,512]{1,0:T(8,128)(2,1)S(1)} %shard_map.113.shard_ref), channel_id=1, source_target_pairs={{0,4},{2,6},{4,0},{6,2},{1,5},{3,7},{5,1},{7,3},{8,12},{10,14},{12... | collective-permute-start | bytes 245768 | tf_op jit(solution)/shard_map/ppermute | solution.py:471
  5.2 6.0 %collective-permute-start.11 = (bf16[80,512]{1,0:T(8,128)(2,1)S(1)}, bf16[80,512]{1,0:T(8,128)(2,1)S(1)}, u32[]{:S(2)}, u32[]{:S(2)}) collective-permute-start(bf16[80,512]{1,0:T(8,128)(2,1)S(1)} %shard_map.113.shard_ref), channel_id=1, source_target_pairs={{0,6},{2,4},{4,2},{6,0},{1,7},{3,5},{5,3},{7,1},{8,14},{10,12},{12... | collective-permute-start | bytes 245768 | tf_op jit(solution)/shard_map/ppermute | solution.py:471
  6.1 5.2 %collective-permute-start.9 = (bf16[80,512]{1,0:T(8,128)(2,1)S(1)}, bf16[80,512]{1,0:T(8,128)(2,1)S(1)}, u32[]{:S(2)}, u32[]{:S(2)}) collective-permute-start(bf16[80,512]{1,0:T(8,128)(2,1)S(1)} %shard_map.113.shard_ref), channel_id=1, source_target_pairs={{0,2},{2,0},{4,6},{6,4},{1,3},{3,1},{5,7},{7,5},{8,10},{10,8},{12,... | collective-permute-start | bytes 245768 | tf_op jit(solution)/shard_map/ppermute | solution.py:471
  11.3 9.3 %collective-permute-start.12 = (bf16[4,80,512]{2,1,0:T(8,128)(2,1)S(1)}, bf16[4,80,512]{2,1,0:T(8,128)(2,1)S(1)}, u32[]{:S(2)}, u32[]{:S(2)}) collective-permute-start(bf16[4,80,512]{2,1,0:T(8,128)(2,1)S(1)} %shard_map.114.line_ref), channel_id=1, source_target_pairs={{0,1},{1,0},{2,3},{3,2},{4,5},{5,4},{6,7},{7,6},{8,9},{9,8},{10,11... | collective-permute-start | bytes 983048 | tf_op jit(solution)/shard_map/ppermute | solution.py:488
  13.5 10.7 %collective-permute-start = (bf16[80,512]{1,0:T(8,128)(2,1)S(1)}, bf16[80,512]{1,0:T(8,128)(2,1)S(1)}, u32[]{:S(2)}, u32[]{:S(2)}) collective-permute-start(bf16[80,512]{1,0:T(8,128)(2,1)S(1)} %get-tuple-element.24), channel_id=1, source_target_pairs={{0,1},{1,0},{2,3},{3,2},{4,5},{5,4},{6,7},{7,6},{8,9},{9,8},{10,11... | collective-permute-start | bytes 245768 | tf_op jit(solution)/shard_map/ppermute | solution.py:467
  15.1 11.9 %collective-permute-start.1 = (bf16[80,512]{1,0:T(8,128)(2,1)S(1)}, bf16[80,512]{1,0:T(8,128)(2,1)S(1)}, u32[]{:S(2)}, u32[]{:S(2)}) collective-permute-start(bf16[80,512]{1,0:T(8,128)(2,1)S(1)} %get-tuple-element.25), channel_id=1, source_target_pairs={{0,2},{1,3},{2,0},{3,1},{4,6},{5,7},{6,4},{7,5},{8,10},{9,11},{10,... | collective-permute-start | bytes 245768 | tf_op jit(solution)/shard_map/ppermute | solution.py:467
  15.1 14.1 %collective-permute-start.2 = (bf16[80,512]{1,0:T(8,128)(2,1)S(1)}, bf16[80,512]{1,0:T(8,128)(2,1)S(1)}, u32[]{:S(2)}, u32[]{:S(2)}) collective-permute-start(bf16[80,512]{1,0:T(8,128)(2,1)S(1)} %get-tuple-element.26), channel_id=1, source_target_pairs={{0,3},{1,2},{2,1},{3,0},{4,7},{5,6},{6,5},{7,4},{8,11},{9,10},{10,... | collective-permute-start | bytes 245768 | tf_op jit(solution)/shard_map/ppermute | solution.py:467
  20.6 46.8 %collective-permute-start.13 = (bf16[8,80,512]{2,1,0:T(8,128)(2,1)S(1)}, bf16[8,80,512]{2,1,0:T(8,128)(2,1)S(1)}, u32[]{:S(2)}, u32[]{:S(2)}) collective-permute-start(bf16[8,80,512]{2,1,0:T(8,128)(2,1)S(1)} %shard_map.115.mine_ref), channel_id=1, source_target_pairs={{0,8},{8,0},{1,9},{9,1},{2,10},{10,2},{3,11},{11,3},{4,12},{12,4},... | collective-permute-start | bytes 1966088 | tf_op jit(solution)/shard_map/ppermute | solution.py:493
  24.2 6.6 %collective-permute-start.3 = (bf16[80,512]{1,0:T(8,128)(2,1)S(1)}, bf16[80,512]{1,0:T(8,128)(2,1)S(1)}, u32[]{:S(2)}, u32[]{:S(2)}) collective-permute-start(bf16[80,512]{1,0:T(8,128)(2,1)S(1)} %get-tuple-element.27), channel_id=1, source_target_pairs={{0,4},{1,5},{2,6},{3,7},{4,0},{5,1},{6,2},{7,3},{8,12},{9,13},{10,... | collective-permute-start | bytes 245768 | tf_op jit(solution)/shard_map/ppermute | solution.py:467
  24.3 6.8 %collective-permute-start.4 = (bf16[80,512]{1,0:T(8,128)(2,1)S(1)}, bf16[80,512]{1,0:T(8,128)(2,1)S(1)}, u32[]{:S(2)}, u32[]{:S(2)}) collective-permute-start(bf16[80,512]{1,0:T(8,128)(2,1)S(1)} %get-tuple-element.28), channel_id=1, source_target_pairs={{0,5},{1,4},{2,7},{3,6},{4,1},{5,0},{6,3},{7,2},{8,13},{9,12},{10,... | collective-permute-start | bytes 245768 | tf_op jit(solution)/shard_map/ppermute | solution.py:467
  26.9 6.7 %collective-permute-start.5 = (bf16[80,512]{1,0:T(8,128)(2,1)S(1)}, bf16[80,512]{1,0:T(8,128)(2,1)S(1)}, u32[]{:S(2)}, u32[]{:S(2)}) collective-permute-start(bf16[80,512]{1,0:T(8,128)(2,1)S(1)} %get-tuple-element.29), channel_id=1, source_target_pairs={{0,6},{1,7},{2,4},{3,5},{4,2},{5,3},{6,0},{7,1},{8,14},{9,15},{10,... | collective-permute-start | bytes 245768 | tf_op jit(solution)/shard_map/ppermute | solution.py:467
  29.2 5.4 %collective-permute-start.6 = (bf16[80,512]{1,0:T(8,128)(2,1)S(1)}, bf16[80,512]{1,0:T(8,128)(2,1)S(1)}, u32[]{:S(2)}, u32[]{:S(2)}) collective-permute-start(bf16[80,512]{1,0:T(8,128)(2,1)S(1)} %get-tuple-element.30), channel_id=1, source_target_pairs={{0,7},{1,6},{2,5},{3,4},{4,3},{5,2},{6,1},{7,0},{8,15},{9,14},{10,... | collective-permute-start | bytes 245768 | tf_op jit(solution)/shard_map/ppermute | solution.py:467
  35.3 30.3 %collective-permute-start.7 = (bf16[8,96,256]{2,1,0:T(8,128)(2,1)S(1)}, bf16[8,96,256]{2,1,0:T(8,128)(2,1)S(1)}, u32[]{:S(2)}, u32[]{:S(2)}) collective-permute-start(bf16[8,96,256]{2,1,0:T(8,128)(2,1)S(1)} %get-tuple-element.32), channel_id=1, source_target_pairs={{0,2},{1,3},{2,0},{3,1},{4,6},{5,7},{6,4},{7,5},{8,10},{9,11},{10,... | collective-permute-start | bytes 1179656 | tf_op jit(solution)/shard_map/ppermute | solution.py:485
  37.0 28.5 %collective-permute-start.8 = (bf16[8,96,256]{2,1,0:T(8,128)(2,1)S(1)}, bf16[8,96,256]{2,1,0:T(8,128)(2,1)S(1)}, u32[]{:S(2)}, u32[]{:S(2)}) collective-permute-start(bf16[8,96,256]{2,1,0:T(8,128)(2,1)S(1)} %get-tuple-element.33), channel_id=1, source_target_pairs={{0,254},{1,255},{2,4},{3,5},{4,2},{5,3},{6,8},{7,9},{8,6},{9,7},{1... | collective-permute-start | bytes 1179656 | tf_op jit(solution)/shard_map/ppermute | solution.py:486
  67.4 21.3 %copy-start.1 = (bf16[200,256]{1,0:T(8,128)(2,1)S(1)}, bf16[200,256]{1,0:T(8,128)(2,1)}, u32[]{:S(2)}) copy-start(bf16[200,256]{1,0:T(8,128)(2,1)} %query_ref.1) | copy-start | bytes 307204
  69.5 19.3 %collective-permute-start.14 = (f32[2,256,256]{2,1,0:T(8,128)S(1)}, f32[2,256,256]{2,1,0:T(8,128)S(1)}, u32[]{:S(2)}, u32[]{:S(2)}) collective-permute-start(f32[2,256,256]{2,1,0:T(8,128)S(1)} %get-tuple-element.39), channel_id=1, source_target_pairs={{0,1},{1,0},{2,3},{3,2},{4,5},{5,4},{6,7},{7,6},{8,9},{9,8},{10,11... | collective-permute-start | bytes 1572872 | tf_op jit(solution)/shard_map/ppermute | solution.py:509

commit v6 on v5

--- a/solution.py
+++ b/solution.py
@@ -19,13 +19,13 @@
 EPS = 1e-05
 F32 = jnp.float32
 BF16 = jnp.bfloat16
-OWN_ROWS = 80
+OWN_ROWS = 120
 VECTORS = 64
 FINE_EDGE = 72
 COARSE_EDGE = 80
 SIDE_ROWS = 96
-MASK_AT = 72
-SHARD_ROWS = 80
+BLOCKS = 5
+MASK_AT = 144
 
 
 def dot(a, b):
@@ -88,12 +88,13 @@
     )
 
 
-def pack_own_kernel(fine_hbm, coarse_hbm, weight_hbm, *refs):
+def pack_own_kernel(fine_hbm, coarse_hbm, weight_hbm, conv_hbm, mask_hbm, *refs):
     vec_hbm, own_refs = refs[:5], refs[5:13]
-    fine_ref, coarse_ref, weight_ref, vec_ref, rows, coarse, sems = refs[13:]
+    fine_ref, coarse_ref, weight_ref, conv_ref, vec_ref, rows, coarse, sems = refs[13:]
     chan = lax.axis_index("chan_0") * 2 + lax.axis_index("chan_1")
     pairs = [(coarse_hbm, coarse_ref), (weight_hbm, weight_ref)]
-    pairs += [(vec, vec_ref.at[i]) for i, vec in enumerate(vec_hbm)] + [(fine_hbm, fine_ref)]
+    pairs += [(vec, vec_ref.at[i]) for i, vec in enumerate(vec_hbm)]
+    pairs += [(conv_hbm, conv_ref.at[pl.ds(0, 9)]), (mask_hbm, conv_ref.at[9]), (fine_hbm, fine_ref)]
     copies = [
         pltpu.make_async_copy(source, target, sems.at[i])
         for i, (source, target) in enumerate(pairs)
@@ -116,6 +117,11 @@
         vec = jnp.where(vec_lane == vec_row, vec_ref[i].astype(F32), 0.0)
         second += jnp.where(lane == VECTORS + i, jnp.sum(vec, axis=1, keepdims=True), 0.0)
     first = weight[:, 0:128].astype(BF16)
+    half = pl.multiple_of(16 * lax.axis_index("band_2"), 16)
+    block = BLOCKS * (lax.axis_index("band_0") % 2)
+    blocks = [conv_ref[block + i, pl.ds(half, 16), :] for i in range(BLOCKS)]
+    last = blocks[4].astype(F32)
+    last = jnp.concatenate([last[0:8], last[8:16]], axis=1).astype(BF16)
     tails = []
     for k in range(8):
         own_ref = own_refs[k]
@@ -123,6 +129,10 @@
         tail = second
         own_ref[48:64, 0:128] = first[0:16]
         own_ref[48:64, 256:384] = first[16:32]
+        for i in range(4):
+            at = 80 + 16 * (i // 2)
+            own_ref[at : at + 16, 256 * (i % 2) : 256 * (i % 2) + 256] = blocks[i]
+        own_ref[112:120, :] = last
         for n in range(2):
             row = coarse[n, h, pl.ds(q, 32, stride=8), :].astype(BF16)
             own_ref[64:80, 128 * n : 128 * n + 128] = row[0:16]
@@ -156,32 +166,15 @@
         own_ref[48:64, 384:512] = tail[16:32]
 
 
-def pack_weights_kernel(conv_ref, mask_ref, shard_ref):
-    half = pl.multiple_of(16 * lax.axis_index("band_2"), 16)
-    for k in range(10):
-        if k < 9:
-            piece = conv_ref[k // 3, k % 3, pl.ds(half, 16), :].astype(F32)
-        else:
-            piece = mask_ref[pl.ds(half, 16), :].astype(F32)
-        piece = jnp.concatenate([piece[0:8], piece[8:16]], axis=1).astype(BF16)
-        shard_ref[8 * k : 8 * k + 8] = piece
-
-
-def line_kernel(shard_ref, one_ref, two_ref, three_ref, line_ref):
-    x = lax.axis_index("chan_0")
-    for k, ref in enumerate((shard_ref, one_ref, two_ref, three_ref)):
-        line_ref[x ^ k] = ref[...]
-
-
-def arrange_kernel(line_ref, partner_ref, all_ref):
-    side = lax.axis_index("chan_1")
-    for x in range(4):
-        all_ref[2 * x + side] = line_ref[x]
-        all_ref[2 * x + 1 - side] = partner_ref[x]
+def arrange_kernel(quarter_ref, other_ref, all_ref):
+    parity = lax.axis_index("band_0") % 2
+    rows = 16 * BLOCKS
+    all_ref[:, pl.ds(pl.multiple_of(rows * parity, 16), rows), :] = quarter_ref[...]
+    all_ref[:, pl.ds(pl.multiple_of(rows - rows * parity, 16), rows), :] = other_ref[...]
 
 
 def lateral_kernel(*refs):
-    own_ref, weight_ref, stats_ref, one_ref, two_ref = refs[8:]
+    own_ref, weight_ref, stats_ref, one_ref, two_ref, quarter_ref = refs[8:]
     chan = lax.axis_index("chan_0") * 2 + lax.axis_index("chan_1")
     for k in range(8):
         own_ref[chan ^ k] = refs[k][...]
@@ -190,6 +183,14 @@
             weight_ref[32 * s + 16 * half : 32 * s + 16 * half + 16, :] = own_ref[
                 s, 48:64, 256 * half : 256 * half + 256
             ]
+    for s in range(8):
+        for i in range(4):
+            at = 80 + 16 * (i // 2)
+            quarter_ref[s, 16 * i : 16 * i + 16] = own_ref[
+                s, at : at + 16, 256 * (i % 2) : 256 * (i % 2) + 256
+            ]
+        last = own_ref[s, 112:120, :]
+        quarter_ref[s, 64:80] = jnp.concatenate([last[:, 0:256], last[:, 256:512]], axis=0)
     odd = lax.axis_index("chan_0") % 2
     for ref, row in ((one_ref, 1 - odd), (two_ref, odd)):
         at = pl.multiple_of(256 * row, 256)
@@ -355,9 +356,8 @@
             at = pl.multiple_of(32 * s + 16 * part, 16)
             for a in range(3):
                 for b in range(3):
-                    piece = ref[s, (a * 3 + b) * 8 : (a * 3 + b) * 8 + 8, :]
-                    both = jnp.concatenate([piece[:, 0:256], piece[:, 256:512]], axis=0)
-                    weight[b, pl.ds(at, 16), 256 * a : 256 * a + 256] = both
+                    block = ref[s, 16 * (3 * a + b) : 16 * (3 * a + b) + 16, :]
+                    weight[b, pl.ds(at, 16), 256 * a : 256 * a + 256] = block
     inner_edge = jnp.where(side == 0, HALF - 1, 0)
     lane = lax.broadcasted_iota(jnp.int32, (GROUPS, 1, 128), 2)
     lane_at = lanes_of((D, HALF))
@@ -390,9 +390,7 @@
     for part, ref in ((core, mine_ref), (1 - core, other_ref)):
         for s in range(8):
             at = pl.multiple_of(32 * s + 16 * part, 16)
-            piece = ref[s, MASK_AT : MASK_AT + 8, :]
-            both = jnp.concatenate([piece[:, 0:256], piece[:, 256:512]], axis=0)
-            weight[pl.ds(at, 16), :] = both
+            weight[pl.ds(at, 16), :] = ref[s, MASK_AT : MASK_AT + 16, :]
     gain = vector_col(lat_weight_ref, 2)
     shift = vector_col(lat_weight_ref, 3)
     bias = vector_col(lat_weight_ref, 4)
@@ -440,8 +438,8 @@
 ):
     everyone = lax.axis_size(ALL)
     stats_shape = jax.ShapeDtypeStruct((everyone, 128), F32)
-    shard_shape = jax.ShapeDtypeStruct((SHARD_ROWS, COLS), BF16)
-    all_shape = jax.ShapeDtypeStruct((8, SHARD_ROWS, COLS), BF16)
+    quarter_shape = jax.ShapeDtypeStruct((8, 16 * BLOCKS, D), BF16)
+    all_shape = jax.ShapeDtypeStruct((8, 32 * BLOCKS, D), BF16)
     side_shape = jax.ShapeDtypeStruct((8, SIDE_ROWS, HALF), BF16)
     half_shape = jax.ShapeDtypeStruct((2, D, HALF), F32)
     own_shape = jax.ShapeDtypeStruct((8, OWN_ROWS, COLS), BF16)
@@ -455,25 +453,27 @@
             pltpu.VMEM((2, 24, 8, COLS), BF16),
             pltpu.VMEM((2, 32, 4, 256), BF16),
             pltpu.VMEM((32, IN_CH), BF16),
+            pltpu.VMEM((10, 32, D), BF16),
             pltpu.VMEM((5, 1, 32), BF16),
             pltpu.VMEM((4, 48 * 8 + 8, 128), F32),
             pltpu.VMEM((2, 2, 256 + 8, 128), F32),
-            pltpu.SemaphoreType.DMA((8,)),
+            pltpu.SemaphoreType.DMA((10,)),
         ),
         space=pltpu.HBM,
         limit=60 << 20,
-    )(fine_features, coarse_level, lat_weight, *vectors)
+    )(
+        fine_features, coarse_level, lat_weight, out_weight.reshape(9, 32, D), mask_weight, *vectors
+    )
     taken_in = [blocks[0]] + [
         lax.ppermute(blocks[k], CHAN, [(i, i ^ k) for i in range(8)]) for k in range(1, 8)
     ]
-    shard = call(pack_weights_kernel, shard_shape)(out_weight, mask_weight)
-    moved = [
-        lax.ppermute(shard, "chan_0", [(i, i ^ k) for i in range(4)]) for k in (1, 2, 3)
-    ]
-
-    own, full_lat, stats, first, second = call(
+
+    own, full_lat, stats, first, second, quarter = call(
         lateral_kernel,
-        [own_shape, jax.ShapeDtypeStruct((D, 256), BF16), stats_shape, side_shape, side_shape],
+        [
+            own_shape, jax.ShapeDtypeStruct((D, 256), BF16), stats_shape,
+            side_shape, side_shape, quarter_shape,
+        ],
         flops=2 * 2 * 256 * 256 * 512,
     )(*taken_in)
     pairs = everyone // 2
@@ -484,12 +484,12 @@
     ]
     first = lax.ppermute(first, ALL, swap_at(0))
     second = lax.ppermute(second, ALL, swap_at(1))
-    line = call(line_kernel, jax.ShapeDtypeStruct((4, SHARD_ROWS, COLS), BF16))(shard, *moved)
-    partner = lax.ppermute(line, "chan_1", swap)
+    depth = lax.axis_size("band_0")
+    other_quarter = lax.ppermute(quarter, "band_0", [(i, i ^ 1) for i in range(depth)])
     stats = lax.all_to_all(stats, ALL, 0, 0, tiled=True)
     stats = call(combine_kernel, jax.ShapeDtypeStruct((8, 128), F32), flops=1 << 20)(stats)
 
-    mine = call(arrange_kernel, all_shape)(line, partner)
+    mine = call(arrange_kernel, all_shape)(quarter, other_quarter)
     other = lax.ppermute(mine, "band_2", swap)
     joined, beside = call(
         join_kernel,

time: 91.5 us -> 88.5 us (0.967)
  starting transfers between devices: 21.2 us -> 17 us
  waiting for transfers between devices: 13.2 us -> 16.9 us
  local copies, waits for them, and re-layouts: 1.63 us -> 0.01 us
    ppermute x7, waiting for transfers between devices: 3.83 us -> 10.5 us  [per_device(): lax.ppermute(blocks[k], CHAN, [(i, i ^ k) for i in range(8)])]
    ppermute x4 -> x1, waiting for transfers between devices: 9.37 us -> 6.43 us  [per_device(): lax.ppermute(quarter, 'band_0', [(i, i ^ 1) for i in range(depth)])]
    ppermute x4 -> x1, starting transfers between devices: 4.52 us -> 1.79 us  [per_device(): lax.ppermute(quarter, 'band_0', [(i, i ^ 1) for i in range(depth)])]
    unnamed x6 -> x2, local copies, waits for them, and re-layouts: 1.63 us -> 0.01 us
    ppermute x1, starting transfers between devices: 1.78 us -> 0.22 us  [per_device(): first = lax.ppermute(first, ALL, swap_at(0))]
    ppermute x1, starting transfers between devices: 3.63 us -> 2.32 us  [per_device(): other = lax.ppermute(mine, 'band_2', swap)]
    pallas_call x9 -> x7, Pallas kernels: 9.3 us -> 9.39 us  [call(): pl.pallas_call(kernel, out_shape=out_shape, in_specs=[pl.BlockSpec(memory...]
  transfers between devices with their start and end apart: 15 -> 12, of which waited for: 6 -> 5; matrix products, arithmetic and copies ran while one was open for 0% -> 0% of each run, Pallas kernels for 5% -> 2%
where the time goes in v6:
time: 88.5 us; the launch traced here: 88.4 us
  blocking collectives  45 us (51%)
  starting transfers between devices  17 us (19%)
  waiting for transfers between devices  16.9 us (19%)
  Pallas kernels  9.39 us (11%)
    all_to_all x2, blocking collectives, per_device(): stats = lax.all_to_all(stats, ALL, 0, 0, tiled=True)  45 us
    ppermute x7, waiting for transfers between devices, per_device(): lax.ppermute(blocks[k], CHAN, [(i, i ^ k) for i in range(8)])  10.5 us
    ppermute x7, starting transfers between devices, per_device(): lax.ppermute(blocks[k], CHAN, [(i, i ^ k) for i in range(8)])  10 us
    pallas_call x7, Pallas kernels, call(): pl.pallas_call(kernel, out_shape=out_shape, in_specs=[pl.BlockSpec(memory...  9.39 us
    ppermute x1, waiting for transfers between devices, per_device(): lax.ppermute(quarter, 'band_0', [(i, i ^ 1) for i in range(depth)])  6.43 us
    ppermute x1, starting transfers between devices, per_device(): other = lax.ppermute(mine, 'band_2', swap)  2.32 us
    ppermute x1, starting transfers between devices, per_device(): second = lax.ppermute(second, ALL, swap_at(1))  2.24 us
    ppermute x1, starting transfers between devices, per_device(): lax.ppermute(quarter, 'band_0', [(i, i ^ 1) for i in range(depth)])  1.79 us
  transfers between devices with their start and end apart: 12, of which 5 were waited for; matrix products, arithmetic and copies ran while one was open for 0% of the time, Pallas kernels for 2%

profile of v6, /device:TPU:1, one launch (start us, length us, event | category | flops | bytes accessed | tf_op | source)
XLA Modules:
  0.0 88.4 jit_solution(14580127180600693480)
XLA Ops:
  0.0 2.3 %shard_map.109 = (bf16[120,512]{1,0:T(8,128)(2,1)S(1)}, bf16[120,512]{1,0:T(8,128)(2,1)S(1)}, bf16[120,512]{1,0:T(8,128)(2,1)S(1)}, bf16[120,512]{1,0:T(8,128)(2...) custom-call(bf16[2,24,8,512]{3,2,1,0:T(8,128)(2,1)} %fine_hbm.1, ...), custom_call_target="tpu_custom_call" | custom-call | bytes 1048576 | tf_op jit(solution)/shard_map/pallas_call | solution.py:415
  2.3 2.2 %collective-permute-start = (bf16[120,512]{1,0:T(8,128)(2,1)S(1)}, bf16[120,512]{1,0:T(8,128)(2,1)S(1)}, u32[]{:S(2)}, u32[]{:S(2)}) collective-permute-start(bf16[120,512]{1,0:T(8,128)(2,1)S(1)} %get-tuple-element.25), channel_id=1, source_target_pairs={{0,1},{1,0},{2,3},{3,2},{4,5},{5,4},{6,7},{7,6},{8,9},{9,8},{10,11... | collective-permute-start | bytes 368648 | tf_op jit(solution)/shard_map/ppermute | solution.py:468
  4.5 1.2 %collective-permute-start.1 = (bf16[120,512]{1,0:T(8,128)(2,1)S(1)}, bf16[120,512]{1,0:T(8,128)(2,1)S(1)}, u32[]{:S(2)}, u32[]{:S(2)}) collective-permute-start(bf16[120,512]{1,0:T(8,128)(2,1)S(1)} %get-tuple-element.26), channel_id=1, source_target_pairs={{0,2},{1,3},{2,0},{3,1},{4,6},{5,7},{6,4},{7,5},{8,10},{9,11},{10,... | collective-permute-start | bytes 368648 | tf_op jit(solution)/shard_map/ppermute | solution.py:468
  5.8 0.1 collective-permute-start.2
  5.8 2.8 %collective-permute-start.3 = (bf16[120,512]{1,0:T(8,128)(2,1)S(1)}, bf16[120,512]{1,0:T(8,128)(2,1)S(1)}, u32[]{:S(2)}, u32[]{:S(2)}) collective-permute-start(bf16[120,512]{1,0:T(8,128)(2,1)S(1)} %get-tuple-element.28), channel_id=1, source_target_pairs={{0,4},{1,5},{2,6},{3,7},{4,0},{5,1},{6,2},{7,3},{8,12},{9,13},{10,... | collective-permute-start | bytes 368648 | tf_op jit(solution)/shard_map/ppermute | solution.py:468
  8.6 1.2 %collective-permute-start.4 = (bf16[120,512]{1,0:T(8,128)(2,1)S(1)}, bf16[120,512]{1,0:T(8,128)(2,1)S(1)}, u32[]{:S(2)}, u32[]{:S(2)}) collective-permute-start(bf16[120,512]{1,0:T(8,128)(2,1)S(1)} %get-tuple-element.29), channel_id=1, source_target_pairs={{0,5},{1,4},{2,7},{3,6},{4,1},{5,0},{6,3},{7,2},{8,13},{9,12},{10,... | collective-permute-start | bytes 368648 | tf_op jit(solution)/shard_map/ppermute | solution.py:468
  9.9 0.0 collective-permute-done.refs_1_
  9.9 2.5 %collective-permute-start.5 = (bf16[120,512]{1,0:T(8,128)(2,1)S(1)}, bf16[120,512]{1,0:T(8,128)(2,1)S(1)}, u32[]{:S(2)}, u32[]{:S(2)}) collective-permute-start(bf16[120,512]{1,0:T(8,128)(2,1)S(1)} %get-tuple-element.30), channel_id=1, source_target_pairs={{0,6},{1,7},{2,4},{3,5},{4,2},{5,3},{6,0},{7,1},{8,14},{9,15},{10,... | collective-permute-start | bytes 368648 | tf_op jit(solution)/shard_map/ppermute | solution.py:468
  12.4 0.0 collective-permute-done.1.refs_2_
  12.4 0.0 collective-permute-start.6
  12.4 0.0 collective-permute-done.2.refs_3_
  12.4 3.3 %collective-permute-done.3.refs_4_ = bf16[120,512]{1,0:T(8,128)(2,1)S(1)} collective-permute-done((bf16[120,512]{1,0:T(8,128)(2,1)S(1)}, bf16[120,512]{1,0:T(8,128)(2,1)S(1)}, u32[]{:S(2)}, u32[]{:S(2)}) %collective-permute-start.3) | collective-permute-done | bytes 122912 | tf_op jit(solution)/shard_map/ppermute | solution.py:468
  15.6 3.2 %collective-permute-done.4.refs_5_ = bf16[120,512]{1,0:T(8,128)(2,1)S(1)} collective-permute-done((bf16[120,512]{1,0:T(8,128)(2,1)S(1)}, bf16[120,512]{1,0:T(8,128)(2,1)S(1)}, u32[]{:S(2)}, u32[]{:S(2)}) %collective-permute-start.4) | collective-permute-done | bytes 122912 | tf_op jit(solution)/shard_map/ppermute | solution.py:468
  18.8 1.4 %collective-permute-done.5.refs_6_ = bf16[120,512]{1,0:T(8,128)(2,1)S(1)} collective-permute-done((bf16[120,512]{1,0:T(8,128)(2,1)S(1)}, bf16[120,512]{1,0:T(8,128)(2,1)S(1)}, u32[]{:S(2)}, u32[]{:S(2)}) %collective-permute-start.5) | collective-permute-done | bytes 122912 | tf_op jit(solution)/shard_map/ppermute | solution.py:468
  20.2 2.7 %collective-permute-done.6.refs_7_ = bf16[120,512]{1,0:T(8,128)(2,1)S(1)} collective-permute-done((bf16[120,512]{1,0:T(8,128)(2,1)S(1)}, bf16[120,512]{1,0:T(8,128)(2,1)S(1)}, u32[]{:S(2)}, u32[]{:S(2)}) %collective-permute-start.6) | collective-permute-done | bytes 122912 | tf_op jit(solution)/shard_map/ppermute | solution.py:468
  22.9 0.7 shard_map.110
  23.6 1.8 %collective-permute-start.9 = (bf16[8,80,256]{2,1,0:T(8,128)(2,1)S(1)}, bf16[8,80,256]{2,1,0:T(8,128)(2,1)S(1)}, u32[]{:S(2)}, u32[]{:S(2)}) collective-permute-start(bf16[8,80,256]{2,1,0:T(8,128)(2,1)S(1)} %get-tuple-element.39.quarter_ref), channel_id=1, source_target_pairs={{0,32},{32,0},{64,96},{96,64},{128,160},{160,128},{192,224},{224,1... | collective-permute-start | bytes 983048 | tf_op jit(solution)/shard_map/ppermute | solution.py:488
  25.4 6.4 %collective-permute-done.9.other_ref = bf16[8,80,256]{2,1,0:T(8,128)(2,1)S(1)} collective-permute-done((bf16[8,80,256]{2,1,0:T(8,128)(2,1)S(1)}, bf16[8,80,256]{2,1,0:T(8,128)(2,1)S(1)}, u32[]{:S(2)}, u32[]{:S(2)}) %collective-permute-start.9) | collective-permute-done | bytes 327712 | tf_op jit(solution)/shard_map/ppermute | solution.py:488
  31.8 0.1 shard_map.113.mine_ref
  31.9 2.3 %collective-permute-start.10 = (bf16[8,160,256]{2,1,0:T(8,128)(2,1)S(1)}, bf16[8,160,256]{2,1,0:T(8,128)(2,1)S(1)}, u32[]{:S(2)}, u32[]{:S(2)}) collective-permute-start(bf16[8,160,256]{2,1,0:T(8,128)(2,1)S(1)} %shard_map.113.mine_ref), channel_id=1, source_target_pairs={{0,8},{8,0},{1,9},{9,1},{2,10},{10,2},{3,11},{11,3},{4,12},{12,4},... | collective-permute-start | bytes 1966088 | tf_op jit(solution)/shard_map/ppermute | solution.py:493
  34.2 0.2 collective-permute-start.7
  34.4 2.2 %collective-permute-start.8 = (bf16[8,96,256]{2,1,0:T(8,128)(2,1)S(1)}, bf16[8,96,256]{2,1,0:T(8,128)(2,1)S(1)}, u32[]{:S(2)}, u32[]{:S(2)}) collective-permute-start(bf16[8,96,256]{2,1,0:T(8,128)(2,1)S(1)} %get-tuple-element.34), channel_id=1, source_target_pairs={{0,254},{1,255},{2,4},{3,5},{4,2},{5,3},{6,8},{7,9},{8,6},{9,7},{1... | collective-permute-start | bytes 1179656 | tf_op jit(solution)/shard_map/ppermute | solution.py:486
  36.7 26.1 %all_to_all.22 = f32[256,1,128]{2,1,0:T(1,128)S(1)} all-to-all(f32[256,1,128]{2,1,0:T(1,128)S(1)} %bitcast.17), channel_id=1, replica_groups=mesh['band_0'=8,'band_1'=2,'band_2'=2,'chan_0'=4,'chan_1'=2] {'band_0','..., dimensions={0} | all-to-all | bytes 262144 | tf_op jit(solution)/shard_map/all_to_all | solution.py:489
  62.8 0.1 shard_map.111.lat_stats_ref
  62.8 0.0 collective-permute-done.7.one_ref
  62.8 0.0 collective-permute-done.8.two_ref
  62.9 1.8 %shard_map.112 = (bf16[2,768,512]{2,1,0:T(8,128)(2,1)S(1)}, bf16[768,128]{1,0:T(8,128)(2,1)S(1)}) custom-call(bf16[8,120,512]{2,1,0:T(8,128)(2,1)S(1)} %get-tuple-element.32.own_ref, bf16[8,96,256]{2,1,0:T(8,128)(2,1)S(1)} %collective-permute-done.7.one_ref, bf16[8,96,256]{2,1,0:T(8,128)(2,1)S(1)} %collective-permute-done.8.two_ref, ...), custom_call_target="tpu_custom_call" | custom-call | flops 939524096 | bytes 1048576 | tf_op jit(solution)/shard_map/pallas_call | solution.py:415
  64.7 0.0 collective-permute-done.10.other_ref
  64.7 0.0 copy-start
  64.7 2.0 %shard_map.114 = (f32[2,256,256]{2,1,0:T(8,128)S(1)}, f32[2,256,256]{2,1,0:T(8,128)S(1)}, f32[256,128]{1,0:T(8,128)S(1)}) custom-call(bf16[2,768,512]{2,1,0:T(8,128)(2,1)S(1)} %get-tuple-element.37.joined_ref, bf16[768,128]{1,0:T(8,128)(2,1)S(1)} %get-tuple-element.38.beside_ref, bf16[8,160,256]{2,1,0:T(8,128)(2,1)S(1)} %shard_map.113.mine_ref, ...), custom_call_target="tpu_custom_call" | custom-call | flops 1207959552 | bytes 1048576 | tf_op jit(solution)/shard_map/pallas_call | solution.py:415
  66.7 0.4 collective-permute-start.11
  67.1 18.9 %all_to_all.23 = f32[256,1,128]{2,1,0:T(1,128)S(1)} all-to-all(f32[256,1,128]{2,1,0:T(1,128)S(1)} %bitcast.18), channel_id=1, replica_groups=mesh['band_0'=8,'band_1'=2,'band_2'=2,'chan_0'=4,'chan_1'=2] {'band_0','..., dimensions={0} | all-to-all | bytes 262144 | tf_op jit(solution)/shard_map/all_to_all | solution.py:510
  85.9 0.0 collective-permute-done.11.taken_ref
  85.9 0.0 copy-done
  85.9 2.5 %shard_map.115 = f32[1600,128]{1,0:T(8,128)} custom-call(f32[2,256,256]{2,1,0:T(8,128)S(1)} %get-tuple-element.40.keep_ref, f32[2,256,256]{2,1,0:T(8,128)S(1)} %collective-permute-done.11.taken_ref, f32[256,128]{1,0:T(8,128)S(1)} %bitcast.15, bf16[256,256]{1,0:T(8,128)(2,1)S(1)} %get-tuple-element.35.lat_weight_ref, ...), custom_call_target="tpu_custom_call" | custom-call | flops 268435456 | bytes 1048576 | tf_op jit(solution)/shard_map/pallas_call | solution.py:415
Async XLA Ops:
  2.3 7.5 %collective-permute-start = (bf16[120,512]{1,0:T(8,128)(2,1)S(1)}, bf16[120,512]{1,0:T(8,128)(2,1)S(1)}, u32[]{:S(2)}, u32[]{:S(2)}) collective-permute-start(bf16[120,512]{1,0:T(8,128)(2,1)S(1)} %get-tuple-element.25), channel_id=1, source_target_pairs={{0,1},{1,0},{2,3},{3,2},{4,5},{5,4},{6,7},{7,6},{8,9},{9,8},{10,11... | collective-permute-start | bytes 368648 | tf_op jit(solution)/shard_map/ppermute | solution.py:468
  4.5 7.8 %collective-permute-start.1 = (bf16[120,512]{1,0:T(8,128)(2,1)S(1)}, bf16[120,512]{1,0:T(8,128)(2,1)S(1)}, u32[]{:S(2)}, u32[]{:S(2)}) collective-permute-start(bf16[120,512]{1,0:T(8,128)(2,1)S(1)} %get-tuple-element.26), channel_id=1, source_target_pairs={{0,2},{1,3},{2,0},{3,1},{4,6},{5,7},{6,4},{7,5},{8,10},{9,11},{10,... | collective-permute-start | bytes 368648 | tf_op jit(solution)/shard_map/ppermute | solution.py:468
  5.8 6.6 %collective-permute-start.2 = (bf16[120,512]{1,0:T(8,128)(2,1)S(1)}, bf16[120,512]{1,0:T(8,128)(2,1)S(1)}, u32[]{:S(2)}, u32[]{:S(2)}) collective-permute-start(bf16[120,512]{1,0:T(8,128)(2,1)S(1)} %get-tuple-element.27), channel_id=1, source_target_pairs={{0,3},{1,2},{2,1},{3,0},{4,7},{5,6},{6,5},{7,4},{8,11},{9,10},{10,... | collective-permute-start | bytes 368648 | tf_op jit(solution)/shard_map/ppermute | solution.py:468
  5.8 9.8 %collective-permute-start.3 = (bf16[120,512]{1,0:T(8,128)(2,1)S(1)}, bf16[120,512]{1,0:T(8,128)(2,1)S(1)}, u32[]{:S(2)}, u32[]{:S(2)}) collective-permute-start(bf16[120,512]{1,0:T(8,128)(2,1)S(1)} %get-tuple-element.28), channel_id=1, source_target_pairs={{0,4},{1,5},{2,6},{3,7},{4,0},{5,1},{6,2},{7,3},{8,12},{9,13},{10,... | collective-permute-start | bytes 368648 | tf_op jit(solution)/shard_map/ppermute | solution.py:468
  8.6 10.2 %collective-permute-start.4 = (bf16[120,512]{1,0:T(8,128)(2,1)S(1)}, bf16[120,512]{1,0:T(8,128)(2,1)S(1)}, u32[]{:S(2)}, u32[]{:S(2)}) collective-permute-start(bf16[120,512]{1,0:T(8,128)(2,1)S(1)} %get-tuple-element.29), channel_id=1, source_target_pairs={{0,5},{1,4},{2,7},{3,6},{4,1},{5,0},{6,3},{7,2},{8,13},{9,12},{10,... | collective-permute-start | bytes 368648 | tf_op jit(solution)/shard_map/ppermute | solution.py:468
  9.9 10.3 %collective-permute-start.5 = (bf16[120,512]{1,0:T(8,128)(2,1)S(1)}, bf16[120,512]{1,0:T(8,128)(2,1)S(1)}, u32[]{:S(2)}, u32[]{:S(2)}) collective-permute-start(bf16[120,512]{1,0:T(8,128)(2,1)S(1)} %get-tuple-element.30), channel_id=1, source_target_pairs={{0,6},{1,7},{2,4},{3,5},{4,2},{5,3},{6,0},{7,1},{8,14},{9,15},{10,... | collective-permute-start | bytes 368648 | tf_op jit(solution)/shard_map/ppermute | solution.py:468
  12.4 10.5 %collective-permute-start.6 = (bf16[120,512]{1,0:T(8,128)(2,1)S(1)}, bf16[120,512]{1,0:T(8,128)(2,1)S(1)}, u32[]{:S(2)}, u32[]{:S(2)}) collective-permute-start(bf16[120,512]{1,0:T(8,128)(2,1)S(1)} %get-tuple-element.31), channel_id=1, source_target_pairs={{0,7},{1,6},{2,5},{3,4},{4,3},{5,2},{6,1},{7,0},{8,15},{9,14},{10,... | collective-permute-start | bytes 368648 | tf_op jit(solution)/shard_map/ppermute | solution.py:468
  23.6 8.2 %collective-permute-start.9 = (bf16[8,80,256]{2,1,0:T(8,128)(2,1)S(1)}, bf16[8,80,256]{2,1,0:T(8,128)(2,1)S(1)}, u32[]{:S(2)}, u32[]{:S(2)}) collective-permute-start(bf16[8,80,256]{2,1,0:T(8,128)(2,1)S(1)} %get-tuple-element.39.quarter_ref), channel_id=1, source_target_pairs={{0,32},{32,0},{64,96},{96,64},{128,160},{160,128},{192,224},{224,1... | collective-permute-start | bytes 983048 | tf_op jit(solution)/shard_map/ppermute | solution.py:488
  31.9 32.8 %collective-permute-start.10 = (bf16[8,160,256]{2,1,0:T(8,128)(2,1)S(1)}, bf16[8,160,256]{2,1,0:T(8,128)(2,1)S(1)}, u32[]{:S(2)}, u32[]{:S(2)}) collective-permute-start(bf16[8,160,256]{2,1,0:T(8,128)(2,1)S(1)} %shard_map.113.mine_ref), channel_id=1, source_target_pairs={{0,8},{8,0},{1,9},{9,1},{2,10},{10,2},{3,11},{11,3},{4,12},{12,4},... | collective-permute-start | bytes 1966088 | tf_op jit(solution)/shard_map/ppermute | solution.py:493
  34.2 28.7 %collective-permute-start.7 = (bf16[8,96,256]{2,1,0:T(8,128)(2,1)S(1)}, bf16[8,96,256]{2,1,0:T(8,128)(2,1)S(1)}, u32[]{:S(2)}, u32[]{:S(2)}) collective-permute-start(bf16[8,96,256]{2,1,0:T(8,128)(2,1)S(1)} %get-tuple-element.33), channel_id=1, source_target_pairs={{0,2},{1,3},{2,0},{3,1},{4,6},{5,7},{6,4},{7,5},{8,10},{9,11},{10,... | collective-permute-start | bytes 1179656 | tf_op jit(solution)/shard_map/ppermute | solution.py:485
  34.4 28.4 %collective-permute-start.8 = (bf16[8,96,256]{2,1,0:T(8,128)(2,1)S(1)}, bf16[8,96,256]{2,1,0:T(8,128)(2,1)S(1)}, u32[]{:S(2)}, u32[]{:S(2)}) collective-permute-start(bf16[8,96,256]{2,1,0:T(8,128)(2,1)S(1)} %get-tuple-element.34), channel_id=1, source_target_pairs={{0,254},{1,255},{2,4},{3,5},{4,2},{5,3},{6,8},{7,9},{8,6},{9,7},{1... | collective-permute-start | bytes 1179656 | tf_op jit(solution)/shard_map/ppermute | solution.py:486
  64.7 21.3 %copy-start = (bf16[200,256]{1,0:T(8,128)(2,1)S(1)}, bf16[200,256]{1,0:T(8,128)(2,1)}, u32[]{:S(2)}) copy-start(bf16[200,256]{1,0:T(8,128)(2,1)} %query_ref.1) | copy-start | bytes 307204
  66.7 19.3 %collective-permute-start.11 = (f32[2,256,256]{2,1,0:T(8,128)S(1)}, f32[2,256,256]{2,1,0:T(8,128)S(1)}, u32[]{:S(2)}, u32[]{:S(2)}) collective-permute-start(f32[2,256,256]{2,1,0:T(8,128)S(1)} %get-tuple-element.41), channel_id=1, source_target_pairs={{0,1},{1,0},{2,3},{3,2},{4,5},{5,4},{6,7},{7,6},{8,9},{9,8},{10,11... | collective-permute-start | bytes 1572872 | tf_op jit(solution)/shard_map/ppermute | solution.py:509

commit v7 on v2

--- a/solution.py
+++ b/solution.py
@@ -106,7 +106,7 @@
         for t in range(2):
             piece = coarse_ref[n, :, :, 128 * t : 128 * t + 128].astype(F32)
             piece = jnp.concatenate([piece, jnp.zeros_like(piece)], axis=1)
-            coarse[n, t] = piece.reshape(256, 128)
+            coarse[n, t, 0:256] = piece.reshape(256, 128)
     lane = lanes_of((32, 128))
     vec_lane = lanes_of((32, 32))
     vec_row = lax.broadcasted_iota(jnp.int32, (32, 32), 0)
@@ -134,7 +134,7 @@
     copies[-1].wait()
     for t in range(4):
         piece = fine_ref[:, :, :, 128 * t : 128 * t + 128].astype(F32)
-        rows[t] = piece.reshape(48 * 8, 128)
+        rows[t, 0:384] = piece.reshape(48 * 8, 128)
     out = []
     for h in range(2):
         for q in range(4):
@@ -222,10 +222,13 @@
     inner_edge = jnp.where(side == 0, HALF - 1, 0)
     near = column // 2
     far = jnp.clip(near - 1 + 2 * (column % 2), 0, 127)
-    spread = (
-        jnp.where(source == near, 0.75, 0.0)
-        + jnp.where(jnp.logical_and(source == far, column != inner_edge), 0.25, 0.0)
-    ).astype(BF16)
+    spread = jnp.where(source == near, 0.75, 0.0) + jnp.where(
+        jnp.logical_and(source == far, column != inner_edge), 0.25, 0.0
+    )
+    spreads = [
+        jnp.concatenate([low * spread, (1.0 - low) * spread], axis=0).astype(BF16)
+        for low in (0.75, 0.25)
+    ]
     gain = vector_col(lat_weight_ref, 0)
     shift = vector_col(lat_weight_ref, 1)
     stats = (lat_stats_ref[0:1], lat_stats_ref[1:2], lat_stats_ref[2:3])
@@ -274,7 +277,7 @@
         lower = jnp.where(at_bottom, middle, lower)
         mains.append((upper, middle, lower))
     edge_at = jnp.where(side == 0, 127, 0)
-    ups, columns = [], []
+    beyond, columns = [], []
     for k, extra in enumerate((extra_above, extra_own, extra_below)):
         edges = []
         for n in range(2):
@@ -283,13 +286,7 @@
                 jnp.sum(jnp.where(small == edge_at, main.astype(F32), 0.0), axis=1, keepdims=True)
             )
         columns.append(0.75 * extra + 0.25 * jnp.where(first_image, edges[0], edges[1]))
-        ups.append(
-            [
-                dot(mains[n][k], spread)
-                + jnp.where(lane_at == inner_edge, 0.25 * extra[:, 4 * n : 4 * n + 1], 0.0)
-                for n in range(2)
-            ]
-        )
+        beyond.append(extra)
 
     lateral = jnp.where(
         time == 0, fine_above, jnp.where(time == 3, fine_below, fine_own)
@@ -320,12 +317,19 @@
 
     for n in range(2):
         mean, scale = norm[n]
-        up = [ups[k][n] for k in range(3)]
+        both = [jnp.concatenate(mains[n][k : k + 2], axis=1) for k in range(2)]
+        edge = [value[:, 4 * n : 4 * n + 1] for value in beyond]
+
+        def upsampled_row(k, which):
+            low = (0.75, 0.25)[which]
+            outer = 0.25 * (low * edge[k] + (1.0 - low) * edge[k + 1])
+            return dot(both[k], spreads[which]) + jnp.where(lane_at == inner_edge, outer, 0.0)
+
         rows = (
-            (fine_rows(above_ref, n, 0, HALF), 0.75 * up[0] + 0.25 * up[1]),
-            (fine_rows(own_ref, n, 0, HALF), 0.25 * up[0] + 0.75 * up[1]),
-            (fine_rows(own_ref, n, HALF, COLS), 0.75 * up[1] + 0.25 * up[2]),
-            (fine_rows(below_ref, n, 0, HALF), 0.25 * up[1] + 0.75 * up[2]),
+            (fine_rows(above_ref, n, 0, HALF), upsampled_row(0, 0)),
+            (fine_rows(own_ref, n, 0, HALF), upsampled_row(0, 1)),
+            (fine_rows(own_ref, n, HALF, COLS), upsampled_row(1, 0)),
+            (fine_rows(below_ref, n, 0, HALF), upsampled_row(1, 1)),
         )
         for t, (fine, upsampled) in enumerate(rows):
             value = ((dot(lat_weight, fine) - mean) * scale + shift + upsampled).astype(BF16)
@@ -451,8 +455,8 @@
             pltpu.VMEM((32, IN_CH), BF16),
             pltpu.VMEM((5, 1, 32), BF16),
             pltpu.VMEM((8, OWN_ROWS, COLS), BF16),
-            pltpu.VMEM((4, 48 * 8, 128), F32),
-            pltpu.VMEM((2, 2, 256, 128), F32),
+            pltpu.VMEM((4, 48 * 8 + 8, 128), F32),
+            pltpu.VMEM((2, 2, 256 + 8, 128), F32),
             pltpu.SemaphoreType.DMA((8,)),
             pltpu.SemaphoreType.DMA((8,)),
         ),

time: 85.5 us -> 85.2 us (level)
  no operation moved by 1% of the time
where the time goes in v7:
time: 85.2 us; the launch traced here: 85 us
  blocking collectives  45.1 us (53%)
  starting transfers between devices  22.5 us (26%)
  Pallas kernels  8.99 us (11%)
  waiting for transfers between devices  8.27 us (10%)
    all_to_all x2, blocking collectives, per_device(): stats = lax.all_to_all(stats, ALL, 0, 0, tiled=True)  45.1 us
    ppermute x7, starting transfers between devices, per_device(): lax.ppermute(shard, CHAN, [(i, i ^ k) for i in range(8)])  13.2 us
    pallas_call x8, Pallas kernels, call(): pl.pallas_call(kernel, out_shape=out_shape, in_specs=[pl.BlockSpec(memory...  8.99 us
    ppermute x7, waiting for transfers between devices, per_device(): lax.ppermute(shard, CHAN, [(i, i ^ k) for i in range(8)])  8.25 us
    all_to_all x1, starting transfers between devices, per_device(): own = lax.all_to_all(own_out, CHAN, 0, 0, tiled=True)  5.86 us
  transfers between devices with their start and end apart: 12, of which 4 were waited for; matrix products, arithmetic and copies ran while one was open for 0% of the time, Pallas kernels for 3%

profile of v7, /device:TPU:1, one launch (start us, length us, event | category | flops | bytes accessed | tf_op | source)
XLA Modules:
  0.0 85.0 jit_solution(5114945320892171191)
XLA Ops:
  0.0 0.0 copy-start
  0.0 0.0 copy-start.2
  0.0 2.3 %shard_map.109 = bf16[8,80,512]{2,1,0:T(8,128)(2,1)} custom-call(bf16[2,24,8,512]{3,2,1,0:T(8,128)(2,1)} %fine_hbm.1, bf16[2,32,4,256]{3,2,1,0:T(4,128)(2,1)} %coarse_hbm.1, bf16[32,192]{1,0:T(8,128)(2,1)} %weight_hbm.1, bf16[1,32]{1,0:T(2,128)(2,1)} %bitcast.18, bf16[1,32]{1,0:T(2,128)(2,1)} %bitcast.19, bf16[1,32]{1,0:T(2,128)(2,1)} %bitcast.20, ...), custom_call_target="tpu_custom_call" | custom-call | bytes 1048576 | tf_op jit(solution)/shard_map/pallas_call | solution.py:416
  2.3 5.9 %all-to-all-start = ((bf16[8,80,512]{2,1,0:T(8,128)(2,1)}), bf16[8,80,512]{2,1,0:T(8,128)(2,1)S(1)}, u32[]{:S(2)}, u32[]{:S(2)}) async-start(bf16[8,80,512]{2,1,0:T(8,128)(2,1)} %shard_map.109), calls=%async_computation | async-start | bytes 1310720 | tf_op jit(solution)/shard_map/all_to_all | solution.py:467
  8.2 0.0 copy-done
  8.2 0.0 copy-done.2
  8.2 1.5 %collective-permute-start.2 = (bf16[80,512]{1,0:T(8,128)(2,1)S(1)}, bf16[80,512]{1,0:T(8,128)(2,1)S(1)}, u32[]{:S(2)}, u32[]{:S(2)}) collective-permute-start(bf16[80,512]{1,0:T(8,128)(2,1)S(1)} %shard_map.113.refs_0_), channel_id=1, source_target_pairs={{0,1},{1,0},{2,3},{3,2},{4,5},{5,4},{6,7},{7,6},{8,9},{9,8},{10,11... | collective-permute-start | bytes 245768 | tf_op jit(solution)/shard_map/ppermute | solution.py:469
  9.7 1.2 %collective-permute-start.3 = (bf16[80,512]{1,0:T(8,128)(2,1)S(1)}, bf16[80,512]{1,0:T(8,128)(2,1)S(1)}, u32[]{:S(2)}, u32[]{:S(2)}) collective-permute-start(bf16[80,512]{1,0:T(8,128)(2,1)S(1)} %shard_map.113.refs_0_), channel_id=1, source_target_pairs={{0,2},{1,3},{2,0},{3,1},{4,6},{5,7},{6,4},{7,5},{8,10},{9,11},{10,... | collective-permute-start | bytes 245768 | tf_op jit(solution)/shard_map/ppermute | solution.py:469
  10.9 0.1 collective-permute-start.4
  11.0 2.9 %collective-permute-start.5 = (bf16[80,512]{1,0:T(8,128)(2,1)S(1)}, bf16[80,512]{1,0:T(8,128)(2,1)S(1)}, u32[]{:S(2)}, u32[]{:S(2)}) collective-permute-start(bf16[80,512]{1,0:T(8,128)(2,1)S(1)} %shard_map.113.refs_0_), channel_id=1, source_target_pairs={{0,4},{1,5},{2,6},{3,7},{4,0},{5,1},{6,2},{7,3},{8,12},{9,13},{10,... | collective-permute-start | bytes 245768 | tf_op jit(solution)/shard_map/ppermute | solution.py:469
  13.9 1.2 %collective-permute-start.6 = (bf16[80,512]{1,0:T(8,128)(2,1)S(1)}, bf16[80,512]{1,0:T(8,128)(2,1)S(1)}, u32[]{:S(2)}, u32[]{:S(2)}) collective-permute-start(bf16[80,512]{1,0:T(8,128)(2,1)S(1)} %shard_map.113.refs_0_), channel_id=1, source_target_pairs={{0,5},{1,4},{2,7},{3,6},{4,1},{5,0},{6,3},{7,2},{8,13},{9,12},{10,... | collective-permute-start | bytes 245768 | tf_op jit(solution)/shard_map/ppermute | solution.py:469
  15.1 1.2 %collective-permute-done.2.refs_1_ = bf16[80,512]{1,0:T(8,128)(2,1)S(1)} collective-permute-done((bf16[80,512]{1,0:T(8,128)(2,1)S(1)}, bf16[80,512]{1,0:T(8,128)(2,1)S(1)}, u32[]{:S(2)}, u32[]{:S(2)}) %collective-permute-start.2) | collective-permute-done | bytes 81952 | tf_op jit(solution)/shard_map/ppermute | solution.py:469
  16.3 5.1 %collective-permute-start.7 = (bf16[80,512]{1,0:T(8,128)(2,1)S(1)}, bf16[80,512]{1,0:T(8,128)(2,1)S(1)}, u32[]{:S(2)}, u32[]{:S(2)}) collective-permute-start(bf16[80,512]{1,0:T(8,128)(2,1)S(1)} %shard_map.113.refs_0_), channel_id=1, source_target_pairs={{0,6},{1,7},{2,4},{3,5},{4,2},{5,3},{6,0},{7,1},{8,14},{9,15},{10,... | collective-permute-start | bytes 245768 | tf_op jit(solution)/shard_map/ppermute | solution.py:469
  21.4 0.0 collective-permute-done.3.refs_2_
  21.4 1.2 %collective-permute-start.8 = (bf16[80,512]{1,0:T(8,128)(2,1)S(1)}, bf16[80,512]{1,0:T(8,128)(2,1)S(1)}, u32[]{:S(2)}, u32[]{:S(2)}) collective-permute-start(bf16[80,512]{1,0:T(8,128)(2,1)S(1)} %shard_map.113.refs_0_), channel_id=1, source_target_pairs={{0,7},{1,6},{2,5},{3,4},{4,3},{5,2},{6,1},{7,0},{8,15},{9,14},{10,... | collective-permute-start | bytes 245768 | tf_op jit(solution)/shard_map/ppermute | solution.py:469
  22.6 0.0 collective-permute-done.4.refs_3_
  22.6 0.5 collective-permute-done.5.refs_4_
  23.2 2.8 %collective-permute-done.6.refs_5_ = bf16[80,512]{1,0:T(8,128)(2,1)S(1)} collective-permute-done((bf16[80,512]{1,0:T(8,128)(2,1)S(1)}, bf16[80,512]{1,0:T(8,128)(2,1)S(1)}, u32[]{:S(2)}, u32[]{:S(2)}) %collective-permute-start.6) | collective-permute-done | bytes 81952 | tf_op jit(solution)/shard_map/ppermute | solution.py:469
  25.9 0.0 collective-permute-done.7.refs_6_
  25.9 3.7 %collective-permute-done.8.refs_7_ = bf16[80,512]{1,0:T(8,128)(2,1)S(1)} collective-permute-done((bf16[80,512]{1,0:T(8,128)(2,1)S(1)}, bf16[80,512]{1,0:T(8,128)(2,1)S(1)}, u32[]{:S(2)}, u32[]{:S(2)}) %collective-permute-start.8) | collective-permute-done | bytes 81952 | tf_op jit(solution)/shard_map/ppermute | solution.py:469
  29.6 0.1 shard_map.114.mine_ref
  29.7 1.1 %collective-permute-start.9 = (bf16[8,80,512]{2,1,0:T(8,128)(2,1)S(1)}, bf16[8,80,512]{2,1,0:T(8,128)(2,1)S(1)}, u32[]{:S(2)}, u32[]{:S(2)}) collective-permute-start(bf16[8,80,512]{2,1,0:T(8,128)(2,1)S(1)} %shard_map.114.mine_ref), channel_id=1, source_target_pairs={{0,8},{8,0},{1,9},{9,1},{2,10},{10,2},{3,11},{11,3},{4,12},{12,4},... | collective-permute-start | bytes 1966088 | tf_op jit(solution)/shard_map/ppermute | solution.py:489
  30.8 0.0 all-to-all-done.own_ref
  30.8 0.6 shard_map.110
  31.4 0.3 collective-permute-start
  31.7 1.4 %collective-permute-start.1 = (bf16[8,96,256]{2,1,0:T(8,128)(2,1)S(1)}, bf16[8,96,256]{2,1,0:T(8,128)(2,1)S(1)}, u32[]{:S(2)}, u32[]{:S(2)}) collective-permute-start(bf16[8,96,256]{2,1,0:T(8,128)(2,1)S(1)} %get-tuple-element.15), channel_id=1, source_target_pairs={{0,254},{1,255},{2,4},{3,5},{4,2},{5,3},{6,8},{7,9},{8,6},{9,7},{1... | collective-permute-start | bytes 1179656 | tf_op jit(solution)/shard_map/ppermute | solution.py:483
  33.2 26.3 %all_to_all.27 = f32[256,1,128]{2,1,0:T(1,128)S(1)} all-to-all(f32[256,1,128]{2,1,0:T(1,128)S(1)} %bitcast.16), channel_id=1, replica_groups=mesh['band_0'=8,'band_1'=2,'band_2'=2,'chan_0'=4,'chan_1'=2] {'band_0','..., dimensions={0} | all-to-all | bytes 262144 | tf_op jit(solution)/shard_map/all_to_all | solution.py:484
  59.4 0.1 shard_map.111.lat_stats_ref
  59.5 0.0 collective-permute-done.one_ref
  59.5 0.0 collective-permute-done.1.two_ref
  59.5 1.5 %shard_map.112 = (bf16[2,768,512]{2,1,0:T(8,128)(2,1)S(1)}, bf16[768,128]{1,0:T(8,128)(2,1)S(1)}) custom-call(bf16[8,80,512]{2,1,0:T(8,128)(2,1)S(1)} %all-to-all-done.own_ref, bf16[8,96,256]{2,1,0:T(8,128)(2,1)S(1)} %collective-permute-done.one_ref, bf16[8,96,256]{2,1,0:T(8,128)(2,1)S(1)} %collective-permute-done.1.two_ref, ...), custom_call_target="tpu_custom_call" | custom-call | flops 939524096 | bytes 1048576 | tf_op jit(solution)/shard_map/pallas_call | solution.py:416
  61.0 0.0 collective-permute-done.9.other_ref
  61.0 0.0 copy-start.1
  61.0 2.0 %shard_map.115 = (f32[2,256,256]{2,1,0:T(8,128)S(1)}, f32[2,256,256]{2,1,0:T(8,128)S(1)}, f32[256,128]{1,0:T(8,128)S(1)}) custom-call(bf16[2,768,512]{2,1,0:T(8,128)(2,1)S(1)} %get-tuple-element.18.joined_ref, bf16[768,128]{1,0:T(8,128)(2,1)S(1)} %get-tuple-element.19.beside_ref, bf16[8,80,512]{2,1,0:T(8,128)(2,1)S(1)} %shard_map.114.mine_ref, ...), custom_call_target="tpu_custom_call" | custom-call | flops 1207959552 | bytes 1048576 | tf_op jit(solution)/shard_map/pallas_call | solution.py:416
  63.1 0.6 collective-permute-start.10
  63.7 18.9 %all_to_all.28 = f32[256,1,128]{2,1,0:T(1,128)S(1)} all-to-all(f32[256,1,128]{2,1,0:T(1,128)S(1)} %bitcast.17), channel_id=1, replica_groups=mesh['band_0'=8,'band_1'=2,'band_2'=2,'chan_0'=4,'chan_1'=2] {'band_0','..., dimensions={0} | all-to-all | bytes 262144 | tf_op jit(solution)/shard_map/all_to_all | solution.py:506
  82.6 0.0 collective-permute-done.10.taken_ref
  82.6 0.0 copy-done.1
  82.6 2.4 %shard_map.116 = f32[1600,128]{1,0:T(8,128)} custom-call(f32[2,256,256]{2,1,0:T(8,128)S(1)} %get-tuple-element.20.keep_ref, f32[2,256,256]{2,1,0:T(8,128)S(1)} %collective-permute-done.10.taken_ref, f32[256,128]{1,0:T(8,128)S(1)} %bitcast.14, bf16[256,256]{1,0:T(8,128)(2,1)S(1)} %get-tuple-element.16.lat_weight_ref, ...), custom_call_target="tpu_custom_call" | custom-call | flops 268435456 | bytes 1048576 | tf_op jit(solution)/shard_map/pallas_call | solution.py:416
  (1 shorter events, 0.0 us)
Async XLA Ops:
  0.0 8.2 %copy-start = (bf16[3,3,32,256]{3,2,1,0:T(8,128)(2,1)S(1)}, bf16[3,3,32,256]{3,2,1,0:T(8,128)(2,1)}, u32[]{:S(2)}) copy-start(bf16[3,3,32,256]{3,2,1,0:T(8,128)(2,1)} %conv_ref.1) | copy-start | bytes 442372
  0.0 8.2 %copy-start.2 = (bf16[32,256]{1,0:T(8,128)(2,1)S(1)}, bf16[32,256]{1,0:T(8,128)(2,1)}, u32[]{:S(2)}) copy-start(bf16[32,256]{1,0:T(8,128)(2,1)} %mask_ref.1) | copy-start | bytes 49156
  2.3 28.5 %all-to-all-start = ((bf16[8,80,512]{2,1,0:T(8,128)(2,1)}), bf16[8,80,512]{2,1,0:T(8,128)(2,1)S(1)}, u32[]{:S(2)}, u32[]{:S(2)}) async-start(bf16[8,80,512]{2,1,0:T(8,128)(2,1)} %shard_map.109), calls=%async_computation | async-start | bytes 1310720 | tf_op jit(solution)/shard_map/all_to_all | solution.py:467
  8.2 8.1 %collective-permute-start.2 = (bf16[80,512]{1,0:T(8,128)(2,1)S(1)}, bf16[80,512]{1,0:T(8,128)(2,1)S(1)}, u32[]{:S(2)}, u32[]{:S(2)}) collective-permute-start(bf16[80,512]{1,0:T(8,128)(2,1)S(1)} %shard_map.113.refs_0_), channel_id=1, source_target_pairs={{0,1},{1,0},{2,3},{3,2},{4,5},{5,4},{6,7},{7,6},{8,9},{9,8},{10,11... | collective-permute-start | bytes 245768 | tf_op jit(solution)/shard_map/ppermute | solution.py:469
  9.7 11.7 %collective-permute-start.3 = (bf16[80,512]{1,0:T(8,128)(2,1)S(1)}, bf16[80,512]{1,0:T(8,128)(2,1)S(1)}, u32[]{:S(2)}, u32[]{:S(2)}) collective-permute-start(bf16[80,512]{1,0:T(8,128)(2,1)S(1)} %shard_map.113.refs_0_), channel_id=1, source_target_pairs={{0,2},{1,3},{2,0},{3,1},{4,6},{5,7},{6,4},{7,5},{8,10},{9,11},{10,... | collective-permute-start | bytes 245768 | tf_op jit(solution)/shard_map/ppermute | solution.py:469
  10.9 11.7 %collective-permute-start.4 = (bf16[80,512]{1,0:T(8,128)(2,1)S(1)}, bf16[80,512]{1,0:T(8,128)(2,1)S(1)}, u32[]{:S(2)}, u32[]{:S(2)}) collective-permute-start(bf16[80,512]{1,0:T(8,128)(2,1)S(1)} %shard_map.113.refs_0_), channel_id=1, source_target_pairs={{0,3},{1,2},{2,1},{3,0},{4,7},{5,6},{6,5},{7,4},{8,11},{9,10},{10,... | collective-permute-start | bytes 245768 | tf_op jit(solution)/shard_map/ppermute | solution.py:469
  11.0 12.1 %collective-permute-start.5 = (bf16[80,512]{1,0:T(8,128)(2,1)S(1)}, bf16[80,512]{1,0:T(8,128)(2,1)S(1)}, u32[]{:S(2)}, u32[]{:S(2)}) collective-permute-start(bf16[80,512]{1,0:T(8,128)(2,1)S(1)} %shard_map.113.refs_0_), channel_id=1, source_target_pairs={{0,4},{1,5},{2,6},{3,7},{4,0},{5,1},{6,2},{7,3},{8,12},{9,13},{10,... | collective-permute-start | bytes 245768 | tf_op jit(solution)/shard_map/ppermute | solution.py:469
  13.9 12.0 %collective-permute-start.6 = (bf16[80,512]{1,0:T(8,128)(2,1)S(1)}, bf16[80,512]{1,0:T(8,128)(2,1)S(1)}, u32[]{:S(2)}, u32[]{:S(2)}) collective-permute-start(bf16[80,512]{1,0:T(8,128)(2,1)S(1)} %shard_map.113.refs_0_), channel_id=1, source_target_pairs={{0,5},{1,4},{2,7},{3,6},{4,1},{5,0},{6,3},{7,2},{8,13},{9,12},{10,... | collective-permute-start | bytes 245768 | tf_op jit(solution)/shard_map/ppermute | solution.py:469
  16.3 9.6 %collective-permute-start.7 = (bf16[80,512]{1,0:T(8,128)(2,1)S(1)}, bf16[80,512]{1,0:T(8,128)(2,1)S(1)}, u32[]{:S(2)}, u32[]{:S(2)}) collective-permute-start(bf16[80,512]{1,0:T(8,128)(2,1)S(1)} %shard_map.113.refs_0_), channel_id=1, source_target_pairs={{0,6},{1,7},{2,4},{3,5},{4,2},{5,3},{6,0},{7,1},{8,14},{9,15},{10,... | collective-permute-start | bytes 245768 | tf_op jit(solution)/shard_map/ppermute | solution.py:469
  21.4 8.2 %collective-permute-start.8 = (bf16[80,512]{1,0:T(8,128)(2,1)S(1)}, bf16[80,512]{1,0:T(8,128)(2,1)S(1)}, u32[]{:S(2)}, u32[]{:S(2)}) collective-permute-start(bf16[80,512]{1,0:T(8,128)(2,1)S(1)} %shard_map.113.refs_0_), channel_id=1, source_target_pairs={{0,7},{1,6},{2,5},{3,4},{4,3},{5,2},{6,1},{7,0},{8,15},{9,14},{10,... | collective-permute-start | bytes 245768 | tf_op jit(solution)/shard_map/ppermute | solution.py:469
  29.7 31.3 %collective-permute-start.9 = (bf16[8,80,512]{2,1,0:T(8,128)(2,1)S(1)}, bf16[8,80,512]{2,1,0:T(8,128)(2,1)S(1)}, u32[]{:S(2)}, u32[]{:S(2)}) collective-permute-start(bf16[8,80,512]{2,1,0:T(8,128)(2,1)S(1)} %shard_map.114.mine_ref), channel_id=1, source_target_pairs={{0,8},{8,0},{1,9},{9,1},{2,10},{10,2},{3,11},{11,3},{4,12},{12,4},... | collective-permute-start | bytes 1966088 | tf_op jit(solution)/shard_map/ppermute | solution.py:489
  31.4 28.1 %collective-permute-start = (bf16[8,96,256]{2,1,0:T(8,128)(2,1)S(1)}, bf16[8,96,256]{2,1,0:T(8,128)(2,1)S(1)}, u32[]{:S(2)}, u32[]{:S(2)}) collective-permute-start(bf16[8,96,256]{2,1,0:T(8,128)(2,1)S(1)} %get-tuple-element.14), channel_id=1, source_target_pairs={{0,2},{1,3},{2,0},{3,1},{4,6},{5,7},{6,4},{7,5},{8,10},{9,11},{10,... | collective-permute-start | bytes 1179656 | tf_op jit(solution)/shard_map/ppermute | solution.py:482
  31.7 27.8 %collective-permute-start.1 = (bf16[8,96,256]{2,1,0:T(8,128)(2,1)S(1)}, bf16[8,96,256]{2,1,0:T(8,128)(2,1)S(1)}, u32[]{:S(2)}, u32[]{:S(2)}) collective-permute-start(bf16[8,96,256]{2,1,0:T(8,128)(2,1)S(1)} %get-tuple-element.15), channel_id=1, source_target_pairs={{0,254},{1,255},{2,4},{3,5},{4,2},{5,3},{6,8},{7,9},{8,6},{9,7},{1... | collective-permute-start | bytes 1179656 | tf_op jit(solution)/shard_map/ppermute | solution.py:483
  61.0 21.5 %copy-start.1 = (bf16[200,256]{1,0:T(8,128)(2,1)S(1)}, bf16[200,256]{1,0:T(8,128)(2,1)}, u32[]{:S(2)}) copy-start(bf16[200,256]{1,0:T(8,128)(2,1)} %query_ref.1) | copy-start | bytes 307204
  63.1 19.5 %collective-permute-start.10 = (f32[2,256,256]{2,1,0:T(8,128)S(1)}, f32[2,256,256]{2,1,0:T(8,128)S(1)}, u32[]{:S(2)}, u32[]{:S(2)}) collective-permute-start(f32[2,256,256]{2,1,0:T(8,128)S(1)} %get-tuple-element.21), channel_id=1, source_target_pairs={{0,1},{1,0},{2,3},{3,2},{4,5},{5,4},{6,7},{7,6},{8,9},{9,8},{10,11... | collective-permute-start | bytes 1572872 | tf_op jit(solution)/shard_map/ppermute | solution.py:505
